TPU v7x, 512 devices: a whole 4x8x8 slice. The times are simulated.
512 devices in a mesh: gx: 16 (over z, core), gy: 4 (over x), gz: 8 (over y).
Axes of the slice: x: 4, y: 8, z: 8, core: 2. Of those that a mesh axis runs over, the one named last changes fastest.
Arguments:
- krylov_basis: float32 [60, 64, 32, 1024], P(None, 'gx', 'gy', 'gz'), may hold values from -6 to 6
- schur_vectors: float32 [60, 20], replicated, may hold values from -1 to 1, as said below
- next_vector: float32 [64, 32, 1024], P('gx', 'gy', 'gz'), may hold values from -10 to 10
- diag_shift: float32 [64, 32, 1024], P('gx', 'gy', 'gz'), may hold values from 0.25 to 2
- velocity: float32 [3, 64, 32, 1024], P(None, 'gx', 'gy', 'gz'), may hold values from -1 to 1
Outputs:
- new_basis: float32 [24, 64, 32, 1024], P(None, 'gx', 'gy', 'gz')
- hessenberg: float32 [24, 3], replicated
Inputs may be any that keep to these rules, and one draw needn't show every extreme that they name: `schur_vectors`: the columns are orthonormal.
All inputs are finite; a program needn't handle non-finite values.
Results may differ from a plain program's by a relative error of at most 0.0003.
Values sent between devices are 32-bit elements; how exact they have to be, the bound alone decides.
No kernel may reach another device: no remote copies, remote signals or barrier semaphores. Data moves between devices by JAX's collectives and lax.ppermute only.
A program may use at most 64 MiB of HBM per device.

v0:
```python
import jax
import jax.numpy as jnp
from jax import lax
from jax.sharding import Mesh
from jax.sharding import PartitionSpec as P

KEEP = 20
EXPAND = 3
ROWS = 24
GX = ("gx_0", "gx_1")
GX_GY_GZ = ("gx_0", "gx_1", "gy", "gz")


def with_halo(value, sides, width):
    for axis, dim in sides:
        count, length = (lax.axis_size(axis), value.shape[dim])
        up = [(i, (i + 1) % count) for i in range(count - 1)]
        down = [(j, i) for i, j in up]
        last = lax.slice_in_dim(value, length - width, length, axis=dim)
        initial = lax.slice_in_dim(value, 0, width, axis=dim)
        before = lax.ppermute(last, axis, up)
        after = lax.ppermute(initial, axis, down)
        value = jnp.concatenate([before, value, after], axis=dim)
    return value


def by_axis(value, axes):
    for axis in axes:
        value = lax.psum(value, axis)
    return value


def combine_terms(
    field, x_ahead, x_behind, y_ahead, y_behind, z_ahead, z_behind, diag_shift, velocity
):
    neighbours = x_ahead + x_behind + y_ahead + y_behind + z_ahead + z_behind
    flow = (
        velocity[0] * (x_ahead - x_behind)
        + velocity[1] * (y_ahead - y_behind)
        + velocity[2] * (z_ahead - z_behind)
    )
    return (6.0 + diag_shift) * field - neighbours + 0.5 * flow


def operate_field(field, diag_shift, velocity):
    along_x = with_halo(field, ((GX, 0),), 1)
    along_y = with_halo(field, (("gy", 1),), 1)
    along_z = with_halo(field, (("gz", 2),), 1)
    return combine_terms(
        field,
        along_x[2:],
        along_x[:-2],
        along_y[:, 2:],
        along_y[:, :-2],
        along_z[:, :, 2:],
        along_z[:, :, :-2],
        diag_shift,
        velocity,
    )


def per_device(krylov_basis, schur_vectors, next_vector, diag_shift, velocity):
    highest = lax.Precision.HIGHEST
    shape_local = next_vector.shape
    cell_count = (
        shape_local[0]
        * shape_local[1]
        * shape_local[2]
        * lax.axis_size(GX)
        * lax.axis_size("gy")
        * lax.axis_size("gz")
    )
    rotated = jnp.einsum("ik,ixyz->kxyz", schur_vectors, krylov_basis, precision=highest)
    columns = []
    starting = jnp.concatenate([rotated, next_vector[None]], axis=0)
    flat_start = starting.reshape(KEEP + 1, -1)
    gram_matrix = (
        by_axis(jnp.dot(flat_start, flat_start.T, precision=highest), GX_GY_GZ) / cell_count
    )
    divisor = jnp.maximum(jnp.sqrt(gram_matrix[KEEP, KEEP]), 0.5)
    factor = jnp.ones((KEEP + 1,), jnp.float32).at[KEEP].set(1.0 / divisor)
    gram_matrix = gram_matrix * factor[:, None] * factor[None, :]
    vectors = jnp.concatenate([rotated, (next_vector / divisor)[None]], axis=0)
    for expansion in range(EXPAND):
        count = vectors.shape[0]
        flat_basis = vectors.reshape(count, -1)
        applied = operate_field(vectors[-1], diag_shift, velocity).reshape(-1)
        dotted, self_sum = (
            by_axis(jnp.dot(flat_basis, applied, precision=highest), GX_GY_GZ),
            by_axis(jnp.sum(applied * applied), GX_GY_GZ),
        )
        first_coeffs = dotted / cell_count
        self_norm = self_sum / cell_count
        second_coeffs = first_coeffs - jnp.dot(gram_matrix, first_coeffs, precision=highest)
        total_coeffs = first_coeffs + second_coeffs
        partly = applied - jnp.dot(first_coeffs, flat_basis, precision=highest)
        cleaned = partly - jnp.dot(second_coeffs, flat_basis, precision=highest)
        length_sq = (
            self_norm
            - 2.0 * jnp.dot(total_coeffs, first_coeffs, precision=highest)
            + jnp.dot(
                total_coeffs,
                jnp.dot(gram_matrix, total_coeffs, precision=highest),
                precision=highest,
            )
        )
        length = jnp.sqrt(jnp.maximum(length_sq, 0.0))
        divisor = jnp.maximum(length, 0.5)
        column = jnp.zeros((ROWS,), jnp.float32)
        column = column.at[:count].set(total_coeffs).at[count].set(length)
        columns.append(column)
        newest = (cleaned / divisor).reshape(shape_local)
        vectors = jnp.concatenate([vectors, newest[None]], axis=0)
        intersect = (
            second_coeffs - jnp.dot(gram_matrix, second_coeffs, precision=highest)
        ) / divisor
        corner = jnp.maximum(length_sq, 0.0) / (divisor * divisor)
        upper_rows = jnp.concatenate([gram_matrix, intersect[:, None]], axis=1)
        lower_row = jnp.concatenate([intersect, corner[None]], axis=0)
        gram_matrix = jnp.concatenate([upper_rows, lower_row[None]], axis=0)
    return (vectors, jnp.stack(columns, axis=1))


def solution(mesh):
    split = Mesh(
        mesh.devices.reshape(8, 2, mesh.shape["gy"], mesh.shape["gz"]), ("gx_0", "gx_1", "gy", "gz")
    )
    return jax.shard_map(
        per_device,
        mesh=split,
        in_specs=(
            P(None, GX, "gy", "gz"),
            P(),
            P(GX, "gy", "gz"),
            P(GX, "gy", "gz"),
            P(None, GX, "gy", "gz"),
        ),
        out_specs=(P(None, GX, "gy", "gz"), P()),
        check_vma=False,
    )
```

profile of v0, /device:TPU:1, one launch (start us, length us, event | category | flops | bytes accessed | tf_op | source)
XLA Modules:
  0.0 300.7 jit_solution(8931274093424022285)
XLA Ops:
  0.7 1.2 copy-done
  1.8 1.9 fusion.10
  3.7 0.5 convolution_bitcast_fusion
  4.2 29.8 %psum.196 = f32[21,21]{1,0:T(8,128)S(1)} all-reduce(f32[21,21]{1,0:T(8,128)S(1)} %convolution_bitcast_fusion), channel_id=1, replica_groups=mesh['gx_0'=8,'gx_1'=2,'gy'=4,'gz'=8] {'gx_0'}, use_global_device_ids=true, to_apply=%region_0.0 | all-reduce | flops 441 | bytes 3528 | tf_op jit(solution)/shard_map/psum | solution.py:29
  34.0 10.8 %psum.197 = f32[21,21]{1,0:T(8,128)S(1)} all-reduce(f32[21,21]{1,0:T(8,128)S(1)} %psum.196), channel_id=1, replica_groups=mesh['gx_0'=8,'gx_1'=2,'gy'=4,'gz'=8] {'gx_1'}, use_global_device_ids=true, to_apply=%region_1.0 | all-reduce | flops 441 | bytes 3528 | tf_op jit(solution)/shard_map/psum | solution.py:29
  44.8 13.1 %psum.198 = f32[21,21]{1,0:T(8,128)S(1)} all-reduce(f32[21,21]{1,0:T(8,128)S(1)} %psum.197), channel_id=1, replica_groups=mesh['gx_0'=8,'gx_1'=2,'gy'=4,'gz'=8] {'gy'}, use_global_device_ids=true, to_apply=%region_2.0 | all-reduce | flops 441 | bytes 3528 | tf_op jit(solution)/shard_map/psum | solution.py:29
  57.8 23.1 %psum.199 = f32[21,21]{1,0:T(8,128)S(1)} all-reduce(f32[21,21]{1,0:T(8,128)S(1)} %psum.198), channel_id=1, replica_groups=mesh['gx_0'=8,'gx_1'=2,'gy'=4,'gz'=8] {'gz'}, use_global_device_ids=true, to_apply=%region_3.0 | all-reduce | flops 441 | bytes 3528 | tf_op jit(solution)/shard_map/psum | solution.py:29
  81.0 0.6 slice.304
  82.3 1.4 collective-permute-start.5
  83.8 1.3 collective-permute-start.3
  85.1 1.3 collective-permute-start.2
  86.4 11.3 %collective-permute-start.1 = (f32[1,8,128]{2,1,0:T(8,128)S(1)}, f32[1,8,128]{2,1,0:T(8,128)S(1)}, u32[]{:S(2)}, u32[]{:S(2)}) collective-permute-start(f32[1,8,128]{2,1,0:T(8,128)S(1)} %get-tuple-element.139), channel_id=1, source_target_pairs={{0,32},{32,64},{64,96},{96,128},{128,160},{160,192},{192,224},{224... | collective-permute-start | bytes 12296 | tf_op jit(solution)/shard_map/ppermute | solution.py:21
  97.7 3.1 %collective-permute-start = (f32[1,8,128]{2,1,0:T(8,128)S(1)}, f32[1,8,128]{2,1,0:T(8,128)S(1)}, u32[]{:S(2)}, u32[]{:S(2)}) collective-permute-start(f32[1,8,128]{2,1,0:T(8,128)S(1)} %get-tuple-element.138), channel_id=1, source_target_pairs={{32,0},{64,32},{96,64},{128,96},{160,128},{192,160},{224,192},{256... | collective-permute-start | bytes 12296 | tf_op jit(solution)/shard_map/ppermute | solution.py:22
  101.2 1.3 collective-permute-start.4
  102.5 0.2 copy.36
  102.8 3.1 %collective-permute-done.4 = f32[4,8,1]{2,1,0:T(8,128)S(1)} collective-permute-done((f32[4,8,1]{2,1,0:T(8,128)S(1)}, f32[4,8,1]{2,1,0:T(8,128)S(1)}, u32[]{:S(2)}, u32[]{:S(2)}) %collective-permute-start.4) | collective-permute-done | bytes 160 | tf_op jit(solution)/shard_map/ppermute | solution.py:22
  105.9 0.7 multiply_reduce_fusion.2
  106.6 0.5 convolution_bitcast_fusion.11
  107.1 12.0 %all-reduce.9 = (f32[21]{0:T(128)S(1)}, f32[]{:T(128)}) all-reduce(f32[21]{0:T(128)S(1)} %convolution_bitcast_fusion.11, f32[]{:T(128)} %get-tuple-element.124), channel_id=1, replica_groups=mesh['gx_0'=8,'gx_1'=2,'gy'=4,'gz'=8] {'gx_0'}, use_global_device_ids=true, to_apply=%region_4.0 | all-reduce | flops 22 | bytes 176 | tf_op jit(solution)/shard_map/psum | solution.py:29
  119.1 8.6 %all-reduce.15 = (f32[21]{0:T(128)S(1)}, f32[]{:T(128)}) all-reduce(f32[21]{0:T(128)S(1)} %get-tuple-element.100, f32[]{:T(128)} %get-tuple-element.101), channel_id=1, replica_groups=mesh['gx_0'=8,'gx_1'=2,'gy'=4,'gz'=8] {'gx_1'}, use_global_device_ids=true, to_apply=%region_5.0 | all-reduce | flops 22 | bytes 176 | tf_op jit(solution)/shard_map/psum | solution.py:29
  127.7 9.3 %all-reduce.12 = (f32[21]{0:T(128)S(1)}, f32[]{:T(128)}) all-reduce(f32[21]{0:T(128)S(1)} %get-tuple-element.112, f32[]{:T(128)} %get-tuple-element.113), channel_id=1, replica_groups=mesh['gx_0'=8,'gx_1'=2,'gy'=4,'gz'=8] {'gy'}, use_global_device_ids=true, to_apply=%region_6.0 | all-reduce | flops 22 | bytes 176 | tf_op jit(solution)/shard_map/psum | solution.py:29
  137.0 14.3 %all-reduce.6 = (f32[21]{0:T(128)S(1)}, f32[]{:T(128)}) all-reduce(f32[21]{0:T(128)S(1)} %get-tuple-element.106, f32[]{:T(128)} %get-tuple-element.107), channel_id=1, replica_groups=mesh['gx_0'=8,'gx_1'=2,'gy'=4,'gz'=8] {'gz'}, use_global_device_ids=true, to_apply=%region_7.0 | all-reduce | flops 22 | bytes 176 | tf_op jit(solution)/shard_map/psum | solution.py:29
  151.3 0.7 multiply_reduce_fusion.5
  152.0 0.3 fusion.34
  152.4 0.3 fusion.33
  153.4 0.7 fusion.12
  155.6 0.1 fusion.8
  155.7 1.6 collective-permute-start.11
  157.3 2.1 collective-permute-start.9
  159.3 1.3 collective-permute-start.8
  160.6 8.0 %collective-permute-start.7 = (f32[1,8,128]{2,1,0:T(8,128)S(1)}, f32[1,8,128]{2,1,0:T(8,128)S(1)}, u32[]{:S(2)}, u32[]{:S(2)}) collective-permute-start(f32[1,8,128]{2,1,0:T(8,128)S(1)} %get-tuple-element.133), channel_id=1, source_target_pairs={{0,32},{32,64},{64,96},{96,128},{128,160},{160,192},{192,224},{224... | collective-permute-start | bytes 12296 | tf_op jit(solution)/shard_map/ppermute | solution.py:21
  168.7 1.9 collective-permute-start.6
  170.9 1.3 collective-permute-start.10
  172.3 3.6 %collective-permute-done.10 = f32[4,8,1]{2,1,0:T(8,128)S(1)} collective-permute-done((f32[4,8,1]{2,1,0:T(8,128)S(1)}, f32[4,8,1]{2,1,0:T(8,128)S(1)}, u32[]{:S(2)}, u32[]{:S(2)}) %collective-permute-start.10) | collective-permute-done | bytes 160 | tf_op jit(solution)/shard_map/ppermute | solution.py:22
  175.9 0.7 multiply_reduce_fusion.1
  176.6 0.5 convolution_bitcast_fusion.10
  177.1 12.9 %all-reduce.8 = (f32[22]{0:T(128)S(1)}, f32[]{:T(128)}) all-reduce(f32[22]{0:T(128)S(1)} %convolution_bitcast_fusion.10, f32[]{:T(128)} %get-tuple-element.120), channel_id=1, replica_groups=mesh['gx_0'=8,'gx_1'=2,'gy'=4,'gz'=8] {'gx_0'}, use_global_device_ids=true, to_apply=%region_13.0 | all-reduce | flops 23 | bytes 184 | tf_op jit(solution)/shard_map/psum | solution.py:29
  190.1 8.8 %all-reduce.14 = (f32[22]{0:T(128)S(1)}, f32[]{:T(128)}) all-reduce(f32[22]{0:T(128)S(1)} %get-tuple-element.98, f32[]{:T(128)} %get-tuple-element.99), channel_id=1, replica_groups=mesh['gx_0'=8,'gx_1'=2,'gy'=4,'gz'=8] {'gx_1'}, use_global_device_ids=true, to_apply=%region_14.0 | all-reduce | flops 23 | bytes 184 | tf_op jit(solution)/shard_map/psum | solution.py:29
  198.8 9.0 %all-reduce.11 = (f32[22]{0:T(128)S(1)}, f32[]{:T(128)}) all-reduce(f32[22]{0:T(128)S(1)} %get-tuple-element.110, f32[]{:T(128)} %get-tuple-element.111), channel_id=1, replica_groups=mesh['gx_0'=8,'gx_1'=2,'gy'=4,'gz'=8] {'gy'}, use_global_device_ids=true, to_apply=%region_15.0 | all-reduce | flops 23 | bytes 184 | tf_op jit(solution)/shard_map/psum | solution.py:29
  207.8 15.5 %all-reduce.5 = (f32[22]{0:T(128)S(1)}, f32[]{:T(128)}) all-reduce(f32[22]{0:T(128)S(1)} %get-tuple-element.104, f32[]{:T(128)} %get-tuple-element.105), channel_id=1, replica_groups=mesh['gx_0'=8,'gx_1'=2,'gy'=4,'gz'=8] {'gz'}, use_global_device_ids=true, to_apply=%region_16.0 | all-reduce | flops 23 | bytes 184 | tf_op jit(solution)/shard_map/psum | solution.py:29
  223.3 0.7 multiply_reduce_fusion.4
  224.0 0.4 fusion.36
  224.4 0.4 fusion.35
  226.0 0.7 fusion.13
  227.7 1.7 collective-permute-start.17
  229.4 1.4 collective-permute-start.15
  230.8 1.3 collective-permute-start.14
  232.1 7.9 %collective-permute-start.13 = (f32[1,8,128]{2,1,0:T(8,128)S(1)}, f32[1,8,128]{2,1,0:T(8,128)S(1)}, u32[]{:S(2)}, u32[]{:S(2)}) collective-permute-start(f32[1,8,128]{2,1,0:T(8,128)S(1)} %get-tuple-element.127), channel_id=1, source_target_pairs={{0,32},{32,64},{64,96},{96,128},{128,160},{160,192},{192,224},{224... | collective-permute-start | bytes 12296 | tf_op jit(solution)/shard_map/ppermute | solution.py:21
  240.0 1.9 collective-permute-start.12
  242.2 1.3 collective-permute-start.16
  243.6 3.6 %collective-permute-done.16 = f32[4,8,1]{2,1,0:T(8,128)S(1)} collective-permute-done((f32[4,8,1]{2,1,0:T(8,128)S(1)}, f32[4,8,1]{2,1,0:T(8,128)S(1)}, u32[]{:S(2)}, u32[]{:S(2)}) %collective-permute-start.16) | collective-permute-done | bytes 160 | tf_op jit(solution)/shard_map/ppermute | solution.py:22
  247.3 0.7 multiply_reduce_fusion
  247.9 0.5 convolution_bitcast_fusion.9
  248.4 13.3 %all-reduce.7 = (f32[23]{0:T(128)S(1)}, f32[]{:T(128)}) all-reduce(f32[23]{0:T(128)S(1)} %convolution_bitcast_fusion.9, f32[]{:T(128)} %get-tuple-element.116), channel_id=1, replica_groups=mesh['gx_0'=8,'gx_1'=2,'gy'=4,'gz'=8] {'gx_0'}, use_global_device_ids=true, to_apply=%region_22.0 | all-reduce | flops 24 | bytes 192 | tf_op jit(solution)/shard_map/psum | solution.py:29
  261.8 8.4 %all-reduce.13 = (f32[23]{0:T(128)S(1)}, f32[]{:T(128)}) all-reduce(f32[23]{0:T(128)S(1)} %get-tuple-element.96, f32[]{:T(128)} %get-tuple-element.97), channel_id=1, replica_groups=mesh['gx_0'=8,'gx_1'=2,'gy'=4,'gz'=8] {'gx_1'}, use_global_device_ids=true, to_apply=%region_23.0 | all-reduce | flops 24 | bytes 192 | tf_op jit(solution)/shard_map/psum | solution.py:29
  270.2 9.0 %all-reduce.10 = (f32[23]{0:T(128)S(1)}, f32[]{:T(128)}) all-reduce(f32[23]{0:T(128)S(1)} %get-tuple-element.108, f32[]{:T(128)} %get-tuple-element.109), channel_id=1, replica_groups=mesh['gx_0'=8,'gx_1'=2,'gy'=4,'gz'=8] {'gy'}, use_global_device_ids=true, to_apply=%region_24.0 | all-reduce | flops 24 | bytes 192 | tf_op jit(solution)/shard_map/psum | solution.py:29
  279.1 15.5 %all-reduce.4 = (f32[23]{0:T(128)S(1)}, f32[]{:T(128)}) all-reduce(f32[23]{0:T(128)S(1)} %get-tuple-element.102, f32[]{:T(128)} %get-tuple-element.103), channel_id=1, replica_groups=mesh['gx_0'=8,'gx_1'=2,'gy'=4,'gz'=8] {'gz'}, use_global_device_ids=true, to_apply=%region_25.0 | all-reduce | flops 24 | bytes 192 | tf_op jit(solution)/shard_map/psum | solution.py:29
  294.6 0.7 multiply_reduce_fusion.3
  295.4 0.8 fusion.14
  296.2 0.4 fusion.38
  296.5 0.4 fusion.37
  299.0 0.2 concatenate.165
  299.2 0.8 copy.15
  300.1 0.6 pad_maximum_fusion.29
  (53 shorter events, 1.6 us)
Async XLA Ops:
  0.6 1.2 copy-start
  0.6 3.1 %copy-start.3 = (f32[4,8,128]{2,1,0:T(8,128)S(1)}, f32[4,8,128]{2,1,0:T(8,128)}, u32[]{:S(2)}) copy-start(f32[4,8,128]{2,1,0:T(8,128)} %param.21) | copy-start | bytes 49156
  82.3 18.9 %collective-permute-start.5 = (f32[4,8,1]{2,1,0:T(8,128)S(1)}, f32[4,8,1]{2,1,0:T(8,128)S(1)}, u32[]{:S(2)}, u32[]{:S(2)}) collective-permute-start(f32[4,8,1]{2,1,0:T(8,128)S(1)} %get-tuple-element.143), channel_id=1, source_target_pairs={{0,1},{1,2},{2,3},{3,4},{4,5},{5,6},{6,7},{8,9},{9,10},{10,11},{11... | collective-permute-start | bytes 392 | tf_op jit(solution)/shard_map/ppermute | solution.py:21
  83.8 22.1 %collective-permute-start.3 = (f32[4,1,128]{2,1,0:T(1,128)S(1)}, f32[4,1,128]{2,1,0:T(1,128)S(1)}, u32[]{:S(2)}, u32[]{:S(2)}) collective-permute-start(f32[4,1,128]{2,1,0:T(1,128)S(1)} %get-tuple-element.141), channel_id=1, source_target_pairs={{0,8},{8,16},{16,24},{1,9},{9,17},{17,25},{2,10},{10,18},{18,26},{... | collective-permute-start | bytes 6152 | tf_op jit(solution)/shard_map/ppermute | solution.py:21
  85.1 20.8 %collective-permute-start.2 = (f32[4,1,128]{2,1,0:T(1,128)S(1)}, f32[4,1,128]{2,1,0:T(1,128)S(1)}, u32[]{:S(2)}, u32[]{:S(2)}) collective-permute-start(f32[4,1,128]{2,1,0:T(1,128)S(1)} %get-tuple-element.140), channel_id=1, source_target_pairs={{8,0},{16,8},{24,16},{9,1},{17,9},{25,17},{10,2},{18,10},{26,18},{... | collective-permute-start | bytes 6152 | tf_op jit(solution)/shard_map/ppermute | solution.py:22
  86.4 19.5 %collective-permute-start.1 = (f32[1,8,128]{2,1,0:T(8,128)S(1)}, f32[1,8,128]{2,1,0:T(8,128)S(1)}, u32[]{:S(2)}, u32[]{:S(2)}) collective-permute-start(f32[1,8,128]{2,1,0:T(8,128)S(1)} %get-tuple-element.139), channel_id=1, source_target_pairs={{0,32},{32,64},{64,96},{96,128},{128,160},{160,192},{192,224},{224... | collective-permute-start | bytes 12296 | tf_op jit(solution)/shard_map/ppermute | solution.py:21
  97.7 8.2 %collective-permute-start = (f32[1,8,128]{2,1,0:T(8,128)S(1)}, f32[1,8,128]{2,1,0:T(8,128)S(1)}, u32[]{:S(2)}, u32[]{:S(2)}) collective-permute-start(f32[1,8,128]{2,1,0:T(8,128)S(1)} %get-tuple-element.138), channel_id=1, source_target_pairs={{32,0},{64,32},{96,64},{128,96},{160,128},{192,160},{224,192},{256... | collective-permute-start | bytes 12296 | tf_op jit(solution)/shard_map/ppermute | solution.py:22
  101.2 4.6 %collective-permute-start.4 = (f32[4,8,1]{2,1,0:T(8,128)S(1)}, f32[4,8,1]{2,1,0:T(8,128)S(1)}, u32[]{:S(2)}, u32[]{:S(2)}) collective-permute-start(f32[4,8,1]{2,1,0:T(8,128)S(1)} %get-tuple-element.142), channel_id=1, source_target_pairs={{1,0},{2,1},{3,2},{4,3},{5,4},{6,5},{7,6},{9,8},{10,9},{11,10},{12... | collective-permute-start | bytes 392 | tf_op jit(solution)/shard_map/ppermute | solution.py:22
  102.5 3.4 %copy-start.1 = (f32[3,4,8,128]{3,2,1,0:T(8,128)S(1)}, f32[3,4,8,128]{3,2,1,0:T(8,128)}, u32[]{:S(2)}) copy-start(f32[3,4,8,128]{3,2,1,0:T(8,128)} %param.23) | copy-start | bytes 147460
  102.5 3.4 %copy-start.2 = (f32[4,8,128]{2,1,0:T(8,128)S(1)}, f32[4,8,128]{2,1,0:T(8,128)}, u32[]{:S(2)}) copy-start(f32[4,8,128]{2,1,0:T(8,128)} %param.22) | copy-start | bytes 49156
  155.7 15.2 %collective-permute-start.11 = (f32[4,8,1]{2,1,0:T(8,128)S(1)}, f32[4,8,1]{2,1,0:T(8,128)S(1)}, u32[]{:S(2)}, u32[]{:S(2)}) collective-permute-start(f32[4,8,1]{2,1,0:T(8,128)S(1)} %get-tuple-element.137), channel_id=1, source_target_pairs={{0,1},{1,2},{2,3},{3,4},{4,5},{5,6},{6,7},{8,9},{9,10},{10,11},{11... | collective-permute-start | bytes 392 | tf_op jit(solution)/shard_map/ppermute | solution.py:21
  157.3 18.7 %collective-permute-start.9 = (f32[4,1,128]{2,1,0:T(1,128)S(1)}, f32[4,1,128]{2,1,0:T(1,128)S(1)}, u32[]{:S(2)}, u32[]{:S(2)}) collective-permute-start(f32[4,1,128]{2,1,0:T(1,128)S(1)} %get-tuple-element.135), channel_id=1, source_target_pairs={{0,8},{8,16},{16,24},{1,9},{9,17},{17,25},{2,10},{10,18},{18,26},{... | collective-permute-start | bytes 6152 | tf_op jit(solution)/shard_map/ppermute | solution.py:21
  159.3 16.6 %collective-permute-start.8 = (f32[4,1,128]{2,1,0:T(1,128)S(1)}, f32[4,1,128]{2,1,0:T(1,128)S(1)}, u32[]{:S(2)}, u32[]{:S(2)}) collective-permute-start(f32[4,1,128]{2,1,0:T(1,128)S(1)} %get-tuple-element.134), channel_id=1, source_target_pairs={{8,0},{16,8},{24,16},{9,1},{17,9},{25,17},{10,2},{18,10},{26,18},{... | collective-permute-start | bytes 6152 | tf_op jit(solution)/shard_map/ppermute | solution.py:22
  160.6 15.3 %collective-permute-start.7 = (f32[1,8,128]{2,1,0:T(8,128)S(1)}, f32[1,8,128]{2,1,0:T(8,128)S(1)}, u32[]{:S(2)}, u32[]{:S(2)}) collective-permute-start(f32[1,8,128]{2,1,0:T(8,128)S(1)} %get-tuple-element.133), channel_id=1, source_target_pairs={{0,32},{32,64},{64,96},{96,128},{128,160},{160,192},{192,224},{224... | collective-permute-start | bytes 12296 | tf_op jit(solution)/shard_map/ppermute | solution.py:21
  168.7 7.3 %collective-permute-start.6 = (f32[1,8,128]{2,1,0:T(8,128)S(1)}, f32[1,8,128]{2,1,0:T(8,128)S(1)}, u32[]{:S(2)}, u32[]{:S(2)}) collective-permute-start(f32[1,8,128]{2,1,0:T(8,128)S(1)} %get-tuple-element.132), channel_id=1, source_target_pairs={{32,0},{64,32},{96,64},{128,96},{160,128},{192,160},{224,192},{256... | collective-permute-start | bytes 12296 | tf_op jit(solution)/shard_map/ppermute | solution.py:22
  170.9 5.0 %collective-permute-start.10 = (f32[4,8,1]{2,1,0:T(8,128)S(1)}, f32[4,8,1]{2,1,0:T(8,128)S(1)}, u32[]{:S(2)}, u32[]{:S(2)}) collective-permute-start(f32[4,8,1]{2,1,0:T(8,128)S(1)} %get-tuple-element.136), channel_id=1, source_target_pairs={{1,0},{2,1},{3,2},{4,3},{5,4},{6,5},{7,6},{9,8},{10,9},{11,10},{12... | collective-permute-start | bytes 392 | tf_op jit(solution)/shard_map/ppermute | solution.py:22
  227.7 14.5 %collective-permute-start.17 = (f32[4,8,1]{2,1,0:T(8,128)S(1)}, f32[4,8,1]{2,1,0:T(8,128)S(1)}, u32[]{:S(2)}, u32[]{:S(2)}) collective-permute-start(f32[4,8,1]{2,1,0:T(8,128)S(1)} %get-tuple-element.131), channel_id=1, source_target_pairs={{0,1},{1,2},{2,3},{3,4},{4,5},{5,6},{6,7},{8,9},{9,10},{10,11},{11... | collective-permute-start | bytes 392 | tf_op jit(solution)/shard_map/ppermute | solution.py:21
  229.4 17.8 %collective-permute-start.15 = (f32[4,1,128]{2,1,0:T(1,128)S(1)}, f32[4,1,128]{2,1,0:T(1,128)S(1)}, u32[]{:S(2)}, u32[]{:S(2)}) collective-permute-start(f32[4,1,128]{2,1,0:T(1,128)S(1)} %get-tuple-element.129), channel_id=1, source_target_pairs={{0,8},{8,16},{16,24},{1,9},{9,17},{17,25},{2,10},{10,18},{18,26},{... | collective-permute-start | bytes 6152 | tf_op jit(solution)/shard_map/ppermute | solution.py:21
  230.8 16.5 %collective-permute-start.14 = (f32[4,1,128]{2,1,0:T(1,128)S(1)}, f32[4,1,128]{2,1,0:T(1,128)S(1)}, u32[]{:S(2)}, u32[]{:S(2)}) collective-permute-start(f32[4,1,128]{2,1,0:T(1,128)S(1)} %get-tuple-element.128), channel_id=1, source_target_pairs={{8,0},{16,8},{24,16},{9,1},{17,9},{25,17},{10,2},{18,10},{26,18},{... | collective-permute-start | bytes 6152 | tf_op jit(solution)/shard_map/ppermute | solution.py:22
  232.1 15.2 %collective-permute-start.13 = (f32[1,8,128]{2,1,0:T(8,128)S(1)}, f32[1,8,128]{2,1,0:T(8,128)S(1)}, u32[]{:S(2)}, u32[]{:S(2)}) collective-permute-start(f32[1,8,128]{2,1,0:T(8,128)S(1)} %get-tuple-element.127), channel_id=1, source_target_pairs={{0,32},{32,64},{64,96},{96,128},{128,160},{160,192},{192,224},{224... | collective-permute-start | bytes 12296 | tf_op jit(solution)/shard_map/ppermute | solution.py:21
  240.0 7.3 %collective-permute-start.12 = (f32[1,8,128]{2,1,0:T(8,128)S(1)}, f32[1,8,128]{2,1,0:T(8,128)S(1)}, u32[]{:S(2)}, u32[]{:S(2)}) collective-permute-start(f32[1,8,128]{2,1,0:T(8,128)S(1)} %get-tuple-element.126), channel_id=1, source_target_pairs={{32,0},{64,32},{96,64},{128,96},{160,128},{192,160},{224,192},{256... | collective-permute-start | bytes 12296 | tf_op jit(solution)/shard_map/ppermute | solution.py:22
  242.2 5.0 %collective-permute-start.16 = (f32[4,8,1]{2,1,0:T(8,128)S(1)}, f32[4,8,1]{2,1,0:T(8,128)S(1)}, u32[]{:S(2)}, u32[]{:S(2)}) collective-permute-start(f32[4,8,1]{2,1,0:T(8,128)S(1)} %get-tuple-element.130), channel_id=1, source_target_pairs={{1,0},{2,1},{3,2},{4,3},{5,4},{6,5},{7,6},{9,8},{10,9},{11,10},{12... | collective-permute-start | bytes 392 | tf_op jit(solution)/shard_map/ppermute | solution.py:22
where the time goes:
time: 305 us; the launch traced here: 301 us
  blocking collectives  213 us (70%)
  starting transfers between devices  51.3 us (17%)
  matrix products  10.7 us (4%)
  waiting for transfers between devices  10.4 us (3%)
  between operations  7.85 us (3%)
  local copies, waits for them, and re-layouts  4 us (1%)
  other arithmetic  3.16 us (1%)
    psum x16, blocking collectives, by_axis(): value = lax.psum(value, axis)  213 us
    ppermute x9, starting transfers between devices, with_halo(): before = lax.ppermute(last, axis, up)  36.6 us
    ppermute x9, starting transfers between devices, with_halo(): after = lax.ppermute(initial, axis, down)  14.7 us
    ppermute x9, waiting for transfers between devices, with_halo(): after = lax.ppermute(initial, axis, down)  10.3 us
  transfers between devices with their start and end apart: 18, of which 3 were waited for; matrix products, arithmetic and copies ran while one was open for 0% of the time, Pallas kernels for 0%

commit v1 on v0

v1 whole, which is shorter than its diff:
```python
import functools

import jax
import jax.numpy as jnp
from jax import lax
from jax.experimental import pallas as pl
from jax.experimental.pallas import tpu as pltpu
from jax.sharding import Mesh
from jax.sharding import PartitionSpec as P

KEEP = 20
EXPAND = 3
ROWS = 24
FIELDS = 25
SPAN = 64
SIGMA = 7.125
GX = ("gx_0", "gx_1")
X, Y, Z = (4, 8, 128)
TILE = (Y, Z)
F32 = jnp.float32


def rows_of():
    return lax.broadcasted_iota(jnp.int32, TILE, 0)


def lanes_of():
    return lax.broadcasted_iota(jnp.int32, TILE, 1)


def shift_rows(tile, by):
    by = by % Y
    return tile if by == 0 else pltpu.roll(tile, by, 0)


def shift_lanes(tile, by):
    return pltpu.roll(tile, by, 1)


def vmem():
    return pl.BlockSpec(memory_space=pltpu.VMEM)


def call(kernel, outs, args, scratch=(), smem=(), flops=100000):
    return pl.pallas_call(
        kernel,
        out_shape=[jax.ShapeDtypeStruct(s, F32) for s in outs],
        in_specs=[
            pl.BlockSpec(memory_space=pltpu.SMEM) if i in smem else vmem() for i in range(len(args))
        ],
        out_specs=[vmem() for _ in outs],
        scratch_shapes=list(scratch),
        cost_estimate=pl.CostEstimate(flops=flops, bytes_accessed=100000, transcendentals=0),
    )(*args)


def rotate_kernel(basis, schur, next_vector, diag, velocity, fields, packed):
    group = 5
    for g in range(KEEP // group):

        def body(i, acc, g=g):
            out = []
            tiles = [basis[i, x] for x in range(X)]
            for f in range(group):
                w = schur[i, g * group + f]
                for x in range(X):
                    out.append(acc[f * X + x] + w * tiles[x])
            return tuple(out)

        zero = tuple(jnp.zeros(TILE, F32) for _ in range(group * X))
        acc = lax.fori_loop(0, basis.shape[0], body, zero, unroll=4)
        for f in range(group):
            for x in range(X):
                fields[g * group + f, x] = acc[f * X + x]
    for x in range(X):
        fields[20, x] = next_vector[x]
        fields[21, x] = 6.0 + diag[x]
        for d in range(3):
            fields[22 + d, x] = 0.5 * velocity[d, x]
    lane = lanes_of()
    for p in range(5):
        total = jnp.zeros(TILE, F32)
        for j in range(20):
            tile = fields[5 * p + j // 4, j % 4]
            moved = shift_lanes(tile, 6 * j + 3)
            total = jnp.where((lane >= 6 * j) & (lane < 6 * j + 6), moved, total)
        packed[p] = total


def pack_y_kernel(fields, from_lo, from_hi, up, down, halo):
    row, lane = rows_of(), lanes_of()
    left = lax.rem(lane, 6) < 3
    for f in range(FIELDS):
        a = jnp.zeros(TILE, F32)
        b = a
        for x in range(X):
            tile = fields[f, x]
            here = (row >= 2 * x) & (row < 2 * x + 2)
            a = jnp.where(here, shift_rows(tile, 2 * x - 6), a)
            b = jnp.where(here, shift_rows(tile, 2 * x), b)
        up[f] = a
        down[f] = b
    a = jnp.zeros(TILE, F32)
    b = a
    for x in range(X):
        tile = fields[20, x]
        a = jnp.where(row == x, shift_rows(tile, x - 5), a)
        b = jnp.where(row == x, shift_rows(tile, x - 2), b)
    up[25] = a
    down[25] = b
    for p in range(5):
        merged = jnp.where(left, from_lo[p], from_hi[p])
        halo[p] = merged
        up[26 + p] = merged
        down[26 + p] = merged


def pack_x_kernel(fields, halo, y_lo, y_hi, up, down):
    first = rows_of() < 4
    for f in range(FIELDS):
        up[2 * f] = fields[f, 2]
        up[2 * f + 1] = fields[f, 3]
        down[2 * f] = fields[f, 0]
        down[2 * f + 1] = fields[f, 1]
        lo, hi = y_lo[f], y_hi[f]
        up[51 + f] = jnp.where(first, shift_rows(lo, 4), hi)
        down[51 + f] = jnp.where(first, lo, shift_rows(hi, 4))
    up[50] = fields[20, 1]
    down[50] = fields[20, 2]
    for out in (up, down):
        for p in range(5):
            out[76 + p] = halo[p]
        out[81] = y_lo[30]
        out[82] = y_hi[30]


def region(radius):
    out = []
    for a, b in ((0, 0), (1, 0), (0, 1), (1, 1)):
        for x in range(-radius + a + b, X + radius - a - b):
            out.append((x, a, b))
    return out


COEF = region(2)


def tile_of(f, key, refs):
    fields, halo, y_lo, y_hi, x_lo, x_hi, y_halo, x_corner = refs
    x, a, b = key
    first = rows_of() < 4
    if b == 0:
        if a == 0:
            if 0 <= x < X:
                return fields[f, x]
            if x == -3:
                return x_lo[50]
            if x == 6:
                return x_hi[50]
            return x_lo[2 * f + x + 2] if x < 0 else x_hi[2 * f + x - 4]
        if 0 <= x < X:
            lo, hi = y_lo[f], y_hi[f]
            tile = jnp.where(first, shift_rows(hi, -2 * x), shift_rows(lo, 6 - 2 * x))
            if isinstance(f, int) and f == 20:
                row = rows_of()
                tile = jnp.where(row == 2, shift_rows(y_hi[25], 2 - x), tile)
                tile = jnp.where(row == 5, shift_rows(y_lo[25], 5 - x), tile)
            return tile
        packed = (x_lo if x < 0 else x_hi)[51 + f]
        if x in (-1, 5):
            return jnp.where(first, shift_rows(packed, 2), shift_rows(packed, 4))
        return jnp.where(first, shift_rows(packed, 4), shift_rows(packed, 6))
    p, q = (f // 5, f % 5) if isinstance(f, int) else (lax.div(f, 5), lax.rem(f, 5))
    place = x if 0 <= x < X else (x + X if x < 0 else x - X)
    by = 128 - 3 - 6 * (4 * q + place)
    if a == 0:
        packed = halo[p] if 0 <= x < X else (x_lo if x < 0 else x_hi)[76 + p]
    elif 0 <= x < X:
        packed = y_halo[p]
    else:
        packed = x_corner[0 if x < 0 else 1]
    return shift_lanes(packed, by)


def apply(get, key, coef):
    x, a, b = key
    row, lane = rows_of(), lanes_of()
    base = COEF.index(key)
    centre = get((x, a, b))
    y_other = get((x, 1 - a, b))
    z_other = get((x, a, 1 - b))
    y_ahead = shift_rows(jnp.where(row == 0, y_other, centre), 7)
    y_behind = shift_rows(jnp.where(row == 7, y_other, centre), 1)
    z_ahead = shift_lanes(jnp.where(lane == 0, z_other, centre), 127)
    z_behind = shift_lanes(jnp.where(lane == 127, z_other, centre), 1)
    near = (
        centre,
        get((x + 1, a, b)),
        get((x - 1, a, b)),
        y_ahead,
        y_behind,
        z_ahead,
        z_behind,
    )
    terms = [coef[base, i] * near[i] for i in range(7)]
    return (terms[0] + (terms[1] + terms[2])) + ((terms[3] + terms[4]) + (terms[5] + terms[6]))


def stencil_kernel(
    copies, fields, halo, y_lo, y_hi, x_lo, x_hi, span, gram, coef, y_halo, x_corner, chain
):
    refs = (fields, halo, y_lo, y_hi, x_lo, x_hi, y_halo, x_corner)
    first = rows_of() < 4
    for p in range(5):
        y_halo[p] = jnp.where(first, y_hi[26 + p], y_lo[26 + p])
    x_corner[0] = jnp.where(first, x_lo[82], x_lo[81])
    x_corner[1] = jnp.where(first, x_hi[82], x_hi[81])
    for at, key in enumerate(COEF):
        diagonal = tile_of(21, key, refs)
        inside = diagonal != 0.0
        coef[at, 0] = jnp.where(inside, diagonal - SIGMA, 0.0)
        for d in range(3):
            half = tile_of(22 + d, key, refs)
            coef[at, 1 + 2 * d] = jnp.where(inside, half - 1.0, 0.0)
            coef[at, 2 + 2 * d] = jnp.where(inside, -1.0 - half, 0.0)

    def store(f, x, tile):
        at = f * (X * Y) + x * Y
        if not isinstance(f, int):
            at = pl.multiple_of(at, Y)
        span[pl.ds(at, Y), :] = tile

    tiles = {key: tile_of(20, key, refs) for key in region(3)}
    for x in range(X):
        store(60, x, tiles[(x, 0, 0)])
    for step in range(EXPAND):
        place = {}
        for at, key in enumerate(tiles):
            chain[at] = tiles[key]
            place[key] = at
        get = lambda key, place=place: chain[place[key]]
        tiles = {key: apply(get, key, coef) for key in region(2 - step)}
        for x in range(X):
            store(61 + step, x, tiles[(x, 0, 0)])

    def body(f, carry):
        held = {}

        def get(key):
            if key not in held:
                held[key] = tile_of(f, key, refs)
            return held[key]

        once = {key: apply(get, key, coef) for key in region(1)}
        for x in range(X):
            store(f, x, get((x, 0, 0)))
            store(f + 20, x, once[(x, 0, 0)])
        for x in range(X):
            store(f + 40, x, apply(once.__getitem__, (x, 0, 0), coef))
        return carry

    lax.fori_loop(0, KEEP, body, 0)

    total = jnp.zeros((SPAN, SPAN), F32)
    for r in range(0, X * Y, 2):
        pair = [span[pl.ds(r + i, SPAN, stride=X * Y), :] for i in range(2)]
        rows = jnp.concatenate(pair, axis=1)
        total = total + lax.dot_general(
            rows,
            rows,
            (((1,), (1,)), ((), ())),
            precision=lax.Precision.HIGHEST,
            preferred_element_type=F32,
        )
    packed = jnp.concatenate([total[:32], total[32:]], axis=1)
    for i in range(copies):
        gram[i] = packed


def sum_kernel(copies, parts, out):
    total = parts[0]
    for i in range(1, parts.shape[0]):
        total = total + parts[i]
    for i in range(copies):
        out[i] = total


def exchange(parts, axis):
    return lax.all_to_all(parts, axis, 0, 0)


def finish_kernel(cell_count, parts, span, basis, hessenberg, spread):
    total = parts[0]
    for i in range(1, parts.shape[0]):
        total = total + parts[i]
    total = total * (1.0 / cell_count)
    lane = lax.broadcasted_iota(jnp.int32, (32, Z), 1)
    gram = jnp.concatenate(
        [jnp.where(lane < SPAN, total, 0.0), jnp.where(lane < SPAN, pltpu.roll(total, 64, 1), 0.0)],
        axis=0,
    )
    row64 = lax.broadcasted_iota(jnp.int32, (SPAN, Z), 0)
    lane64 = lax.broadcasted_iota(jnp.int32, (SPAN, Z), 1)
    eye = row64 == lane64
    row = lax.broadcasted_iota(jnp.int32, (ROWS, Z), 0)
    lane = lax.broadcasted_iota(jnp.int32, (ROWS, Z), 1)
    lane1 = lax.broadcasted_iota(jnp.int32, (1, Z), 1)

    def column(vector):
        return jnp.sum(jnp.where(eye, vector, 0.0), axis=1, keepdims=True)

    first_row = gram[60:61, :]
    norm_sq = jnp.sum(jnp.where(lane1 == 60, first_row, 0.0), axis=1, keepdims=True)
    inverse = 1.0 / jnp.maximum(jnp.sqrt(norm_sq), 0.5)
    last = jnp.where(lane1 == 60, inverse, 0.0)
    last_gram = first_row * inverse
    q = jnp.where((row == lane) & (row < KEEP), 1.0, 0.0)
    q = jnp.where(row == KEEP, last, q)
    qg = jnp.where(row < KEEP, gram[:ROWS, :], 0.0)
    qg = jnp.where(row == KEEP, last_gram, qg)
    spread[3] = jnp.broadcast_to(inverse, TILE)
    columns = []
    for k in range(EXPAND):
        up = jnp.where(
            (lane1 >= KEEP) & (lane1 < 60),
            pltpu.roll(last, KEEP, 1),
            jnp.where((lane1 > 60) & (lane1 < SPAN), pltpu.roll(last, 1, 1), 0.0),
        )
        image = up + SIGMA * last
        image_gram = jnp.sum(column(up) * gram, axis=0, keepdims=True) + SIGMA * last_gram
        c = jnp.sum(q * image_gram, axis=1, keepdims=True)
        partly = image - jnp.sum(c * q, axis=0, keepdims=True)
        partly_gram = image_gram - jnp.sum(c * qg, axis=0, keepdims=True)
        e = jnp.sum(q * partly_gram, axis=1, keepdims=True)
        cleaned = partly - jnp.sum(e * q, axis=0, keepdims=True)
        cleaned_gram = partly_gram - jnp.sum(e * qg, axis=0, keepdims=True)
        length_sq = jnp.sum(cleaned * cleaned_gram, axis=1, keepdims=True)
        length = jnp.sqrt(jnp.maximum(length_sq, 0.0))
        inverse = 1.0 / jnp.maximum(length, 0.5)
        last = cleaned * inverse
        last_gram = cleaned_gram * inverse
        q = jnp.where(row == KEEP + 1 + k, last, q)
        qg = jnp.where(row == KEEP + 1 + k, last_gram, qg)
        columns.append(jnp.where(row == KEEP + 1 + k, length, c + e))
        spread[pl.ds(4 + 8 * k, 8)] = jnp.broadcast_to(column(last), (SPAN, Z)).reshape(8, 8, Z)
    hessenberg[...] = jnp.where(lane == 0, columns[0], jnp.where(lane == 1, columns[1], columns[2]))[
        :, :EXPAND
    ]

    for f in range(KEEP):
        basis[f] = span[f]
    for x in range(X):
        basis[KEEP, x] = span[60, x] * spread[3]
    acc = [[jnp.zeros(TILE, F32) for _ in range(X)] for _ in range(EXPAND)]
    for f in range(SPAN):
        tiles = [span[f, x] for x in range(X)]
        for k in range(EXPAND):
            w = spread[4 + 8 * k + f // 8, f % 8 : f % 8 + 1, :]
            for x in range(X):
                acc[k][x] = acc[k][x] + w * tiles[x]
    for k in range(EXPAND):
        for x in range(X):
            basis[KEEP + 1 + k, x] = acc[k][x]


def send(value, axis, forward):
    count = lax.axis_size(axis)
    up = [(i, i + 1) for i in range(count - 1)]
    return lax.ppermute(value, axis, up if forward else [(j, i) for i, j in up])


def per_device(krylov_basis, schur_vectors, next_vector, diag_shift, velocity):
    axes = (*GX, "gy", "gz")
    cell_count = next_vector.size
    for axis in axes:
        cell_count *= lax.axis_size(axis)
    fields, packed = call(
        rotate_kernel,
        [(FIELDS, X, Y, Z), (5, Y, Z)],
        [krylov_basis, schur_vectors, next_vector, diag_shift, velocity],
        smem=(1,),
    )
    z_lo, z_hi = send(packed, "gz", True), send(packed, "gz", False)
    up, down, halo = call(
        pack_y_kernel, [(31, Y, Z), (31, Y, Z), (5, Y, Z)], [fields, z_lo, z_hi]
    )
    y_lo, y_hi = send(up, "gy", True), send(down, "gy", False)
    up, down = call(pack_x_kernel, [(83, Y, Z), (83, Y, Z)], [fields, halo, y_lo, y_hi])
    x_lo, x_hi = send(up, GX, True), send(down, GX, False)
    stages = (("gx_1", "gy"), ("gz",), ("gx_0",))
    sizes = []
    for stage in stages:
        size = 1
        for axis in stage:
            size *= lax.axis_size(axis)
        sizes.append(size)
    span, parts = call(
        functools.partial(stencil_kernel, sizes[0]),
        [(SPAN * X * Y, Z), (sizes[0], 32, Z)],
        [fields, halo, y_lo, y_hi, x_lo, x_hi],
        scratch=[
            pltpu.VMEM((len(COEF), 7, Y, Z), F32),
            pltpu.VMEM((5, Y, Z), F32),
            pltpu.VMEM((2, Y, Z), F32),
            pltpu.VMEM((len(region(3)), Y, Z), F32),
        ],
    )
    for i, stage in enumerate(stages):
        parts = exchange(parts, stage)
        if i + 1 < len(stages):
            (parts,) = call(
                functools.partial(sum_kernel, sizes[i + 1]), [(sizes[i + 1], 32, Z)], [parts]
            )
    basis, hessenberg = call(
        functools.partial(finish_kernel, cell_count),
        [(ROWS, X, Y, Z), (ROWS, EXPAND)],
        [parts, span.reshape(SPAN, X, Y, Z)],
        scratch=[pltpu.VMEM((4 + 8 * EXPAND, Y, Z), F32)],
    )
    return basis, hessenberg


def solution(mesh):
    split = Mesh(
        mesh.devices.reshape(-1, 2, mesh.shape["gy"], mesh.shape["gz"]),
        ("gx_0", "gx_1", "gy", "gz"),
    )
    return jax.shard_map(
        per_device,
        mesh=split,
        in_specs=(
            P(None, GX, "gy", "gz"),
            P(),
            P(GX, "gy", "gz"),
            P(GX, "gy", "gz"),
            P(None, GX, "gy", "gz"),
        ),
        out_specs=(P(None, GX, "gy", "gz"), P()),
        check_vma=False,
    )
```

time: 305 us -> 106 us (0.35)
  the two profiles are of different devices: /device:TPU:1 before, /device:TPU:2 now
where the time goes in v1:
time: 106 us
  blocking collectives  51.5 us (49%)
  Pallas kernels  23 us (22%)
  starting transfers between devices  17.5 us (17%)
  waiting for transfers between devices  8.04 us (8%)
  local copies, waits for them, and re-layouts  4.74 us (4%)
    all_to_all x3, blocking collectives, exchange(): return lax.all_to_all(parts, axis, 0, 0)  51.5 us
    pallas_call x7, Pallas kernels, call(): pl.pallas_call(kernel, out_shape=[jax.ShapeDtypeStruct(s, F32) for s in o...  23 us
    ppermute x6, starting transfers between devices, send(): return lax.ppermute(value, axis, up if forward else [(j, i) for i, j in up])  17.5 us
    ppermute x6, waiting for transfers between devices, send(): return lax.ppermute(value, axis, up if forward else [(j, i) for i, j in up])  8.04 us
    unnamed x13, local copies, waits for them, and re-layouts  3.39 us
  transfers between devices with their start and end apart: 6, of which 5 were waited for; matrix products, arithmetic and copies ran while one was open for 0% of the time, Pallas kernels for 0%

profile of v1, /device:TPU:2, one launch (start us, length us, event | category | flops | bytes accessed | tf_op | source)
XLA Modules:
  0.0 105.5 jit_solution(4143446804905663988)
XLA Ops:
  0.6 1.4 %copy.7.schur = f32[60,20]{1,0:T(8,128)} copy(f32[60,20]{0,1:T(8,128)} %param.6) | data formatting | bytes 9600 | tf_op args[1]
  2.0 4.1 %shard_map.68 = (f32[25,4,8,128]{3,2,1,0:T(8,128)}, f32[5,8,128]{2,1,0:T(8,128)}) custom-call(f32[60,4,8,128]{3,2,1,0:T(8,128)} %basis.1, f32[60,20]{1,0:T(8,128)} %copy.7.schur, f32[4,8,128]{2,1,0:T(8,128)} %next_vector.1, f32[4,8,128]{2,1,0:T(8,128)} %diag.1, f32[3,4,8,128]{3,2,1,0:T(8,128)} %velocity.1), custom_call_target="tpu_custom_call" | custom-call | flops 100000 | bytes 100000 | tf_op jit(solution)/shard_map/pallas_call | solution.py:45
  6.2 1.3 %collective-permute-start.1 = (f32[5,8,128]{2,1,0:T(8,128)}, f32[5,8,128]{2,1,0:T(8,128)S(1)}, u32[]{:S(2)}, u32[]{:S(2)}) collective-permute-start(f32[5,8,128]{2,1,0:T(8,128)} %get-tuple-element.12), channel_id=1, source_target_pairs={{1,0},{2,1},{3,2},{4,3},{5,4},{6,5},{7,6},{9,8},{10,9},{11,10},{12... | collective-permute-start | bytes 61448 | tf_op jit(solution)/shard_map/ppermute | solution.py:369
  7.4 4.5 %collective-permute-start = (f32[5,8,128]{2,1,0:T(8,128)}, f32[5,8,128]{2,1,0:T(8,128)S(1)}, u32[]{:S(2)}, u32[]{:S(2)}) collective-permute-start(f32[5,8,128]{2,1,0:T(8,128)} %get-tuple-element.12), channel_id=1, source_target_pairs={{0,1},{1,2},{2,3},{3,4},{4,5},{5,6},{6,7},{8,9},{9,10},{10,11},{11... | collective-permute-start | bytes 61448 | tf_op jit(solution)/shard_map/ppermute | solution.py:369
  12.0 0.0 collective-permute-done.1.from_hi
  12.0 0.0 copy-start.4
  12.0 1.6 %collective-permute-done.from_lo = f32[5,8,128]{2,1,0:T(8,128)S(1)} collective-permute-done((f32[5,8,128]{2,1,0:T(8,128)}, f32[5,8,128]{2,1,0:T(8,128)S(1)}, u32[]{:S(2)}, u32[]{:S(2)}) %collective-permute-start) | collective-permute-done | bytes 20512 | tf_op jit(solution)/shard_map/ppermute | solution.py:369
  13.7 0.0 copy-start.5
  13.7 0.0 copy-done.4
  13.7 0.6 copy-done.5
  14.3 1.8 %shard_map.69 = (f32[31,8,128]{2,1,0:T(8,128)}, f32[31,8,128]{2,1,0:T(8,128)}, f32[5,8,128]{2,1,0:T(8,128)}) custom-call(f32[25,4,8,128]{3,2,1,0:T(8,128)} %get-tuple-element.11.fields, f32[5,8,128]{2,1,0:T(8,128)} %copy-done.5, f32[5,8,128]{2,1,0:T(8,128)} %copy-done.4), custom_call_target="tpu_custom_call" | custom-call | flops 100000 | bytes 100000 | tf_op jit(solution)/shard_map/pallas_call | solution.py:45
  16.0 3.4 %collective-permute-start.2 = (f32[31,8,128]{2,1,0:T(8,128)}, f32[31,8,128]{2,1,0:T(8,128)S(1)}, u32[]{:S(2)}, u32[]{:S(2)}) collective-permute-start(f32[31,8,128]{2,1,0:T(8,128)} %get-tuple-element.14), channel_id=1, source_target_pairs={{0,8},{8,16},{16,24},{1,9},{9,17},{17,25},{2,10},{10,18},{18,26},{... | collective-permute-start | bytes 380936 | tf_op jit(solution)/shard_map/ppermute | solution.py:369
  19.4 5.7 %collective-permute-start.3 = (f32[31,8,128]{2,1,0:T(8,128)}, f32[31,8,128]{2,1,0:T(8,128)S(1)}, u32[]{:S(2)}, u32[]{:S(2)}) collective-permute-start(f32[31,8,128]{2,1,0:T(8,128)} %get-tuple-element.15), channel_id=1, source_target_pairs={{8,0},{16,8},{24,16},{9,1},{17,9},{25,17},{10,2},{18,10},{26,18},{... | collective-permute-start | bytes 380936 | tf_op jit(solution)/shard_map/ppermute | solution.py:369
  25.1 1.2 %collective-permute-done.2.y_lo = f32[31,8,128]{2,1,0:T(8,128)S(1)} collective-permute-done((f32[31,8,128]{2,1,0:T(8,128)}, f32[31,8,128]{2,1,0:T(8,128)S(1)}, u32[]{:S(2)}, u32[]{:S(2)}) %collective-permute-start.2) | collective-permute-done | bytes 127008 | tf_op jit(solution)/shard_map/ppermute | solution.py:369
  26.3 0.0 copy-start
  26.3 1.6 %collective-permute-done.3.y_hi = f32[31,8,128]{2,1,0:T(8,128)S(1)} collective-permute-done((f32[31,8,128]{2,1,0:T(8,128)}, f32[31,8,128]{2,1,0:T(8,128)S(1)}, u32[]{:S(2)}, u32[]{:S(2)}) %collective-permute-start.3) | collective-permute-done | bytes 127008 | tf_op jit(solution)/shard_map/ppermute | solution.py:369
  27.9 0.0 copy-start.1
  27.9 0.0 copy-done
  27.9 0.6 copy-done.1
  28.5 2.0 %shard_map.70 = (f32[83,8,128]{2,1,0:T(8,128)}, f32[83,8,128]{2,1,0:T(8,128)}) custom-call(f32[25,4,8,128]{3,2,1,0:T(8,128)} %get-tuple-element.11.fields, f32[5,8,128]{2,1,0:T(8,128)} %get-tuple-element.13.halo, f32[31,8,128]{2,1,0:T(8,128)} %copy-done, f32[31,8,128]{2,1,0:T(8,128)} %copy-done.1), custom_call_target="tpu_custom_call" | custom-call | flops 100000 | bytes 100000 | tf_op jit(solution)/shard_map/pallas_call | solution.py:45
  30.5 1.3 %collective-permute-start.4 = (f32[83,8,128]{2,1,0:T(8,128)}, f32[83,8,128]{2,1,0:T(8,128)S(1)}, u32[]{:S(2)}, u32[]{:S(2)}) collective-permute-start(f32[83,8,128]{2,1,0:T(8,128)} %get-tuple-element.16), channel_id=1, source_target_pairs={{0,32},{32,64},{64,96},{96,128},{128,160},{160,192},{192,224},{224... | collective-permute-start | bytes 1019912 | tf_op jit(solution)/shard_map/ppermute | solution.py:369
  31.8 1.3 %collective-permute-start.5 = (f32[83,8,128]{2,1,0:T(8,128)}, f32[83,8,128]{2,1,0:T(8,128)S(1)}, u32[]{:S(2)}, u32[]{:S(2)}) collective-permute-start(f32[83,8,128]{2,1,0:T(8,128)} %get-tuple-element.17), channel_id=1, source_target_pairs={{32,0},{64,32},{96,64},{128,96},{160,128},{192,160},{224,192},{256... | collective-permute-start | bytes 1019912 | tf_op jit(solution)/shard_map/ppermute | solution.py:369
  33.1 0.1 collective-permute-done.4.x_lo
  33.3 0.0 copy-start.2
  33.3 3.4 %collective-permute-done.5.x_hi = f32[83,8,128]{2,1,0:T(8,128)S(1)} collective-permute-done((f32[83,8,128]{2,1,0:T(8,128)}, f32[83,8,128]{2,1,0:T(8,128)S(1)}, u32[]{:S(2)}, u32[]{:S(2)}) %collective-permute-start.5) | collective-permute-done | bytes 340000 | tf_op jit(solution)/shard_map/ppermute | solution.py:369
  36.7 0.0 copy-done.2
  36.7 0.0 copy-start.3
  36.7 0.7 copy-done.3
  37.5 8.2 %shard_map.71 = (f32[2048,128]{1,0:T(8,128)}, f32[8,32,128]{2,1,0:T(8,128)}) custom-call(f32[25,4,8,128]{3,2,1,0:T(8,128)} %get-tuple-element.11.fields, f32[5,8,128]{2,1,0:T(8,128)} %get-tuple-element.13.halo, f32[31,8,128]{2,1,0:T(8,128)} %copy-done, f32[31,8,128]{2,1,0:T(8,128)} %copy-done.1, f32[83,8,128]{2,1,0:T(8,128)} %copy-done.2, ...), custom_call_target="tpu_custom_call" | custom-call | flops 100000 | bytes 100000 | tf_op jit(solution)/shard_map/pallas_call | solution.py:45
  45.7 14.2 %all_to_all.15.parts = f32[8,32,128]{2,1,0:T(8,128)} all-to-all(f32[8,32,128]{2,1,0:T(8,128)} %get-tuple-element.18), channel_id=1, replica_groups=mesh['gx_0'=8,'gx_1'=2,'gy'=4,'gz'=8] {'gx_1','gy'}, dimensions={0} | all-to-all | bytes 262144 | tf_op jit(solution)/shard_map/all_to_all | solution.py:289
  59.9 1.6 %shard_map.72 = f32[8,32,128]{2,1,0:T(8,128)} custom-call(f32[8,32,128]{2,1,0:T(8,128)} %all_to_all.15.parts), custom_call_target="tpu_custom_call" | custom-call | flops 100000 | bytes 100000 | tf_op jit(solution)/shard_map/pallas_call | solution.py:45
  61.5 18.5 %all_to_all.16.parts = f32[8,32,128]{2,1,0:T(8,128)} all-to-all(f32[8,32,128]{2,1,0:T(8,128)} %shard_map.72), channel_id=1, replica_groups=mesh['gx_0'=8,'gx_1'=2,'gy'=4,'gz'=8] {'gz'}, dimensions={0} | all-to-all | bytes 262144 | tf_op jit(solution)/shard_map/all_to_all | solution.py:289
  79.9 1.6 %shard_map.73 = f32[8,32,128]{2,1,0:T(8,128)} custom-call(f32[8,32,128]{2,1,0:T(8,128)} %all_to_all.16.parts), custom_call_target="tpu_custom_call" | custom-call | flops 100000 | bytes 100000 | tf_op jit(solution)/shard_map/pallas_call | solution.py:45
  81.5 18.9 %all_to_all.17.parts = f32[8,32,128]{2,1,0:T(8,128)} all-to-all(f32[8,32,128]{2,1,0:T(8,128)} %shard_map.73), channel_id=1, replica_groups=mesh['gx_0'=8,'gx_1'=2,'gy'=4,'gz'=8] {'gx_0'}, dimensions={0} | all-to-all | bytes 262144 | tf_op jit(solution)/shard_map/all_to_all | solution.py:289
  100.4 3.8 %shard_map.74 = (f32[24,4,8,128]{3,2,1,0:T(8,128)}, f32[24,3]{1,0:T(8,128)}) custom-call(f32[8,32,128]{2,1,0:T(8,128)} %all_to_all.17.parts, f32[64,4,8,128]{3,2,1,0:T(8,128)} %bitcast.1), custom_call_target="tpu_custom_call" | custom-call | flops 100000 | bytes 100000 | tf_op jit(solution)/shard_map/pallas_call | solution.py:45
  104.2 1.4 %copy.8 = f32[24,3]{0,1:T(4,128)} copy(f32[24,3]{1,0:T(8,128)} %get-tuple-element.21) | data formatting | bytes 576 | tf_op jit(solution)/shard_map/pallas_call | solution.py:45
Async XLA Ops:
  6.2 5.9 %collective-permute-start.1 = (f32[5,8,128]{2,1,0:T(8,128)}, f32[5,8,128]{2,1,0:T(8,128)S(1)}, u32[]{:S(2)}, u32[]{:S(2)}) collective-permute-start(f32[5,8,128]{2,1,0:T(8,128)} %get-tuple-element.12), channel_id=1, source_target_pairs={{1,0},{2,1},{3,2},{4,3},{5,4},{6,5},{7,6},{9,8},{10,9},{11,10},{12... | collective-permute-start | bytes 61448 | tf_op jit(solution)/shard_map/ppermute | solution.py:369
  7.4 6.2 %collective-permute-start = (f32[5,8,128]{2,1,0:T(8,128)}, f32[5,8,128]{2,1,0:T(8,128)S(1)}, u32[]{:S(2)}, u32[]{:S(2)}) collective-permute-start(f32[5,8,128]{2,1,0:T(8,128)} %get-tuple-element.12), channel_id=1, source_target_pairs={{0,1},{1,2},{2,3},{3,4},{4,5},{5,6},{6,7},{8,9},{9,10},{10,11},{11... | collective-permute-start | bytes 61448 | tf_op jit(solution)/shard_map/ppermute | solution.py:369
  12.0 1.6 %copy-start.4 = (f32[5,8,128]{2,1,0:T(8,128)}, f32[5,8,128]{2,1,0:T(8,128)S(1)}, u32[]{:S(2)}) copy-start(f32[5,8,128]{2,1,0:T(8,128)S(1)} %collective-permute-done.1.from_hi) | copy-start | bytes 61444
  13.7 0.6 copy-start.5
  16.0 10.3 %collective-permute-start.2 = (f32[31,8,128]{2,1,0:T(8,128)}, f32[31,8,128]{2,1,0:T(8,128)S(1)}, u32[]{:S(2)}, u32[]{:S(2)}) collective-permute-start(f32[31,8,128]{2,1,0:T(8,128)} %get-tuple-element.14), channel_id=1, source_target_pairs={{0,8},{8,16},{16,24},{1,9},{9,17},{17,25},{2,10},{10,18},{18,26},{... | collective-permute-start | bytes 380936 | tf_op jit(solution)/shard_map/ppermute | solution.py:369
  19.4 8.5 %collective-permute-start.3 = (f32[31,8,128]{2,1,0:T(8,128)}, f32[31,8,128]{2,1,0:T(8,128)S(1)}, u32[]{:S(2)}, u32[]{:S(2)}) collective-permute-start(f32[31,8,128]{2,1,0:T(8,128)} %get-tuple-element.15), channel_id=1, source_target_pairs={{8,0},{16,8},{24,16},{9,1},{17,9},{25,17},{10,2},{18,10},{26,18},{... | collective-permute-start | bytes 380936 | tf_op jit(solution)/shard_map/ppermute | solution.py:369
  26.3 1.6 %copy-start = (f32[31,8,128]{2,1,0:T(8,128)}, f32[31,8,128]{2,1,0:T(8,128)S(1)}, u32[]{:S(2)}) copy-start(f32[31,8,128]{2,1,0:T(8,128)S(1)} %collective-permute-done.2.y_lo) | copy-start | bytes 380932
  27.9 0.6 copy-start.1
  30.5 2.8 %collective-permute-start.4 = (f32[83,8,128]{2,1,0:T(8,128)}, f32[83,8,128]{2,1,0:T(8,128)S(1)}, u32[]{:S(2)}, u32[]{:S(2)}) collective-permute-start(f32[83,8,128]{2,1,0:T(8,128)} %get-tuple-element.16), channel_id=1, source_target_pairs={{0,32},{32,64},{64,96},{96,128},{128,160},{160,192},{192,224},{224... | collective-permute-start | bytes 1019912 | tf_op jit(solution)/shard_map/ppermute | solution.py:369
  31.8 4.9 %collective-permute-start.5 = (f32[83,8,128]{2,1,0:T(8,128)}, f32[83,8,128]{2,1,0:T(8,128)S(1)}, u32[]{:S(2)}, u32[]{:S(2)}) collective-permute-start(f32[83,8,128]{2,1,0:T(8,128)} %get-tuple-element.17), channel_id=1, source_target_pairs={{32,0},{64,32},{96,64},{128,96},{160,128},{192,160},{224,192},{256... | collective-permute-start | bytes 1019912 | tf_op jit(solution)/shard_map/ppermute | solution.py:369
  33.3 3.5 %copy-start.2 = (f32[83,8,128]{2,1,0:T(8,128)}, f32[83,8,128]{2,1,0:T(8,128)S(1)}, u32[]{:S(2)}) copy-start(f32[83,8,128]{2,1,0:T(8,128)S(1)} %collective-permute-done.4.x_lo) | copy-start | bytes 1019908
  36.7 0.7 copy-start.3

commit v2 on v1

--- a/solution.py
+++ b/solution.py
@@ -41,7 +41,7 @@
     return pl.BlockSpec(memory_space=pltpu.VMEM)
 
 
-def call(kernel, outs, args, scratch=(), smem=(), flops=100000):
+def call(kernel, outs, args, scratch=(), smem=(), flops=100000, limit=2):
     return pl.pallas_call(
         kernel,
         out_shape=[jax.ShapeDtypeStruct(s, F32) for s in outs],
@@ -51,6 +51,7 @@
         out_specs=[vmem() for _ in outs],
         scratch_shapes=list(scratch),
         cost_estimate=pl.CostEstimate(flops=flops, bytes_accessed=100000, transcendentals=0),
+        compiler_params=pltpu.CompilerParams(vmem_limit_bytes=limit * 2**20),
     )(*args)
 
 
@@ -62,7 +63,7 @@
             out = []
             tiles = [basis[i, x] for x in range(X)]
             for f in range(group):
-                w = schur[i, g * group + f]
+                w = schur[g * group + f, i]
                 for x in range(X):
                     out.append(acc[f * X + x] + w * tiles[x])
             return tuple(out)
@@ -319,7 +320,6 @@
     qg = jnp.where(row < KEEP, gram[:ROWS, :], 0.0)
     qg = jnp.where(row == KEEP, last_gram, qg)
     spread[3] = jnp.broadcast_to(inverse, TILE)
-    columns = []
     for k in range(EXPAND):
         up = jnp.where(
             (lane1 >= KEEP) & (lane1 < 60),
@@ -341,11 +341,10 @@
         last_gram = cleaned_gram * inverse
         q = jnp.where(row == KEEP + 1 + k, last, q)
         qg = jnp.where(row == KEEP + 1 + k, last_gram, qg)
-        columns.append(jnp.where(row == KEEP + 1 + k, length, c + e))
+        column_k = jnp.where(row == KEEP + 1 + k, length, c + e)
+        turned = jnp.sum(jnp.where(row == lane, column_k, 0.0), axis=0, keepdims=True)
+        hessenberg[k : k + 1, :] = turned[:, :ROWS]
         spread[pl.ds(4 + 8 * k, 8)] = jnp.broadcast_to(column(last), (SPAN, Z)).reshape(8, 8, Z)
-    hessenberg[...] = jnp.where(lane == 0, columns[0], jnp.where(lane == 1, columns[1], columns[2]))[
-        :, :EXPAND
-    ]
 
     for f in range(KEEP):
         basis[f] = span[f]
@@ -377,8 +376,9 @@
     fields, packed = call(
         rotate_kernel,
         [(FIELDS, X, Y, Z), (5, Y, Z)],
-        [krylov_basis, schur_vectors, next_vector, diag_shift, velocity],
+        [krylov_basis, schur_vectors.T, next_vector, diag_shift, velocity],
         smem=(1,),
+        limit=4,
     )
     z_lo, z_hi = send(packed, "gz", True), send(packed, "gz", False)
     up, down, halo = call(
@@ -404,6 +404,7 @@
             pltpu.VMEM((2, Y, Z), F32),
             pltpu.VMEM((len(region(3)), Y, Z), F32),
         ],
+        limit=8,
     )
     for i, stage in enumerate(stages):
         parts = exchange(parts, stage)
@@ -413,11 +414,12 @@
             )
     basis, hessenberg = call(
         functools.partial(finish_kernel, cell_count),
-        [(ROWS, X, Y, Z), (ROWS, EXPAND)],
+        [(ROWS, X, Y, Z), (EXPAND, ROWS)],
         [parts, span.reshape(SPAN, X, Y, Z)],
         scratch=[pltpu.VMEM((4 + 8 * EXPAND, Y, Z), F32)],
-    )
-    return basis, hessenberg
+        limit=4,
+    )
+    return basis, hessenberg.T
 
 
 def solution(mesh):

time: 106 us -> 92.9 us (0.88)
  Pallas kernels: 23 us -> 11.9 us
    pallas_call x7, Pallas kernels: 23 us -> 11.9 us  [call(): pl.pallas_call(kernel, out_shape=[jax.ShapeDtypeStruct(s, F32) for s in o...]
    pallas_call x1 -> x0, local copies, waits for them, and re-layouts: 1.36 us -> none  [call(): pl.pallas_call(kernel, out_shape=[jax.ShapeDtypeStruct(s, F32) for s in o...]
    unnamed x13 -> x10, local copies, waits for them, and re-layouts: 3.39 us -> 4.13 us
  transfers between devices with their start and end apart: 6 -> 6, of which waited for: 5 -> 4; matrix products, arithmetic and copies ran while one was open for 0% -> 0% of each run, Pallas kernels for 0% -> 0%
where the time goes in v2:
time: 92.9 us; the launch traced here: 92.3 us
  blocking collectives  50.6 us (54%)
  starting transfers between devices  17.5 us (19%)
  Pallas kernels  11.9 us (13%)
  waiting for transfers between devices  7.4 us (8%)
  local copies, waits for them, and re-layouts  4.13 us (4%)
    all_to_all x3, blocking collectives, exchange(): return lax.all_to_all(parts, axis, 0, 0)  50.6 us
    ppermute x6, starting transfers between devices, send(): return lax.ppermute(value, axis, up if forward else [(j, i) for i, j in up])  17.5 us
    pallas_call x7, Pallas kernels, call(): pl.pallas_call(kernel, out_shape=[jax.ShapeDtypeStruct(s, F32) for s in o...  11.9 us
    ppermute x6, waiting for transfers between devices, send(): return lax.ppermute(value, axis, up if forward else [(j, i) for i, j in up])  7.4 us
    unnamed x10, local copies, waits for them, and re-layouts  4.13 us
  transfers between devices with their start and end apart: 6, of which 4 were waited for; matrix products, arithmetic and copies ran while one was open for 0% of the time, Pallas kernels for 0%

profile of v2, /device:TPU:2, one launch (start us, length us, event | category | flops | bytes accessed | tf_op | source)
XLA Modules:
  0.0 92.3 jit_solution(15882197085678277348)
XLA Ops:
  0.6 0.0 copy-start
  0.6 1.2 %copy-done = f32[60,4,8,128]{3,2,1,0:T(8,128)S(1)} copy-done((f32[60,4,8,128]{3,2,1,0:T(8,128)S(1)}, f32[60,4,8,128]{3,2,1,0:T(8,128)}, u32[]{:S(2)}) %copy-start) | copy-done | bytes 983064
  1.8 0.0 copy-start.1
  1.8 0.8 copy-done.1
  2.6 0.0 copy-start.2
  2.6 0.7 copy-done.2
  3.4 0.0 copy-start.3
  3.4 0.7 copy-done.3
  4.1 0.0 copy-start.4
  4.1 0.7 copy-done.4
  4.8 2.9 %shard_map.68 = (f32[25,4,8,128]{3,2,1,0:T(8,128)S(1)}, f32[5,8,128]{2,1,0:T(8,128)S(1)}) custom-call(f32[60,4,8,128]{3,2,1,0:T(8,128)S(1)} %copy-done, f32[20,60]{1,0:T(8,128)S(1)} %bitcast.4, f32[4,8,128]{2,1,0:T(8,128)S(1)} %copy-done.2, f32[4,8,128]{2,1,0:T(8,128)S(1)} %copy-done.3, f32[3,4,8,128]{3,2,1,0:T(8,128)S(1)} %copy-done.1), custom_call_target="tpu_custom_call" | custom-call | flops 100000 | bytes 100000 | tf_op jit(solution)/shard_map/pallas_call | solution.py:45
  7.7 1.3 %collective-permute-start.1 = (f32[5,8,128]{2,1,0:T(8,128)S(1)}, f32[5,8,128]{2,1,0:T(8,128)S(1)}, u32[]{:S(2)}, u32[]{:S(2)}) collective-permute-start(f32[5,8,128]{2,1,0:T(8,128)S(1)} %get-tuple-element.14), channel_id=1, source_target_pairs={{1,0},{2,1},{3,2},{4,3},{5,4},{6,5},{7,6},{9,8},{10,9},{11,10},{12... | collective-permute-start | bytes 61448 | tf_op jit(solution)/shard_map/ppermute | solution.py:368
  9.0 4.5 %collective-permute-start = (f32[5,8,128]{2,1,0:T(8,128)S(1)}, f32[5,8,128]{2,1,0:T(8,128)S(1)}, u32[]{:S(2)}, u32[]{:S(2)}) collective-permute-start(f32[5,8,128]{2,1,0:T(8,128)S(1)} %get-tuple-element.14), channel_id=1, source_target_pairs={{0,1},{1,2},{2,3},{3,4},{4,5},{5,6},{6,7},{8,9},{9,10},{10,11},{11... | collective-permute-start | bytes 61448 | tf_op jit(solution)/shard_map/ppermute | solution.py:368
  13.5 0.0 collective-permute-done.1.from_hi
  13.5 1.5 %collective-permute-done.from_lo = f32[5,8,128]{2,1,0:T(8,128)S(1)} collective-permute-done((f32[5,8,128]{2,1,0:T(8,128)S(1)}, f32[5,8,128]{2,1,0:T(8,128)S(1)}, u32[]{:S(2)}, u32[]{:S(2)}) %collective-permute-start) | collective-permute-done | bytes 20512 | tf_op jit(solution)/shard_map/ppermute | solution.py:368
  15.0 0.1 shard_map.69
  15.1 3.4 %collective-permute-start.2 = (f32[31,8,128]{2,1,0:T(8,128)S(1)}, f32[31,8,128]{2,1,0:T(8,128)S(1)}, u32[]{:S(2)}, u32[]{:S(2)}) collective-permute-start(f32[31,8,128]{2,1,0:T(8,128)S(1)} %get-tuple-element.16), channel_id=1, source_target_pairs={{0,8},{8,16},{16,24},{1,9},{9,17},{17,25},{2,10},{10,18},{18,26},{... | collective-permute-start | bytes 380936 | tf_op jit(solution)/shard_map/ppermute | solution.py:368
  18.5 5.7 %collective-permute-start.3 = (f32[31,8,128]{2,1,0:T(8,128)S(1)}, f32[31,8,128]{2,1,0:T(8,128)S(1)}, u32[]{:S(2)}, u32[]{:S(2)}) collective-permute-start(f32[31,8,128]{2,1,0:T(8,128)S(1)} %get-tuple-element.17), channel_id=1, source_target_pairs={{8,0},{16,8},{24,16},{9,1},{17,9},{25,17},{10,2},{18,10},{26,18},{... | collective-permute-start | bytes 380936 | tf_op jit(solution)/shard_map/ppermute | solution.py:368
  24.2 1.0 %collective-permute-done.2.y_lo = f32[31,8,128]{2,1,0:T(8,128)S(1)} collective-permute-done((f32[31,8,128]{2,1,0:T(8,128)S(1)}, f32[31,8,128]{2,1,0:T(8,128)S(1)}, u32[]{:S(2)}, u32[]{:S(2)}) %collective-permute-start.2) | collective-permute-done | bytes 127008 | tf_op jit(solution)/shard_map/ppermute | solution.py:368
  25.1 1.5 %collective-permute-done.3.y_hi = f32[31,8,128]{2,1,0:T(8,128)S(1)} collective-permute-done((f32[31,8,128]{2,1,0:T(8,128)S(1)}, f32[31,8,128]{2,1,0:T(8,128)S(1)}, u32[]{:S(2)}, u32[]{:S(2)}) %collective-permute-start.3) | collective-permute-done | bytes 127008 | tf_op jit(solution)/shard_map/ppermute | solution.py:368
  26.7 1.3 %collective-permute-start.4 = (f32[83,8,128]{2,1,0:T(8,128)S(1)}, f32[83,8,128]{2,1,0:T(8,128)S(1)}, u32[]{:S(2)}, u32[]{:S(2)}) collective-permute-start(f32[83,8,128]{2,1,0:T(8,128)S(1)} %get-tuple-element.18), channel_id=1, source_target_pairs={{0,32},{32,64},{64,96},{96,128},{128,160},{160,192},{192,224},{224... | collective-permute-start | bytes 1019912 | tf_op jit(solution)/shard_map/ppermute | solution.py:368
  28.0 1.3 %collective-permute-start.5 = (f32[83,8,128]{2,1,0:T(8,128)S(1)}, f32[83,8,128]{2,1,0:T(8,128)S(1)}, u32[]{:S(2)}, u32[]{:S(2)}) collective-permute-start(f32[83,8,128]{2,1,0:T(8,128)S(1)} %get-tuple-element.19), channel_id=1, source_target_pairs={{32,0},{64,32},{96,64},{128,96},{160,128},{192,160},{224,192},{256... | collective-permute-start | bytes 1019912 | tf_op jit(solution)/shard_map/ppermute | solution.py:368
  29.3 0.0 collective-permute-done.4.x_lo
  29.3 3.5 %collective-permute-done.5.x_hi = f32[83,8,128]{2,1,0:T(8,128)S(1)} collective-permute-done((f32[83,8,128]{2,1,0:T(8,128)S(1)}, f32[83,8,128]{2,1,0:T(8,128)S(1)}, u32[]{:S(2)}, u32[]{:S(2)}) %collective-permute-start.5) | collective-permute-done | bytes 340000 | tf_op jit(solution)/shard_map/ppermute | solution.py:368
  32.8 6.3 %shard_map.71 = (f32[2048,128]{1,0:T(8,128)S(1)}, f32[8,32,128]{2,1,0:T(8,128)S(1)}) custom-call(f32[25,4,8,128]{3,2,1,0:T(8,128)S(1)} %get-tuple-element.13.fields, f32[5,8,128]{2,1,0:T(8,128)S(1)} %get-tuple-element.15.halo, f32[31,8,128]{2,1,0:T(8,128)S(1)} %collective-permute-done.2.y_lo, f32[31,8,128]{2,1,0:T(8,128)S(1)} %collective-permute-done.3.y_hi, ...), custom_call_target="tpu_custom_call" | custom-call | flops 100000 | bytes 100000 | tf_op jit(solution)/shard_map/pallas_call | solution.py:45
  39.1 13.9 %all_to_all.15.parts = f32[8,32,128]{2,1,0:T(8,128)S(1)} all-to-all(f32[8,32,128]{2,1,0:T(8,128)S(1)} %get-tuple-element.20), channel_id=1, replica_groups=mesh['gx_0'=8,'gx_1'=2,'gy'=4,'gz'=8] {'gx_1','gy'}, dimensions={0} | all-to-all | bytes 262144 | tf_op jit(solution)/shard_map/all_to_all | solution.py:290
  53.0 18.2 %all_to_all.16.parts = f32[8,32,128]{2,1,0:T(8,128)S(1)} all-to-all(f32[8,32,128]{2,1,0:T(8,128)S(1)} %shard_map.72), channel_id=1, replica_groups=mesh['gx_0'=8,'gx_1'=2,'gy'=4,'gz'=8] {'gz'}, dimensions={0} | all-to-all | bytes 262144 | tf_op jit(solution)/shard_map/all_to_all | solution.py:290
  71.2 18.6 %all_to_all.17.parts = f32[8,32,128]{2,1,0:T(8,128)S(1)} all-to-all(f32[8,32,128]{2,1,0:T(8,128)S(1)} %shard_map.73), channel_id=1, replica_groups=mesh['gx_0'=8,'gx_1'=2,'gy'=4,'gz'=8] {'gx_0'}, dimensions={0} | all-to-all | bytes 262144 | tf_op jit(solution)/shard_map/all_to_all | solution.py:290
  89.8 2.5 %shard_map.74 = (f32[24,4,8,128]{3,2,1,0:T(8,128)}, f32[3,24]{1,0:T(4,128)}) custom-call(f32[8,32,128]{2,1,0:T(8,128)S(1)} %all_to_all.17.parts, f32[64,4,8,128]{3,2,1,0:T(8,128)S(1)} %bitcast.3), custom_call_target="tpu_custom_call" | custom-call | flops 100000 | bytes 100000 | tf_op jit(solution)/shard_map/pallas_call | solution.py:45
  (3 shorter events, 0.1 us)
Async XLA Ops:
  0.6 1.2 %copy-start = (f32[60,4,8,128]{3,2,1,0:T(8,128)S(1)}, f32[60,4,8,128]{3,2,1,0:T(8,128)}, u32[]{:S(2)}) copy-start(f32[60,4,8,128]{3,2,1,0:T(8,128)} %basis.1) | copy-start | bytes 2949124
  1.8 0.8 copy-start.1
  2.6 0.7 copy-start.2
  3.4 0.7 copy-start.3
  4.1 0.7 copy-start.4
  7.7 5.9 %collective-permute-start.1 = (f32[5,8,128]{2,1,0:T(8,128)S(1)}, f32[5,8,128]{2,1,0:T(8,128)S(1)}, u32[]{:S(2)}, u32[]{:S(2)}) collective-permute-start(f32[5,8,128]{2,1,0:T(8,128)S(1)} %get-tuple-element.14), channel_id=1, source_target_pairs={{1,0},{2,1},{3,2},{4,3},{5,4},{6,5},{7,6},{9,8},{10,9},{11,10},{12... | collective-permute-start | bytes 61448 | tf_op jit(solution)/shard_map/ppermute | solution.py:368
  9.0 6.0 %collective-permute-start = (f32[5,8,128]{2,1,0:T(8,128)S(1)}, f32[5,8,128]{2,1,0:T(8,128)S(1)}, u32[]{:S(2)}, u32[]{:S(2)}) collective-permute-start(f32[5,8,128]{2,1,0:T(8,128)S(1)} %get-tuple-element.14), channel_id=1, source_target_pairs={{0,1},{1,2},{2,3},{3,4},{4,5},{5,6},{6,7},{8,9},{9,10},{10,11},{11... | collective-permute-start | bytes 61448 | tf_op jit(solution)/shard_map/ppermute | solution.py:368
  15.1 10.1 %collective-permute-start.2 = (f32[31,8,128]{2,1,0:T(8,128)S(1)}, f32[31,8,128]{2,1,0:T(8,128)S(1)}, u32[]{:S(2)}, u32[]{:S(2)}) collective-permute-start(f32[31,8,128]{2,1,0:T(8,128)S(1)} %get-tuple-element.16), channel_id=1, source_target_pairs={{0,8},{8,16},{16,24},{1,9},{9,17},{17,25},{2,10},{10,18},{18,26},{... | collective-permute-start | bytes 380936 | tf_op jit(solution)/shard_map/ppermute | solution.py:368
  18.5 8.2 %collective-permute-start.3 = (f32[31,8,128]{2,1,0:T(8,128)S(1)}, f32[31,8,128]{2,1,0:T(8,128)S(1)}, u32[]{:S(2)}, u32[]{:S(2)}) collective-permute-start(f32[31,8,128]{2,1,0:T(8,128)S(1)} %get-tuple-element.17), channel_id=1, source_target_pairs={{8,0},{16,8},{24,16},{9,1},{17,9},{25,17},{10,2},{18,10},{26,18},{... | collective-permute-start | bytes 380936 | tf_op jit(solution)/shard_map/ppermute | solution.py:368
  26.7 2.6 %collective-permute-start.4 = (f32[83,8,128]{2,1,0:T(8,128)S(1)}, f32[83,8,128]{2,1,0:T(8,128)S(1)}, u32[]{:S(2)}, u32[]{:S(2)}) collective-permute-start(f32[83,8,128]{2,1,0:T(8,128)S(1)} %get-tuple-element.18), channel_id=1, source_target_pairs={{0,32},{32,64},{64,96},{96,128},{128,160},{160,192},{192,224},{224... | collective-permute-start | bytes 1019912 | tf_op jit(solution)/shard_map/ppermute | solution.py:368
  28.0 4.8 %collective-permute-start.5 = (f32[83,8,128]{2,1,0:T(8,128)S(1)}, f32[83,8,128]{2,1,0:T(8,128)S(1)}, u32[]{:S(2)}, u32[]{:S(2)}) collective-permute-start(f32[83,8,128]{2,1,0:T(8,128)S(1)} %get-tuple-element.19), channel_id=1, source_target_pairs={{32,0},{64,32},{96,64},{128,96},{160,128},{192,160},{224,192},{256... | collective-permute-start | bytes 1019912 | tf_op jit(solution)/shard_map/ppermute | solution.py:368

commit v3 on v2

--- a/solution.py
+++ b/solution.py
@@ -123,16 +123,29 @@
         up[2 * f + 1] = fields[f, 3]
         down[2 * f] = fields[f, 0]
         down[2 * f + 1] = fields[f, 1]
-        lo, hi = y_lo[f], y_hi[f]
-        up[51 + f] = jnp.where(first, shift_rows(lo, 4), hi)
-        down[51 + f] = jnp.where(first, lo, shift_rows(hi, 4))
     up[50] = fields[20, 1]
     down[50] = fields[20, 2]
+    lo, hi = y_lo[20], y_hi[20]
+    up[51] = jnp.where(first, shift_rows(lo, 4), hi)
+    down[51] = jnp.where(first, lo, shift_rows(hi, 4))
+    row = rows_of()
+    for v in range(6):
+        a = jnp.zeros(TILE, F32)
+        b = a
+        for k in range(4):
+            f = 4 * v + k + (1 if v == 5 else 0)
+            lo, hi = y_lo[f], y_hi[f]
+            a = jnp.where(row == 2 * k, shift_rows(lo, 2 * k - 7), a)
+            a = jnp.where(row == 2 * k + 1, shift_rows(hi, 2 * k - 5), a)
+            b = jnp.where(row == 2 * k, shift_rows(lo, 2 * k - 1), b)
+            b = jnp.where(row == 2 * k + 1, shift_rows(hi, 2 * k + 1), b)
+        up[52 + v] = a
+        down[52 + v] = b
     for out in (up, down):
         for p in range(5):
-            out[76 + p] = halo[p]
-        out[81] = y_lo[30]
-        out[82] = y_hi[30]
+            out[58 + p] = halo[p]
+        out[63] = y_lo[30]
+        out[64] = y_hi[30]
 
 
 def region(radius):
@@ -167,7 +180,12 @@
                 tile = jnp.where(row == 2, shift_rows(y_hi[25], 2 - x), tile)
                 tile = jnp.where(row == 5, shift_rows(y_lo[25], 5 - x), tile)
             return tile
-        packed = (x_lo if x < 0 else x_hi)[51 + f]
+        side = x_lo if x < 0 else x_hi
+        if not (isinstance(f, int) and f == 20):
+            g = f - 1 if isinstance(f, int) and f > 20 else f
+            v, k = (g // 4, g % 4) if isinstance(g, int) else (lax.div(g, 4), lax.rem(g, 4))
+            return pltpu.roll(side[52 + v], 7 - 2 * k, 0)
+        packed = side[51]
         if x in (-1, 5):
             return jnp.where(first, shift_rows(packed, 2), shift_rows(packed, 4))
         return jnp.where(first, shift_rows(packed, 4), shift_rows(packed, 6))
@@ -175,7 +193,7 @@
     place = x if 0 <= x < X else (x + X if x < 0 else x - X)
     by = 128 - 3 - 6 * (4 * q + place)
     if a == 0:
-        packed = halo[p] if 0 <= x < X else (x_lo if x < 0 else x_hi)[76 + p]
+        packed = halo[p] if 0 <= x < X else (x_lo if x < 0 else x_hi)[58 + p]
     elif 0 <= x < X:
         packed = y_halo[p]
     else:
@@ -214,8 +232,8 @@
     first = rows_of() < 4
     for p in range(5):
         y_halo[p] = jnp.where(first, y_hi[26 + p], y_lo[26 + p])
-    x_corner[0] = jnp.where(first, x_lo[82], x_lo[81])
-    x_corner[1] = jnp.where(first, x_hi[82], x_hi[81])
+    x_corner[0] = jnp.where(first, x_lo[64], x_lo[63])
+    x_corner[1] = jnp.where(first, x_hi[64], x_hi[63])
     for at, key in enumerate(COEF):
         diagonal = tile_of(21, key, refs)
         inside = diagonal != 0.0
@@ -260,7 +278,7 @@
             store(f + 40, x, apply(once.__getitem__, (x, 0, 0), coef))
         return carry
 
-    lax.fori_loop(0, KEEP, body, 0)
+    lax.fori_loop(0, KEEP, body, 0, unroll=4)
 
     total = jnp.zeros((SPAN, SPAN), F32)
     for r in range(0, X * Y, 2):
@@ -275,7 +293,7 @@
         )
     packed = jnp.concatenate([total[:32], total[32:]], axis=1)
     for i in range(copies):
-        gram[i] = packed
+        gram[i] = packed[:16] if i < copies // 2 else packed[16:]
 
 
 def sum_kernel(copies, parts, out):
@@ -291,10 +309,7 @@
 
 
 def finish_kernel(cell_count, parts, span, basis, hessenberg, spread):
-    total = parts[0]
-    for i in range(1, parts.shape[0]):
-        total = total + parts[i]
-    total = total * (1.0 / cell_count)
+    total = jnp.concatenate([parts[0], parts[1]], axis=0) * (1.0 / cell_count)
     lane = lax.broadcasted_iota(jnp.int32, (32, Z), 1)
     gram = jnp.concatenate(
         [jnp.where(lane < SPAN, total, 0.0), jnp.where(lane < SPAN, pltpu.roll(total, 64, 1), 0.0)],
@@ -385,18 +400,13 @@
         pack_y_kernel, [(31, Y, Z), (31, Y, Z), (5, Y, Z)], [fields, z_lo, z_hi]
     )
     y_lo, y_hi = send(up, "gy", True), send(down, "gy", False)
-    up, down = call(pack_x_kernel, [(83, Y, Z), (83, Y, Z)], [fields, halo, y_lo, y_hi])
+    up, down = call(pack_x_kernel, [(65, Y, Z), (65, Y, Z)], [fields, halo, y_lo, y_hi])
     x_lo, x_hi = send(up, GX, True), send(down, GX, False)
-    stages = (("gx_1", "gy"), ("gz",), ("gx_0",))
-    sizes = []
-    for stage in stages:
-        size = 1
-        for axis in stage:
-            size *= lax.axis_size(axis)
-        sizes.append(size)
+    stages = (("gx_1", "gz"), ("gx_0", "gy"))
+    sizes = [lax.axis_size(stage) for stage in stages]
     span, parts = call(
         functools.partial(stencil_kernel, sizes[0]),
-        [(SPAN * X * Y, Z), (sizes[0], 32, Z)],
+        [(SPAN * X * Y, Z), (sizes[0], 16, Z)],
         [fields, halo, y_lo, y_hi, x_lo, x_hi],
         scratch=[
             pltpu.VMEM((len(COEF), 7, Y, Z), F32),
@@ -406,16 +416,15 @@
         ],
         limit=8,
     )
-    for i, stage in enumerate(stages):
-        parts = exchange(parts, stage)
-        if i + 1 < len(stages):
-            (parts,) = call(
-                functools.partial(sum_kernel, sizes[i + 1]), [(sizes[i + 1], 32, Z)], [parts]
-            )
+    parts = exchange(parts, stages[0])
+    (parts,) = call(functools.partial(sum_kernel, sizes[1]), [(sizes[1], 16, Z)], [parts])
+    parts = exchange(parts, stages[1])
+    (half,) = call(functools.partial(sum_kernel, 1), [(1, 16, Z)], [parts])
+    whole = lax.all_gather(half, "gx_1", axis=0, tiled=True)
     basis, hessenberg = call(
         functools.partial(finish_kernel, cell_count),
         [(ROWS, X, Y, Z), (EXPAND, ROWS)],
-        [parts, span.reshape(SPAN, X, Y, Z)],
+        [whole, span.reshape(SPAN, X, Y, Z)],
         scratch=[pltpu.VMEM((4 + 8 * EXPAND, Y, Z), F32)],
         limit=4,
     )

time: 92.9 us -> 88.8 us (0.956)
  the two profiles are of different devices: /device:TPU:2 before, /device:TPU:1 now
where the time goes in v3:
time: 88.8 us; the launch traced here: 88.2 us
  blocking collectives  43.5 us (49%)
  starting transfers between devices  20.2 us (23%)
  waiting for transfers between devices  10.4 us (12%)
  Pallas kernels  9.26 us (10%)
  local copies, waits for them, and re-layouts  4.13 us (5%)
    all_to_all x2, blocking collectives, exchange(): return lax.all_to_all(parts, axis, 0, 0)  38.8 us
    ppermute x6, starting transfers between devices, send(): return lax.ppermute(value, axis, up if forward else [(j, i) for i, j in up])  20.2 us
    ppermute x6, waiting for transfers between devices, send(): return lax.ppermute(value, axis, up if forward else [(j, i) for i, j in up])  10.4 us
    pallas_call x7, Pallas kernels, call(): pl.pallas_call(kernel, out_shape=[jax.ShapeDtypeStruct(s, F32) for s in o...  9.26 us
    all_gather x1, blocking collectives, per_device(): whole = lax.all_gather(half, 'gx_1', axis=0, tiled=True)  4.68 us
    unnamed x10, local copies, waits for them, and re-layouts  4.13 us
  transfers between devices with their start and end apart: 6, of which 5 were waited for; matrix products, arithmetic and copies ran while one was open for 0% of the time, Pallas kernels for 0%

profile of v3, /device:TPU:1, one launch (start us, length us, event | category | flops | bytes accessed | tf_op | source)
XLA Modules:
  0.0 88.2 jit_solution(9529679622259872366)
XLA Ops:
  0.6 0.0 copy-start
  0.6 1.2 %copy-done = f32[60,4,8,128]{3,2,1,0:T(8,128)S(1)} copy-done((f32[60,4,8,128]{3,2,1,0:T(8,128)S(1)}, f32[60,4,8,128]{3,2,1,0:T(8,128)}, u32[]{:S(2)}) %copy-start) | copy-done | bytes 983064
  1.8 0.0 copy-start.1
  1.8 0.8 copy-done.1
  2.6 0.0 copy-start.2
  2.6 0.7 copy-done.2
  3.4 0.0 copy-start.3
  3.4 0.7 copy-done.3
  4.1 0.0 copy-start.4
  4.1 0.7 copy-done.4
  4.8 2.9 %shard_map.68 = (f32[25,4,8,128]{3,2,1,0:T(8,128)S(1)}, f32[5,8,128]{2,1,0:T(8,128)S(1)}) custom-call(f32[60,4,8,128]{3,2,1,0:T(8,128)S(1)} %copy-done, f32[20,60]{1,0:T(8,128)S(1)} %bitcast.4, f32[4,8,128]{2,1,0:T(8,128)S(1)} %copy-done.2, f32[4,8,128]{2,1,0:T(8,128)S(1)} %copy-done.3, f32[3,4,8,128]{3,2,1,0:T(8,128)S(1)} %copy-done.1), custom_call_target="tpu_custom_call" | custom-call | flops 100000 | bytes 100000 | tf_op jit(solution)/shard_map/pallas_call | solution.py:45
  7.7 1.3 %collective-permute-start.1 = (f32[5,8,128]{2,1,0:T(8,128)S(1)}, f32[5,8,128]{2,1,0:T(8,128)S(1)}, u32[]{:S(2)}, u32[]{:S(2)}) collective-permute-start(f32[5,8,128]{2,1,0:T(8,128)S(1)} %get-tuple-element.14), channel_id=1, source_target_pairs={{1,0},{2,1},{3,2},{4,3},{5,4},{6,5},{7,6},{9,8},{10,9},{11,10},{12... | collective-permute-start | bytes 61448 | tf_op jit(solution)/shard_map/ppermute | solution.py:383
  9.0 4.6 %collective-permute-start = (f32[5,8,128]{2,1,0:T(8,128)S(1)}, f32[5,8,128]{2,1,0:T(8,128)S(1)}, u32[]{:S(2)}, u32[]{:S(2)}) collective-permute-start(f32[5,8,128]{2,1,0:T(8,128)S(1)} %get-tuple-element.14), channel_id=1, source_target_pairs={{0,1},{1,2},{2,3},{3,4},{4,5},{5,6},{6,7},{8,9},{9,10},{10,11},{11... | collective-permute-start | bytes 61448 | tf_op jit(solution)/shard_map/ppermute | solution.py:383
  13.6 0.0 collective-permute-done.1.from_hi
  13.6 0.9 collective-permute-done.from_lo
  14.5 0.1 shard_map.69
  14.6 3.3 %collective-permute-start.2 = (f32[31,8,128]{2,1,0:T(8,128)S(1)}, f32[31,8,128]{2,1,0:T(8,128)S(1)}, u32[]{:S(2)}, u32[]{:S(2)}) collective-permute-start(f32[31,8,128]{2,1,0:T(8,128)S(1)} %get-tuple-element.16), channel_id=1, source_target_pairs={{0,8},{8,16},{16,24},{1,9},{9,17},{17,25},{2,10},{10,18},{18,26},{... | collective-permute-start | bytes 380936 | tf_op jit(solution)/shard_map/ppermute | solution.py:383
  17.9 1.3 %collective-permute-start.3 = (f32[31,8,128]{2,1,0:T(8,128)S(1)}, f32[31,8,128]{2,1,0:T(8,128)S(1)}, u32[]{:S(2)}, u32[]{:S(2)}) collective-permute-start(f32[31,8,128]{2,1,0:T(8,128)S(1)} %get-tuple-element.17), channel_id=1, source_target_pairs={{8,0},{16,8},{24,16},{9,1},{17,9},{25,17},{10,2},{18,10},{26,18},{... | collective-permute-start | bytes 380936 | tf_op jit(solution)/shard_map/ppermute | solution.py:383
  19.2 0.6 collective-permute-done.2.y_lo
  19.8 3.8 %collective-permute-done.3.y_hi = f32[31,8,128]{2,1,0:T(8,128)S(1)} collective-permute-done((f32[31,8,128]{2,1,0:T(8,128)S(1)}, f32[31,8,128]{2,1,0:T(8,128)S(1)}, u32[]{:S(2)}, u32[]{:S(2)}) %collective-permute-start.3) | collective-permute-done | bytes 127008 | tf_op jit(solution)/shard_map/ppermute | solution.py:383
  23.5 0.1 shard_map.70
  23.6 7.1 %collective-permute-start.4 = (f32[65,8,128]{2,1,0:T(8,128)S(1)}, f32[65,8,128]{2,1,0:T(8,128)S(1)}, u32[]{:S(2)}, u32[]{:S(2)}) collective-permute-start(f32[65,8,128]{2,1,0:T(8,128)S(1)} %get-tuple-element.18), channel_id=1, source_target_pairs={{0,32},{32,64},{64,96},{96,128},{128,160},{160,192},{192,224},{224... | collective-permute-start | bytes 798728 | tf_op jit(solution)/shard_map/ppermute | solution.py:383
  30.7 2.6 %collective-permute-start.5 = (f32[65,8,128]{2,1,0:T(8,128)S(1)}, f32[65,8,128]{2,1,0:T(8,128)S(1)}, u32[]{:S(2)}, u32[]{:S(2)}) collective-permute-start(f32[65,8,128]{2,1,0:T(8,128)S(1)} %get-tuple-element.19), channel_id=1, source_target_pairs={{32,0},{64,32},{96,64},{128,96},{160,128},{192,160},{224,192},{256... | collective-permute-start | bytes 798728 | tf_op jit(solution)/shard_map/ppermute | solution.py:383
  33.3 0.8 collective-permute-done.4.x_lo
  34.1 4.4 %collective-permute-done.5.x_hi = f32[65,8,128]{2,1,0:T(8,128)S(1)} collective-permute-done((f32[65,8,128]{2,1,0:T(8,128)S(1)}, f32[65,8,128]{2,1,0:T(8,128)S(1)}, u32[]{:S(2)}, u32[]{:S(2)}) %collective-permute-start.5) | collective-permute-done | bytes 266272 | tf_op jit(solution)/shard_map/ppermute | solution.py:383
  38.5 3.7 %shard_map.71 = (f32[2048,128]{1,0:T(8,128)S(1)}, f32[16,16,128]{2,1,0:T(8,128)S(1)}) custom-call(f32[25,4,8,128]{3,2,1,0:T(8,128)S(1)} %get-tuple-element.13.fields, f32[5,8,128]{2,1,0:T(8,128)S(1)} %get-tuple-element.15.halo, f32[31,8,128]{2,1,0:T(8,128)S(1)} %collective-permute-done.2.y_lo, f32[31,8,128]{2,1,0:T(8,128)S(1)} %collective-permute-done.3.y_hi, ...), custom_call_target="tpu_custom_call" | custom-call | flops 100000 | bytes 100000 | tf_op jit(solution)/shard_map/pallas_call | solution.py:45
  42.1 16.3 %all_to_all.10.parts = f32[16,16,128]{2,1,0:T(8,128)S(1)} all-to-all(f32[16,16,128]{2,1,0:T(8,128)S(1)} %get-tuple-element.20), channel_id=1, replica_groups=mesh['gx_0'=8,'gx_1'=2,'gy'=4,'gz'=8] {'gx_1','gz'}, dimensions={0} | all-to-all | bytes 262144 | tf_op jit(solution)/shard_map/all_to_all | solution.py:308
  58.5 22.4 %all_to_all.11.parts = f32[32,16,128]{2,1,0:T(8,128)S(1)} all-to-all(f32[32,16,128]{2,1,0:T(8,128)S(1)} %shard_map.72), channel_id=1, replica_groups=mesh['gx_0'=8,'gx_1'=2,'gy'=4,'gz'=8] {'gx_0','gy'}, dimensions={0} | all-to-all | bytes 524288 | tf_op jit(solution)/shard_map/all_to_all | solution.py:308
  81.0 4.7 %all_gather.3.parts = f32[2,16,128]{2,1,0:T(8,128)S(1)} all-gather(f32[1,16,128]{2,1,0:T(8,128)S(1)} %shard_map.73), channel_id=1, replica_groups=mesh['gx_0'=8,'gx_1'=2,'gy'=4,'gz'=8] {'gx_1'}, dimensions={0}, use_global_device_ids=true | all-gather | bytes 24576 | tf_op jit(solution)/shard_map/all_gather | solution.py:423
  85.7 2.5 %shard_map.74 = (f32[24,4,8,128]{3,2,1,0:T(8,128)}, f32[3,24]{1,0:T(4,128)}) custom-call(f32[2,16,128]{2,1,0:T(8,128)S(1)} %all_gather.3.parts, f32[64,4,8,128]{3,2,1,0:T(8,128)S(1)} %bitcast.3), custom_call_target="tpu_custom_call" | custom-call | flops 100000 | bytes 100000 | tf_op jit(solution)/shard_map/pallas_call | solution.py:45
  (2 shorter events, 0.1 us)
Async XLA Ops:
  0.6 1.2 %copy-start = (f32[60,4,8,128]{3,2,1,0:T(8,128)S(1)}, f32[60,4,8,128]{3,2,1,0:T(8,128)}, u32[]{:S(2)}) copy-start(f32[60,4,8,128]{3,2,1,0:T(8,128)} %basis.1) | copy-start | bytes 2949124
  1.8 0.8 copy-start.1
  2.6 0.7 copy-start.2
  3.4 0.7 copy-start.3
  4.1 0.7 copy-start.4
  7.7 6.0 %collective-permute-start.1 = (f32[5,8,128]{2,1,0:T(8,128)S(1)}, f32[5,8,128]{2,1,0:T(8,128)S(1)}, u32[]{:S(2)}, u32[]{:S(2)}) collective-permute-start(f32[5,8,128]{2,1,0:T(8,128)S(1)} %get-tuple-element.14), channel_id=1, source_target_pairs={{1,0},{2,1},{3,2},{4,3},{5,4},{6,5},{7,6},{9,8},{10,9},{11,10},{12... | collective-permute-start | bytes 61448 | tf_op jit(solution)/shard_map/ppermute | solution.py:383
  9.0 5.5 %collective-permute-start = (f32[5,8,128]{2,1,0:T(8,128)S(1)}, f32[5,8,128]{2,1,0:T(8,128)S(1)}, u32[]{:S(2)}, u32[]{:S(2)}) collective-permute-start(f32[5,8,128]{2,1,0:T(8,128)S(1)} %get-tuple-element.14), channel_id=1, source_target_pairs={{0,1},{1,2},{2,3},{3,4},{4,5},{5,6},{6,7},{8,9},{9,10},{10,11},{11... | collective-permute-start | bytes 61448 | tf_op jit(solution)/shard_map/ppermute | solution.py:383
  14.6 5.2 %collective-permute-start.2 = (f32[31,8,128]{2,1,0:T(8,128)S(1)}, f32[31,8,128]{2,1,0:T(8,128)S(1)}, u32[]{:S(2)}, u32[]{:S(2)}) collective-permute-start(f32[31,8,128]{2,1,0:T(8,128)S(1)} %get-tuple-element.16), channel_id=1, source_target_pairs={{0,8},{8,16},{16,24},{1,9},{9,17},{17,25},{2,10},{10,18},{18,26},{... | collective-permute-start | bytes 380936 | tf_op jit(solution)/shard_map/ppermute | solution.py:383
  17.9 5.7 %collective-permute-start.3 = (f32[31,8,128]{2,1,0:T(8,128)S(1)}, f32[31,8,128]{2,1,0:T(8,128)S(1)}, u32[]{:S(2)}, u32[]{:S(2)}) collective-permute-start(f32[31,8,128]{2,1,0:T(8,128)S(1)} %get-tuple-element.17), channel_id=1, source_target_pairs={{8,0},{16,8},{24,16},{9,1},{17,9},{25,17},{10,2},{18,10},{26,18},{... | collective-permute-start | bytes 380936 | tf_op jit(solution)/shard_map/ppermute | solution.py:383
  23.6 10.5 %collective-permute-start.4 = (f32[65,8,128]{2,1,0:T(8,128)S(1)}, f32[65,8,128]{2,1,0:T(8,128)S(1)}, u32[]{:S(2)}, u32[]{:S(2)}) collective-permute-start(f32[65,8,128]{2,1,0:T(8,128)S(1)} %get-tuple-element.18), channel_id=1, source_target_pairs={{0,32},{32,64},{64,96},{96,128},{128,160},{160,192},{192,224},{224... | collective-permute-start | bytes 798728 | tf_op jit(solution)/shard_map/ppermute | solution.py:383
  30.7 7.7 %collective-permute-start.5 = (f32[65,8,128]{2,1,0:T(8,128)S(1)}, f32[65,8,128]{2,1,0:T(8,128)S(1)}, u32[]{:S(2)}, u32[]{:S(2)}) collective-permute-start(f32[65,8,128]{2,1,0:T(8,128)S(1)} %get-tuple-element.19), channel_id=1, source_target_pairs={{32,0},{64,32},{96,64},{128,96},{160,128},{192,160},{224,192},{256... | collective-permute-start | bytes 798728 | tf_op jit(solution)/shard_map/ppermute | solution.py:383

commit v4 on v3

--- a/solution.py
+++ b/solution.py
@@ -37,25 +37,75 @@
     return pltpu.roll(tile, by, 1)
 
 
-def vmem():
-    return pl.BlockSpec(memory_space=pltpu.VMEM)
-
-
-def call(kernel, outs, args, scratch=(), smem=(), flops=100000, limit=2):
+def place_of(kind):
+    return pl.BlockSpec(memory_space={"v": pltpu.VMEM, "s": pltpu.SMEM, "h": pltpu.HBM}[kind])
+
+
+def call(kernel, outs, args, scratch=(), ins="", out="", flops=100000, limit=2):
+    ins, out = ins or "v" * len(args), out or "v" * len(outs)
     return pl.pallas_call(
         kernel,
         out_shape=[jax.ShapeDtypeStruct(s, F32) for s in outs],
-        in_specs=[
-            pl.BlockSpec(memory_space=pltpu.SMEM) if i in smem else vmem() for i in range(len(args))
-        ],
-        out_specs=[vmem() for _ in outs],
+        in_specs=[place_of(k) for k in ins],
+        out_specs=[place_of(k) for k in out],
         scratch_shapes=list(scratch),
         cost_estimate=pl.CostEstimate(flops=flops, bytes_accessed=100000, transcendentals=0),
         compiler_params=pltpu.CompilerParams(vmem_limit_bytes=limit * 2**20),
     )(*args)
 
 
-def rotate_kernel(basis, schur, next_vector, diag, velocity, fields, packed):
+CHUNK = 10
+
+
+def edge_kernel(
+    basis, schur, next_vector, diag, velocity, held, rest, packed, weights, small, sems
+):
+    chunks = basis.shape[0] // CHUNK
+    copies = [
+        pltpu.make_async_copy(schur, weights, sems.at[0]),
+        *(
+            pltpu.make_async_copy(
+                basis.at[pl.ds(c * CHUNK, CHUNK)], held.at[pl.ds(c * CHUNK, CHUNK)], sems.at[1 + c]
+            )
+            for c in range(chunks)
+        ),
+        pltpu.make_async_copy(next_vector, rest.at[0], sems.at[1 + chunks]),
+        pltpu.make_async_copy(diag, small.at[0], sems.at[2 + chunks]),
+        pltpu.make_async_copy(velocity, small.at[pl.ds(1, 3)], sems.at[3 + chunks]),
+    ]
+    for copy in copies:
+        copy.start()
+    lane = lanes_of()
+    copies[0].wait()
+    acc = [jnp.zeros(TILE, F32) for _ in range(KEEP)]
+    for c in range(chunks):
+        copies[1 + c].wait()
+        for i in range(c * CHUNK, (c + 1) * CHUNK):
+            edge = jnp.zeros(TILE, F32)
+            for x in range(X):
+                here = (lane >= 6 * x) & (lane < 6 * x + 6)
+                edge = jnp.where(here, shift_lanes(held[i, x], 6 * x + 3), edge)
+            for f in range(KEEP):
+                acc[f] = acc[f] + weights[f, i] * edge
+    for p in range(4):
+        total = acc[5 * p]
+        for q in range(1, 5):
+            total = jnp.where(lane < 24 * q, total, shift_lanes(acc[5 * p + q], 24 * q))
+        packed[p] = total
+    for copy in copies[1 + chunks :]:
+        copy.wait()
+    for x in range(X):
+        rest[1, x] = 6.0 + small[0, x]
+        for d in range(3):
+            rest[2 + d, x] = 0.5 * small[1 + d, x]
+    total = jnp.zeros(TILE, F32)
+    for j in range(20):
+        moved = shift_lanes(rest[j // 4, j % 4], 6 * j + 3)
+        total = jnp.where((lane >= 6 * j) & (lane < 6 * j + 6), moved, total)
+    packed[4] = total
+
+
+def rotate_kernel(basis, schur, rotated):
     group = 5
     for g in range(KEEP // group):
 
@@ -72,23 +122,22 @@
         acc = lax.fori_loop(0, basis.shape[0], body, zero, unroll=4)
         for f in range(group):
             for x in range(X):
-                fields[g * group + f, x] = acc[f * X + x]
-    for x in range(X):
-        fields[20, x] = next_vector[x]
-        fields[21, x] = 6.0 + diag[x]
-        for d in range(3):
-            fields[22 + d, x] = 0.5 * velocity[d, x]
-    lane = lanes_of()
-    for p in range(5):
-        total = jnp.zeros(TILE, F32)
-        for j in range(20):
-            tile = fields[5 * p + j // 4, j % 4]
-            moved = shift_lanes(tile, 6 * j + 3)
-            total = jnp.where((lane >= 6 * j) & (lane < 6 * j + 6), moved, total)
-        packed[p] = total
-
-
-def pack_y_kernel(fields, from_lo, from_hi, up, down, halo):
+                rotated[g * group + f, x] = acc[f * X + x]
+
+
+class Fields:
+    def __init__(self, rotated, rest):
+        self.rotated, self.rest = rotated, rest
+
+    def __getitem__(self, at):
+        f, x = at
+        if isinstance(f, int) and f >= KEEP:
+            return self.rest[f - KEEP, x]
+        return self.rotated[f, x]
+
+
+def pack_y_kernel(rotated, rest, from_lo, from_hi, up, down, halo):
+    fields = Fields(rotated, rest)
     row, lane = rows_of(), lanes_of()
     left = lax.rem(lane, 6) < 3
     for f in range(FIELDS):
@@ -116,19 +165,21 @@
         down[26 + p] = merged
 
 
-def pack_x_kernel(fields, halo, y_lo, y_hi, up, down):
-    first = rows_of() < 4
+def pack_x_kernel(rotated, rest, halo, y_lo, y_hi, off, on):
+    fields = Fields(rotated, rest)
+    first, row = rows_of() < 4, rows_of()
+    upper = lax.axis_index("gx_1") == 1
+
+    def put(at, up, down):
+        off[at] = jnp.where(upper, up, down)
+        on[at] = jnp.where(upper, down, up)
+
     for f in range(FIELDS):
-        up[2 * f] = fields[f, 2]
-        up[2 * f + 1] = fields[f, 3]
-        down[2 * f] = fields[f, 0]
-        down[2 * f + 1] = fields[f, 1]
-    up[50] = fields[20, 1]
-    down[50] = fields[20, 2]
+        put(2 * f, fields[f, 2], fields[f, 0])
+        put(2 * f + 1, fields[f, 3], fields[f, 1])
+    put(50, fields[20, 1], fields[20, 2])
     lo, hi = y_lo[20], y_hi[20]
-    up[51] = jnp.where(first, shift_rows(lo, 4), hi)
-    down[51] = jnp.where(first, lo, shift_rows(hi, 4))
-    row = rows_of()
+    put(51, jnp.where(first, shift_rows(lo, 4), hi), jnp.where(first, lo, shift_rows(hi, 4)))
     for v in range(6):
         a = jnp.zeros(TILE, F32)
         b = a
@@ -139,9 +190,8 @@
             a = jnp.where(row == 2 * k + 1, shift_rows(hi, 2 * k - 5), a)
             b = jnp.where(row == 2 * k, shift_rows(lo, 2 * k - 1), b)
             b = jnp.where(row == 2 * k + 1, shift_rows(hi, 2 * k + 1), b)
-        up[52 + v] = a
-        down[52 + v] = b
-    for out in (up, down):
+        put(52 + v, a, b)
+    for out in (off, on):
         for p in range(5):
             out[58 + p] = halo[p]
         out[63] = y_lo[30]
@@ -226,8 +276,28 @@
 
 
 def stencil_kernel(
-    copies, fields, halo, y_lo, y_hi, x_lo, x_hi, span, gram, coef, y_halo, x_corner, chain
+    copies,
+    rotated,
+    rest,
+    halo,
+    y_lo,
+    y_hi,
+    off,
+    on,
+    span,
+    gram,
+    coef,
+    y_halo,
+    x_corner,
+    chain,
+    x_lo,
+    x_hi,
 ):
+    fields = Fields(rotated, rest)
+    upper = lax.axis_index("gx_1") == 1
+    for i in range(off.shape[0]):
+        x_lo[i] = jnp.where(upper, on[i], off[i])
+        x_hi[i] = jnp.where(upper, off[i], on[i])
     refs = (fields, halo, y_lo, y_hi, x_lo, x_hi, y_halo, x_corner)
     first = rows_of() < 4
     for p in range(5):
@@ -308,7 +378,11 @@
     return lax.all_to_all(parts, axis, 0, 0)
 
 
-def finish_kernel(cell_count, parts, span, basis, hessenberg, spread):
+def finish_kernel(cell_count, parts, span, basis, hessenberg, spread, fresh, sems):
+    early = pltpu.make_async_copy(
+        span.at[pl.ds(0, KEEP)], basis.at[pl.ds(0, KEEP)], sems.at[0]
+    )
+    early.start()
     total = jnp.concatenate([parts[0], parts[1]], axis=0) * (1.0 / cell_count)
     lane = lax.broadcasted_iota(jnp.int32, (32, Z), 1)
     gram = jnp.concatenate(
@@ -318,18 +392,22 @@
     row64 = lax.broadcasted_iota(jnp.int32, (SPAN, Z), 0)
     lane64 = lax.broadcasted_iota(jnp.int32, (SPAN, Z), 1)
     eye = row64 == lane64
+    moved = ((row64 >= KEEP) & (row64 < 60) & (lane64 == row64 - KEEP)) | (
+        (row64 > 60) & (lane64 == row64 - 1)
+    )
     row = lax.broadcasted_iota(jnp.int32, (ROWS, Z), 0)
     lane = lax.broadcasted_iota(jnp.int32, (ROWS, Z), 1)
     lane1 = lax.broadcasted_iota(jnp.int32, (1, Z), 1)
 
-    def column(vector):
-        return jnp.sum(jnp.where(eye, vector, 0.0), axis=1, keepdims=True)
+    def column(vector, picks):
+        return jnp.sum(jnp.where(picks, vector, 0.0), axis=1, keepdims=True)
 
     first_row = gram[60:61, :]
     norm_sq = jnp.sum(jnp.where(lane1 == 60, first_row, 0.0), axis=1, keepdims=True)
-    inverse = 1.0 / jnp.maximum(jnp.sqrt(norm_sq), 0.5)
+    inverse = lax.rsqrt(jnp.maximum(norm_sq, 0.25))
     last = jnp.where(lane1 == 60, inverse, 0.0)
     last_gram = first_row * inverse
+    up_column = jnp.where(lax.broadcasted_iota(jnp.int32, (SPAN, 1), 0) == 61, inverse, 0.0)
     q = jnp.where((row == lane) & (row < KEEP), 1.0, 0.0)
     q = jnp.where(row == KEEP, last, q)
     qg = jnp.where(row < KEEP, gram[:ROWS, :], 0.0)
@@ -342,7 +420,7 @@
             jnp.where((lane1 > 60) & (lane1 < SPAN), pltpu.roll(last, 1, 1), 0.0),
         )
         image = up + SIGMA * last
-        image_gram = jnp.sum(column(up) * gram, axis=0, keepdims=True) + SIGMA * last_gram
+        image_gram = jnp.sum(up_column * gram, axis=0, keepdims=True) + SIGMA * last_gram
         c = jnp.sum(q * image_gram, axis=1, keepdims=True)
         partly = image - jnp.sum(c * q, axis=0, keepdims=True)
         partly_gram = image_gram - jnp.sum(c * qg, axis=0, keepdims=True)
@@ -350,21 +428,21 @@
         cleaned = partly - jnp.sum(e * q, axis=0, keepdims=True)
         cleaned_gram = partly_gram - jnp.sum(e * qg, axis=0, keepdims=True)
         length_sq = jnp.sum(cleaned * cleaned_gram, axis=1, keepdims=True)
-        length = jnp.sqrt(jnp.maximum(length_sq, 0.0))
-        inverse = 1.0 / jnp.maximum(length, 0.5)
+        here, shifted = column(cleaned, eye), column(cleaned, moved)
+        inverse = lax.rsqrt(jnp.maximum(length_sq, 0.25))
         last = cleaned * inverse
         last_gram = cleaned_gram * inverse
+        up_column = shifted * inverse
         q = jnp.where(row == KEEP + 1 + k, last, q)
         qg = jnp.where(row == KEEP + 1 + k, last_gram, qg)
-        column_k = jnp.where(row == KEEP + 1 + k, length, c + e)
-        turned = jnp.sum(jnp.where(row == lane, column_k, 0.0), axis=0, keepdims=True)
+        length = jnp.sqrt(jnp.maximum(length_sq, 0.0))
+        entries = jnp.where(row == KEEP + 1 + k, length, c + e)
+        turned = jnp.sum(jnp.where(row == lane, entries, 0.0), axis=0, keepdims=True)
         hessenberg[k : k + 1, :] = turned[:, :ROWS]
-        spread[pl.ds(4 + 8 * k, 8)] = jnp.broadcast_to(column(last), (SPAN, Z)).reshape(8, 8, Z)
-
-    for f in range(KEEP):
-        basis[f] = span[f]
+        spread[pl.ds(4 + 8 * k, 8)] = jnp.broadcast_to(here * inverse, (SPAN, Z)).reshape(8, 8, Z)
+
     for x in range(X):
-        basis[KEEP, x] = span[60, x] * spread[3]
+        fresh[0, x] = span[60, x] * spread[3]
     acc = [[jnp.zeros(TILE, F32) for _ in range(X)] for _ in range(EXPAND)]
     for f in range(SPAN):
         tiles = [span[f, x] for x in range(X)]
@@ -374,7 +452,11 @@
                 acc[k][x] = acc[k][x] + w * tiles[x]
     for k in range(EXPAND):
         for x in range(X):
-            basis[KEEP + 1 + k, x] = acc[k][x]
+            fresh[1 + k, x] = acc[k][x]
+    late = pltpu.make_async_copy(fresh, basis.at[pl.ds(KEEP, ROWS - KEEP)], sems.at[1])
+    late.start()
+    early.wait()
+    late.wait()
 
 
 def send(value, axis, forward):
@@ -388,31 +470,54 @@
     cell_count = next_vector.size
     for axis in axes:
         cell_count *= lax.axis_size(axis)
-    fields, packed = call(
+    held, rest, packed = call(
+        edge_kernel,
+        [krylov_basis.shape, (FIELDS - KEEP, X, Y, Z), (5, Y, Z)],
+        [
+            pltpu.with_memory_space_constraint(value, pltpu.HBM)
+            for value in (krylov_basis, schur_vectors.T, next_vector, diag_shift, velocity)
+        ],
+        scratch=[
+            pltpu.SMEM((KEEP, krylov_basis.shape[0]), F32),
+            pltpu.VMEM((4, X, Y, Z), F32),
+            pltpu.SemaphoreType.DMA((4 + krylov_basis.shape[0] // CHUNK,)),
+        ],
+        ins="hhhhh",
+        limit=4,
+    )
+    z_lo, z_hi = send(packed, "gz", True), send(packed, "gz", False)
+    (rotated,) = call(
         rotate_kernel,
-        [(FIELDS, X, Y, Z), (5, Y, Z)],
-        [krylov_basis, schur_vectors.T, next_vector, diag_shift, velocity],
-        smem=(1,),
+        [(KEEP, X, Y, Z)],
+        [held, schur_vectors.T],
+        ins="vs",
         limit=4,
-    )
-    z_lo, z_hi = send(packed, "gz", True), send(packed, "gz", False)
+        flops=10**9,
+    )
     up, down, halo = call(
-        pack_y_kernel, [(31, Y, Z), (31, Y, Z), (5, Y, Z)], [fields, z_lo, z_hi]
+        pack_y_kernel, [(31, Y, Z), (31, Y, Z), (5, Y, Z)], [rotated, rest, z_lo, z_hi]
     )
     y_lo, y_hi = send(up, "gy", True), send(down, "gy", False)
-    up, down = call(pack_x_kernel, [(65, Y, Z), (65, Y, Z)], [fields, halo, y_lo, y_hi])
-    x_lo, x_hi = send(up, GX, True), send(down, GX, False)
+    off, on = call(
+        pack_x_kernel, [(65, Y, Z), (65, Y, Z)], [rotated, rest, halo, y_lo, y_hi]
+    )
+    count = lax.axis_size(GX)
+    swap = [(i, i + 1) for i in range(1, count - 1, 2)]
+    off = lax.ppermute(off, GX, swap + [(j, i) for i, j in swap])
+    on = lax.ppermute(on, "gx_1", [(0, 1), (1, 0)])
     stages = (("gx_1", "gz"), ("gx_0", "gy"))
     sizes = [lax.axis_size(stage) for stage in stages]
     span, parts = call(
         functools.partial(stencil_kernel, sizes[0]),
         [(SPAN * X * Y, Z), (sizes[0], 16, Z)],
-        [fields, halo, y_lo, y_hi, x_lo, x_hi],
+        [rotated, rest, halo, y_lo, y_hi, off, on],
         scratch=[
             pltpu.VMEM((len(COEF), 7, Y, Z), F32),
             pltpu.VMEM((5, Y, Z), F32),
             pltpu.VMEM((2, Y, Z), F32),
             pltpu.VMEM((len(region(3)), Y, Z), F32),
+            pltpu.VMEM((65, Y, Z), F32),
+            pltpu.VMEM((65, Y, Z), F32),
         ],
         limit=8,
     )
@@ -425,7 +530,12 @@
         functools.partial(finish_kernel, cell_count),
         [(ROWS, X, Y, Z), (EXPAND, ROWS)],
         [whole, span.reshape(SPAN, X, Y, Z)],
-        scratch=[pltpu.VMEM((4 + 8 * EXPAND, Y, Z), F32)],
+        scratch=[
+            pltpu.VMEM((4 + 8 * EXPAND, Y, Z), F32),
+            pltpu.VMEM((ROWS - KEEP, X, Y, Z), F32),
+            pltpu.SemaphoreType.DMA((2,)),
+        ],
+        out="hv",
         limit=4,
     )
     return basis, hessenberg.T

time: 88.8 us -> 81.4 us (0.917)
  local copies, waits for them, and re-layouts: 4.13 us -> 0.01 us
  waiting for transfers between devices: 10.4 us -> 6.51 us
  Pallas kernels: 9.26 us -> 11.1 us
  starting transfers between devices: 20.2 us -> 19 us
    ppermute x6 -> x4, starting transfers between devices: 20.2 us -> 10.5 us  [send(): return lax.ppermute(value, axis, up if forward else [(j, i) for i, j in up])]
    ppermute x0 -> x2, starting transfers between devices: none -> 8.49 us  [the longest x1 6.55 us: per_device(): off = lax.ppermute(off, GX, swap + [(j, i) for i, j in swap])]
    ppermute x6 -> x4, waiting for transfers between devices: 10.4 us -> 4.37 us  [send(): return lax.ppermute(value, axis, up if forward else [(j, i) for i, j in up])]
    unnamed x10 -> x2, local copies, waits for them, and re-layouts: 4.13 us -> 0.01 us
    ppermute x0 -> x2, waiting for transfers between devices: none -> 2.14 us  [the longest x1 2.14 us: per_device(): off = lax.ppermute(off, GX, swap + [(j, i) for i, j in swap])]
    pallas_call x7 -> x8, Pallas kernels: 9.26 us -> 11.1 us  [call(): pl.pallas_call(kernel, out_shape=[jax.ShapeDtypeStruct(s, F32) for s in o...]
  transfers between devices with their start and end apart: 6 -> 6, of which waited for: 5 -> 3; matrix products, arithmetic and copies ran while one was open for 0% -> 0% of each run, Pallas kernels for 0% -> 3%
where the time goes in v4:
time: 81.4 us; the launch traced here: 81 us
  blocking collectives  43.6 us (54%)
  starting transfers between devices  19 us (23%)
  Pallas kernels  11.1 us (14%)
  waiting for transfers between devices  6.51 us (8%)
    all_to_all x2, blocking collectives, exchange(): return lax.all_to_all(parts, axis, 0, 0)  38.9 us
    pallas_call x8, Pallas kernels, call(): pl.pallas_call(kernel, out_shape=[jax.ShapeDtypeStruct(s, F32) for s in o...  11.1 us
    ppermute x4, starting transfers between devices, send(): return lax.ppermute(value, axis, up if forward else [(j, i) for i, j in up])  10.5 us
    ppermute x1, starting transfers between devices, per_device(): off = lax.ppermute(off, GX, swap + [(j, i) for i, j in swap])  6.55 us
    all_gather x1, blocking collectives, per_device(): whole = lax.all_gather(half, 'gx_1', axis=0, tiled=True)  4.68 us
    ppermute x4, waiting for transfers between devices, send(): return lax.ppermute(value, axis, up if forward else [(j, i) for i, j in up])  4.37 us
    ppermute x1, waiting for transfers between devices, per_device(): off = lax.ppermute(off, GX, swap + [(j, i) for i, j in swap])  2.14 us
    ppermute x1, starting transfers between devices, per_device(): on = lax.ppermute(on, 'gx_1', [(0, 1), (1, 0)])  1.94 us
  transfers between devices with their start and end apart: 6, of which 3 were waited for; matrix products, arithmetic and copies ran while one was open for 0% of the time, Pallas kernels for 3%

profile of v4, /device:TPU:1, one launch (start us, length us, event | category | flops | bytes accessed | tf_op | source)
XLA Modules:
  0.0 81.0 jit_solution(16251823731326789230)
XLA Ops:
  0.6 0.0 copy-start
  0.6 2.1 %shard_map.68 = (f32[60,4,8,128]{3,2,1,0:T(8,128)S(1)}, f32[5,4,8,128]{3,2,1,0:T(8,128)S(1)}, f32[5,8,128]{2,1,0:T(8,128)S(1)}) custom-call(f32[60,4,8,128]{3,2,1,0:T(8,128)} %basis.1, f32[20,60]{1,0:T(8,128)} %bitcast.4, f32[4,8,128]{2,1,0:T(8,128)} %next_vector.1, f32[4,8,128]{2,1,0:T(8,128)} %diag.1, f32[3,4,8,128]{3,2,1,0:T(8,128)} %velocity.1), custom_call_target="tpu_custom_call" | custom-call | flops 100000 | bytes 100000 | tf_op jit(solution)/shard_map/pallas_call | solution.py:46
  2.7 1.3 %collective-permute-start.1 = (f32[5,8,128]{2,1,0:T(8,128)S(1)}, f32[5,8,128]{2,1,0:T(8,128)S(1)}, u32[]{:S(2)}, u32[]{:S(2)}) collective-permute-start(f32[5,8,128]{2,1,0:T(8,128)S(1)} %get-tuple-element.16), channel_id=1, source_target_pairs={{1,0},{2,1},{3,2},{4,3},{5,4},{6,5},{7,6},{9,8},{10,9},{11,10},{12... | collective-permute-start | bytes 61448 | tf_op jit(solution)/shard_map/ppermute | solution.py:465
  4.0 4.6 %collective-permute-start = (f32[5,8,128]{2,1,0:T(8,128)S(1)}, f32[5,8,128]{2,1,0:T(8,128)S(1)}, u32[]{:S(2)}, u32[]{:S(2)}) collective-permute-start(f32[5,8,128]{2,1,0:T(8,128)S(1)} %get-tuple-element.16), channel_id=1, source_target_pairs={{0,1},{1,2},{2,3},{3,4},{4,5},{5,6},{6,7},{8,9},{9,10},{10,11},{11... | collective-permute-start | bytes 61448 | tf_op jit(solution)/shard_map/ppermute | solution.py:465
  8.7 0.0 copy-done
  8.7 2.7 %shard_map.69.rotated = f32[20,4,8,128]{3,2,1,0:T(8,128)S(1)} custom-call(f32[60,4,8,128]{3,2,1,0:T(8,128)S(1)} %get-tuple-element.14.basis, f32[20,60]{1,0:T(8,128)S(1)} %bitcast.5), custom_call_target="tpu_custom_call" | custom-call | flops 1000000000 | bytes 100000 | tf_op jit(solution)/shard_map/pallas_call | solution.py:46
  11.4 0.0 collective-permute-done.1.from_hi
  11.4 0.0 collective-permute-done.from_lo
  11.4 0.1 shard_map.70
  11.5 3.3 %collective-permute-start.2 = (f32[31,8,128]{2,1,0:T(8,128)S(1)}, f32[31,8,128]{2,1,0:T(8,128)S(1)}, u32[]{:S(2)}, u32[]{:S(2)}) collective-permute-start(f32[31,8,128]{2,1,0:T(8,128)S(1)} %get-tuple-element.18), channel_id=1, source_target_pairs={{0,8},{8,16},{16,24},{1,9},{9,17},{17,25},{2,10},{10,18},{18,26},{... | collective-permute-start | bytes 380936 | tf_op jit(solution)/shard_map/ppermute | solution.py:465
  14.8 1.3 %collective-permute-start.3 = (f32[31,8,128]{2,1,0:T(8,128)S(1)}, f32[31,8,128]{2,1,0:T(8,128)S(1)}, u32[]{:S(2)}, u32[]{:S(2)}) collective-permute-start(f32[31,8,128]{2,1,0:T(8,128)S(1)} %get-tuple-element.19), channel_id=1, source_target_pairs={{8,0},{16,8},{24,16},{9,1},{17,9},{25,17},{10,2},{18,10},{26,18},{... | collective-permute-start | bytes 380936 | tf_op jit(solution)/shard_map/ppermute | solution.py:465
  16.1 0.6 collective-permute-done.2.y_lo
  16.7 3.8 %collective-permute-done.3.y_hi = f32[31,8,128]{2,1,0:T(8,128)S(1)} collective-permute-done((f32[31,8,128]{2,1,0:T(8,128)S(1)}, f32[31,8,128]{2,1,0:T(8,128)S(1)}, u32[]{:S(2)}, u32[]{:S(2)}) %collective-permute-start.3) | collective-permute-done | bytes 127008 | tf_op jit(solution)/shard_map/ppermute | solution.py:465
  20.5 0.1 shard_map.71
  20.5 6.6 %collective-permute-start.4 = (f32[65,8,128]{2,1,0:T(8,128)S(1)}, f32[65,8,128]{2,1,0:T(8,128)S(1)}, u32[]{:S(2)}, u32[]{:S(2)}) collective-permute-start(f32[65,8,128]{2,1,0:T(8,128)S(1)} %get-tuple-element.20), channel_id=1, source_target_pairs={{32,64},{96,128},{160,192},{224,256},{288,320},{352,384},{416,448}... | collective-permute-start | bytes 798728 | tf_op jit(solution)/shard_map/ppermute | solution.py:506
  27.1 1.9 %collective-permute-start.5 = (f32[65,8,128]{2,1,0:T(8,128)S(1)}, f32[65,8,128]{2,1,0:T(8,128)S(1)}, u32[]{:S(2)}, u32[]{:S(2)}) collective-permute-start(f32[65,8,128]{2,1,0:T(8,128)S(1)} %get-tuple-element.21), channel_id=1, source_target_pairs={{0,32},{32,0},{1,33},{33,1},{2,34},{34,2},{3,35},{35,3},{4,36},{36... | collective-permute-start | bytes 798728 | tf_op jit(solution)/shard_map/ppermute | solution.py:507
  29.0 2.1 %collective-permute-done.4.off = f32[65,8,128]{2,1,0:T(8,128)S(1)} collective-permute-done((f32[65,8,128]{2,1,0:T(8,128)S(1)}, f32[65,8,128]{2,1,0:T(8,128)S(1)}, u32[]{:S(2)}, u32[]{:S(2)}) %collective-permute-start.4) | collective-permute-done | bytes 266272 | tf_op jit(solution)/shard_map/ppermute | solution.py:506
  31.2 0.0 collective-permute-done.5.on
  31.2 3.7 %shard_map.72 = (f32[2048,128]{1,0:T(8,128)S(1)}, f32[16,16,128]{2,1,0:T(8,128)S(1)}) custom-call(f32[20,4,8,128]{3,2,1,0:T(8,128)S(1)} %shard_map.69.rotated, f32[5,4,8,128]{3,2,1,0:T(8,128)S(1)} %get-tuple-element.15.rest, f32[5,8,128]{2,1,0:T(8,128)S(1)} %get-tuple-element.17.halo, f32[31,8,128]{2,1,0:T(8,128)S(1)} %collective-permute-done.2.y_lo, ...), custom_call_target="tpu_custom_call" | custom-call | flops 100000 | bytes 100000 | tf_op jit(solution)/shard_map/pallas_call | solution.py:46
  34.9 15.0 %all_to_all.10.parts = f32[16,16,128]{2,1,0:T(8,128)S(1)} all-to-all(f32[16,16,128]{2,1,0:T(8,128)S(1)} %get-tuple-element.22), channel_id=1, replica_groups=mesh['gx_0'=8,'gx_1'=2,'gy'=4,'gz'=8] {'gx_1','gz'}, dimensions={0} | all-to-all | bytes 262144 | tf_op jit(solution)/shard_map/all_to_all | solution.py:378
  49.9 23.9 %all_to_all.11.parts = f32[32,16,128]{2,1,0:T(8,128)S(1)} all-to-all(f32[32,16,128]{2,1,0:T(8,128)S(1)} %shard_map.73), channel_id=1, replica_groups=mesh['gx_0'=8,'gx_1'=2,'gy'=4,'gz'=8] {'gx_0','gy'}, dimensions={0} | all-to-all | bytes 524288 | tf_op jit(solution)/shard_map/all_to_all | solution.py:378
  73.9 4.7 %all_gather.3.parts = f32[2,16,128]{2,1,0:T(8,128)S(1)} all-gather(f32[1,16,128]{2,1,0:T(8,128)S(1)} %shard_map.74), channel_id=1, replica_groups=mesh['gx_0'=8,'gx_1'=2,'gy'=4,'gz'=8] {'gx_1'}, dimensions={0}, use_global_device_ids=true | all-gather | bytes 24576 | tf_op jit(solution)/shard_map/all_gather | solution.py:528
  78.5 2.5 %shard_map.75 = (f32[24,4,8,128]{3,2,1,0:T(8,128)}, f32[3,24]{1,0:T(4,128)}) custom-call(f32[2,16,128]{2,1,0:T(8,128)S(1)} %all_gather.3.parts, f32[64,4,8,128]{3,2,1,0:T(8,128)S(1)} %bitcast.3), custom_call_target="tpu_custom_call" | custom-call | flops 100000 | bytes 100000 | tf_op jit(solution)/shard_map/pallas_call | solution.py:46
  (2 shorter events, 0.1 us)
Async XLA Ops:
  0.6 8.1 %copy-start = (f32[60,20]{0,1:T(8,128)S(1)}, f32[60,20]{0,1:T(8,128)}, u32[]{:S(2)}) copy-start(f32[60,20]{0,1:T(8,128)} %param.6) | copy-start | bytes 14404
  2.7 8.7 %collective-permute-start.1 = (f32[5,8,128]{2,1,0:T(8,128)S(1)}, f32[5,8,128]{2,1,0:T(8,128)S(1)}, u32[]{:S(2)}, u32[]{:S(2)}) collective-permute-start(f32[5,8,128]{2,1,0:T(8,128)S(1)} %get-tuple-element.16), channel_id=1, source_target_pairs={{1,0},{2,1},{3,2},{4,3},{5,4},{6,5},{7,6},{9,8},{10,9},{11,10},{12... | collective-permute-start | bytes 61448 | tf_op jit(solution)/shard_map/ppermute | solution.py:465
  4.0 7.4 %collective-permute-start = (f32[5,8,128]{2,1,0:T(8,128)S(1)}, f32[5,8,128]{2,1,0:T(8,128)S(1)}, u32[]{:S(2)}, u32[]{:S(2)}) collective-permute-start(f32[5,8,128]{2,1,0:T(8,128)S(1)} %get-tuple-element.16), channel_id=1, source_target_pairs={{0,1},{1,2},{2,3},{3,4},{4,5},{5,6},{6,7},{8,9},{9,10},{10,11},{11... | collective-permute-start | bytes 61448 | tf_op jit(solution)/shard_map/ppermute | solution.py:465
  11.5 5.2 %collective-permute-start.2 = (f32[31,8,128]{2,1,0:T(8,128)S(1)}, f32[31,8,128]{2,1,0:T(8,128)S(1)}, u32[]{:S(2)}, u32[]{:S(2)}) collective-permute-start(f32[31,8,128]{2,1,0:T(8,128)S(1)} %get-tuple-element.18), channel_id=1, source_target_pairs={{0,8},{8,16},{16,24},{1,9},{9,17},{17,25},{2,10},{10,18},{18,26},{... | collective-permute-start | bytes 380936 | tf_op jit(solution)/shard_map/ppermute | solution.py:465
  14.8 5.7 %collective-permute-start.3 = (f32[31,8,128]{2,1,0:T(8,128)S(1)}, f32[31,8,128]{2,1,0:T(8,128)S(1)}, u32[]{:S(2)}, u32[]{:S(2)}) collective-permute-start(f32[31,8,128]{2,1,0:T(8,128)S(1)} %get-tuple-element.19), channel_id=1, source_target_pairs={{8,0},{16,8},{24,16},{9,1},{17,9},{25,17},{10,2},{18,10},{26,18},{... | collective-permute-start | bytes 380936 | tf_op jit(solution)/shard_map/ppermute | solution.py:465
  20.5 10.6 %collective-permute-start.4 = (f32[65,8,128]{2,1,0:T(8,128)S(1)}, f32[65,8,128]{2,1,0:T(8,128)S(1)}, u32[]{:S(2)}, u32[]{:S(2)}) collective-permute-start(f32[65,8,128]{2,1,0:T(8,128)S(1)} %get-tuple-element.20), channel_id=1, source_target_pairs={{32,64},{96,128},{160,192},{224,256},{288,320},{352,384},{416,448}... | collective-permute-start | bytes 798728 | tf_op jit(solution)/shard_map/ppermute | solution.py:506
  27.1 4.1 %collective-permute-start.5 = (f32[65,8,128]{2,1,0:T(8,128)S(1)}, f32[65,8,128]{2,1,0:T(8,128)S(1)}, u32[]{:S(2)}, u32[]{:S(2)}) collective-permute-start(f32[65,8,128]{2,1,0:T(8,128)S(1)} %get-tuple-element.21), channel_id=1, source_target_pairs={{0,32},{32,0},{1,33},{33,1},{2,34},{34,2},{3,35},{35,3},{4,36},{36... | collective-permute-start | bytes 798728 | tf_op jit(solution)/shard_map/ppermute | solution.py:507

commit v5 on v4

--- a/solution.py
+++ b/solution.py
@@ -251,10 +251,9 @@
     return shift_lanes(packed, by)
 
 
-def apply(get, key, coef):
+def apply(get, key, coef, skip=()):
     x, a, b = key
     row, lane = rows_of(), lanes_of()
-    base = COEF.index(key)
     centre = get((x, a, b))
     y_other = get((x, 1 - a, b))
     z_other = get((x, a, 1 - b))
@@ -262,17 +261,59 @@
     y_behind = shift_rows(jnp.where(row == 7, y_other, centre), 1)
     z_ahead = shift_lanes(jnp.where(lane == 0, z_other, centre), 127)
     z_behind = shift_lanes(jnp.where(lane == 127, z_other, centre), 1)
-    near = (
-        centre,
-        get((x + 1, a, b)),
-        get((x - 1, a, b)),
-        y_ahead,
-        y_behind,
-        z_ahead,
-        z_behind,
-    )
-    terms = [coef[base, i] * near[i] for i in range(7)]
-    return (terms[0] + (terms[1] + terms[2])) + ((terms[3] + terms[4]) + (terms[5] + terms[6]))
+    total = coef(key, 3) * y_ahead + coef(key, 4) * y_behind
+    total = total + (coef(key, 5) * z_ahead + coef(key, 6) * z_behind)
+    total = total + coef(key, 0) * centre
+    for i, at in ((1, (x + 1, a, b)), (2, (x - 1, a, b))):
+        if i not in skip:
+            total = total + coef(key, i) * get(at)
+    return total
+
+
+def fill_coefficients(keys, out, refs):
+    for at, key in enumerate(keys):
+        diagonal = tile_of(21, key, refs)
+        inside = diagonal != 0.0
+        out[at, 0] = jnp.where(inside, diagonal - SIGMA, 0.0)
+        for d in range(3):
+            half = tile_of(22 + d, key, refs)
+            out[at, 1 + 2 * d] = jnp.where(inside, half - 1.0, 0.0)
+            out[at, 2 + 2 * d] = jnp.where(inside, -1.0 - half, 0.0)
+
+
+def cached(f, refs):
+    held = {}
+
+    def get(key):
+        if key not in held:
+            held[key] = tile_of(f, key, refs)
+        return held[key]
+
+    return get
+
+
+INNER = [key for key in COEF if 0 <= key[0] < X]
+OUTER = [key for key in COEF if not 0 <= key[0] < X]
+ONCE = [key for key in region(1) if 0 <= key[0] < X]
+SIDES = {0: (2, -1), X - 1: (1, X)}
+
+
+def inner_kernel(rotated, rest, halo, y_lo, y_hi, coef_in, partial, y_halo):
+    first = rows_of() < 4
+    for p in range(5):
+        y_halo[p] = jnp.where(first, y_hi[26 + p], y_lo[26 + p])
+    refs = (Fields(rotated, rest), halo, y_lo, y_hi, None, None, y_halo, None)
+    fill_coefficients(INNER, coef_in, refs)
+    coef = lambda key, i: coef_in[INNER.index(key), i]
+
+    def body(f, carry):
+        get = cached(f, refs)
+        for at, key in enumerate(ONCE):
+            skip = (SIDES[key[0]][0],) if key[0] in SIDES else ()
+            partial[f, at] = apply(get, key, coef, skip)
+        return carry
+
+    lax.fori_loop(0, KEEP, body, 0, unroll=4)
 
 
 def stencil_kernel(
@@ -282,11 +323,13 @@
     halo,
     y_lo,
     y_hi,
+    coef_in,
+    partial,
     off,
     on,
     span,
     gram,
-    coef,
+    coef_out,
     y_halo,
     x_corner,
     chain,
@@ -304,14 +347,12 @@
         y_halo[p] = jnp.where(first, y_hi[26 + p], y_lo[26 + p])
     x_corner[0] = jnp.where(first, x_lo[64], x_lo[63])
     x_corner[1] = jnp.where(first, x_hi[64], x_hi[63])
-    for at, key in enumerate(COEF):
-        diagonal = tile_of(21, key, refs)
-        inside = diagonal != 0.0
-        coef[at, 0] = jnp.where(inside, diagonal - SIGMA, 0.0)
-        for d in range(3):
-            half = tile_of(22 + d, key, refs)
-            coef[at, 1 + 2 * d] = jnp.where(inside, half - 1.0, 0.0)
-            coef[at, 2 + 2 * d] = jnp.where(inside, -1.0 - half, 0.0)
+    fill_coefficients(OUTER, coef_out, refs)
+
+    def coef(key, i):
+        if key in INNER:
+            return coef_in[INNER.index(key), i]
+        return coef_out[OUTER.index(key), i]
 
     def store(f, x, tile):
         at = f * (X * Y) + x * Y
@@ -333,14 +374,17 @@
             store(61 + step, x, tiles[(x, 0, 0)])
 
     def body(f, carry):
-        held = {}
-
-        def get(key):
-            if key not in held:
-                held[key] = tile_of(f, key, refs)
-            return held[key]
-
-        once = {key: apply(get, key, coef) for key in region(1)}
+        get = cached(f, refs)
+        once = {}
+        for at, key in enumerate(ONCE):
+            x, a, b = key
+            tile = partial[f, at]
+            if x in SIDES:
+                i, side = SIDES[x]
+                tile = tile + coef(key, i) * get((side, a, b))
+            once[key] = tile
+        for x in (-1, X):
+            once[(x, 0, 0)] = apply(get, (x, 0, 0), coef)
         for x in range(X):
             store(f, x, get((x, 0, 0)))
             store(f + 20, x, once[(x, 0, 0)])
@@ -383,6 +427,10 @@
         span.at[pl.ds(0, KEEP)], basis.at[pl.ds(0, KEEP)], sems.at[0]
     )
     early.start()
+    late = [
+        pltpu.make_async_copy(fresh.at[k], basis.at[KEEP + k], sems.at[1 + k])
+        for k in range(ROWS - KEEP)
+    ]
     total = jnp.concatenate([parts[0], parts[1]], axis=0) * (1.0 / cell_count)
     lane = lax.broadcasted_iota(jnp.int32, (32, Z), 1)
     gram = jnp.concatenate(
@@ -412,7 +460,10 @@
     q = jnp.where(row == KEEP, last, q)
     qg = jnp.where(row < KEEP, gram[:ROWS, :], 0.0)
     qg = jnp.where(row == KEEP, last_gram, qg)
-    spread[3] = jnp.broadcast_to(inverse, TILE)
+    scale = jnp.broadcast_to(inverse, TILE)
+    for x in range(X):
+        fresh[0, x] = span[60, x] * scale
+    late[0].start()
     for k in range(EXPAND):
         up = jnp.where(
             (lane1 >= KEEP) & (lane1 < 60),
@@ -439,24 +490,19 @@
         entries = jnp.where(row == KEEP + 1 + k, length, c + e)
         turned = jnp.sum(jnp.where(row == lane, entries, 0.0), axis=0, keepdims=True)
         hessenberg[k : k + 1, :] = turned[:, :ROWS]
-        spread[pl.ds(4 + 8 * k, 8)] = jnp.broadcast_to(here * inverse, (SPAN, Z)).reshape(8, 8, Z)
-
-    for x in range(X):
-        fresh[0, x] = span[60, x] * spread[3]
-    acc = [[jnp.zeros(TILE, F32) for _ in range(X)] for _ in range(EXPAND)]
-    for f in range(SPAN):
-        tiles = [span[f, x] for x in range(X)]
-        for k in range(EXPAND):
-            w = spread[4 + 8 * k + f // 8, f % 8 : f % 8 + 1, :]
+        spread[pl.ds(8 * k, 8)] = jnp.broadcast_to(here * inverse, (SPAN, Z)).reshape(8, 8, Z)
+        fields = [*range(KEEP * (k + 1)), *range(60, 62 + k)]
+        acc = [jnp.zeros(TILE, F32) for _ in range(X)]
+        for f in fields:
+            w = spread[8 * k + f // 8, f % 8 : f % 8 + 1, :]
             for x in range(X):
-                acc[k][x] = acc[k][x] + w * tiles[x]
-    for k in range(EXPAND):
+                acc[x] = acc[x] + w * span[f, x]
         for x in range(X):
-            fresh[1 + k, x] = acc[k][x]
-    late = pltpu.make_async_copy(fresh, basis.at[pl.ds(KEEP, ROWS - KEEP)], sems.at[1])
-    late.start()
+            fresh[1 + k, x] = acc[x]
+        late[1 + k].start()
     early.wait()
-    late.wait()
+    for copy in late:
+        copy.wait()
 
 
 def send(value, axis, forward):
@@ -507,12 +553,20 @@
     on = lax.ppermute(on, "gx_1", [(0, 1), (1, 0)])
     stages = (("gx_1", "gz"), ("gx_0", "gy"))
     sizes = [lax.axis_size(stage) for stage in stages]
+    coef_in, partial = call(
+        inner_kernel,
+        [(len(INNER), 7, Y, Z), (KEEP, len(ONCE), Y, Z)],
+        [rotated, rest, halo, y_lo, y_hi],
+        scratch=[pltpu.VMEM((5, Y, Z), F32)],
+        limit=6,
+        flops=10**9,
+    )
     span, parts = call(
         functools.partial(stencil_kernel, sizes[0]),
         [(SPAN * X * Y, Z), (sizes[0], 16, Z)],
-        [rotated, rest, halo, y_lo, y_hi, off, on],
+        [rotated, rest, halo, y_lo, y_hi, coef_in, partial, off, on],
         scratch=[
-            pltpu.VMEM((len(COEF), 7, Y, Z), F32),
+            pltpu.VMEM((len(OUTER), 7, Y, Z), F32),
             pltpu.VMEM((5, Y, Z), F32),
             pltpu.VMEM((2, Y, Z), F32),
             pltpu.VMEM((len(region(3)), Y, Z), F32),
@@ -531,9 +585,9 @@
         [(ROWS, X, Y, Z), (EXPAND, ROWS)],
         [whole, span.reshape(SPAN, X, Y, Z)],
         scratch=[
-            pltpu.VMEM((4 + 8 * EXPAND, Y, Z), F32),
+            pltpu.VMEM((8 * EXPAND, Y, Z), F32),
             pltpu.VMEM((ROWS - KEEP, X, Y, Z), F32),
-            pltpu.SemaphoreType.DMA((2,)),
+            pltpu.SemaphoreType.DMA((1 + ROWS - KEEP,)),
         ],
         out="hv",
         limit=4,

time: 81.4 us -> 80.4 us (0.988)
  waiting for transfers between devices: 6.51 us -> 4.74 us
    ppermute x1, waiting for transfers between devices: 2.14 us -> 0.37 us  [per_device(): off = lax.ppermute(off, GX, swap + [(j, i) for i, j in swap])]
    pallas_call x8 -> x9, Pallas kernels: 11.1 us -> 11.8 us  [call(): pl.pallas_call(kernel, out_shape=[jax.ShapeDtypeStruct(s, F32) for s in o...]
  transfers between devices with their start and end apart: 6 -> 6, of which waited for: 3 -> 3; matrix products, arithmetic and copies ran while one was open for 0% -> 0% of each run, Pallas kernels for 3% -> 6%
where the time goes in v5:
time: 80.4 us; the launch traced here: 79.9 us
  blocking collectives  43 us (53%)
  starting transfers between devices  19 us (24%)
  Pallas kernels  11.8 us (15%)
  waiting for transfers between devices  4.74 us (6%)
    all_to_all x2, blocking collectives, exchange(): return lax.all_to_all(parts, axis, 0, 0)  38.3 us
    pallas_call x9, Pallas kernels, call(): pl.pallas_call(kernel, out_shape=[jax.ShapeDtypeStruct(s, F32) for s in o...  11.8 us
    ppermute x4, starting transfers between devices, send(): return lax.ppermute(value, axis, up if forward else [(j, i) for i, j in up])  10.5 us
    ppermute x1, starting transfers between devices, per_device(): off = lax.ppermute(off, GX, swap + [(j, i) for i, j in swap])  6.55 us
    all_gather x1, blocking collectives, per_device(): whole = lax.all_gather(half, 'gx_1', axis=0, tiled=True)  4.68 us
    ppermute x4, waiting for transfers between devices, send(): return lax.ppermute(value, axis, up if forward else [(j, i) for i, j in up])  4.37 us
    ppermute x1, starting transfers between devices, per_device(): on = lax.ppermute(on, 'gx_1', [(0, 1), (1, 0)])  1.94 us
  transfers between devices with their start and end apart: 6, of which 3 were waited for; matrix products, arithmetic and copies ran while one was open for 0% of the time, Pallas kernels for 6%

profile of v5, /device:TPU:1, one launch (start us, length us, event | category | flops | bytes accessed | tf_op | source)
XLA Modules:
  0.0 79.9 jit_solution(12143155919336499407)
XLA Ops:
  0.6 2.0 %shard_map.68 = (f32[60,4,8,128]{3,2,1,0:T(8,128)S(1)}, f32[5,4,8,128]{3,2,1,0:T(8,128)S(1)}, f32[5,8,128]{2,1,0:T(8,128)S(1)}) custom-call(f32[60,4,8,128]{3,2,1,0:T(8,128)} %basis.1, f32[20,60]{1,0:T(8,128)} %bitcast.4, f32[4,8,128]{2,1,0:T(8,128)} %next_vector.1, f32[4,8,128]{2,1,0:T(8,128)} %diag.1, f32[3,4,8,128]{3,2,1,0:T(8,128)} %velocity.1), custom_call_target="tpu_custom_call" | custom-call | flops 100000 | bytes 100000 | tf_op jit(solution)/shard_map/pallas_call | solution.py:46
  2.7 1.3 %collective-permute-start.1 = (f32[5,8,128]{2,1,0:T(8,128)S(1)}, f32[5,8,128]{2,1,0:T(8,128)S(1)}, u32[]{:S(2)}, u32[]{:S(2)}) collective-permute-start(f32[5,8,128]{2,1,0:T(8,128)S(1)} %get-tuple-element.18), channel_id=1, source_target_pairs={{1,0},{2,1},{3,2},{4,3},{5,4},{6,5},{7,6},{9,8},{10,9},{11,10},{12... | collective-permute-start | bytes 61448 | tf_op jit(solution)/shard_map/ppermute | solution.py:511
  4.0 4.6 %collective-permute-start = (f32[5,8,128]{2,1,0:T(8,128)S(1)}, f32[5,8,128]{2,1,0:T(8,128)S(1)}, u32[]{:S(2)}, u32[]{:S(2)}) collective-permute-start(f32[5,8,128]{2,1,0:T(8,128)S(1)} %get-tuple-element.18), channel_id=1, source_target_pairs={{0,1},{1,2},{2,3},{3,4},{4,5},{5,6},{6,7},{8,9},{9,10},{10,11},{11... | collective-permute-start | bytes 61448 | tf_op jit(solution)/shard_map/ppermute | solution.py:511
  8.6 0.0 copy-start
  8.7 0.7 copy-done
  9.4 2.7 %shard_map.69.rotated = f32[20,4,8,128]{3,2,1,0:T(8,128)S(1)} custom-call(f32[60,4,8,128]{3,2,1,0:T(8,128)S(1)} %get-tuple-element.16.basis, f32[20,60]{1,0:T(8,128)S(1)} %bitcast.5), custom_call_target="tpu_custom_call" | custom-call | flops 1000000000 | bytes 100000 | tf_op jit(solution)/shard_map/pallas_call | solution.py:46
  12.1 0.0 collective-permute-done.1.from_hi
  12.1 0.0 collective-permute-done.from_lo
  12.1 0.1 shard_map.70
  12.2 3.3 %collective-permute-start.2 = (f32[31,8,128]{2,1,0:T(8,128)S(1)}, f32[31,8,128]{2,1,0:T(8,128)S(1)}, u32[]{:S(2)}, u32[]{:S(2)}) collective-permute-start(f32[31,8,128]{2,1,0:T(8,128)S(1)} %get-tuple-element.20), channel_id=1, source_target_pairs={{0,8},{8,16},{16,24},{1,9},{9,17},{17,25},{2,10},{10,18},{18,26},{... | collective-permute-start | bytes 380936 | tf_op jit(solution)/shard_map/ppermute | solution.py:511
  15.5 1.3 %collective-permute-start.3 = (f32[31,8,128]{2,1,0:T(8,128)S(1)}, f32[31,8,128]{2,1,0:T(8,128)S(1)}, u32[]{:S(2)}, u32[]{:S(2)}) collective-permute-start(f32[31,8,128]{2,1,0:T(8,128)S(1)} %get-tuple-element.21), channel_id=1, source_target_pairs={{8,0},{16,8},{24,16},{9,1},{17,9},{25,17},{10,2},{18,10},{26,18},{... | collective-permute-start | bytes 380936 | tf_op jit(solution)/shard_map/ppermute | solution.py:511
  16.8 0.6 collective-permute-done.2.y_lo
  17.3 3.8 %collective-permute-done.3.y_hi = f32[31,8,128]{2,1,0:T(8,128)S(1)} collective-permute-done((f32[31,8,128]{2,1,0:T(8,128)S(1)}, f32[31,8,128]{2,1,0:T(8,128)S(1)}, u32[]{:S(2)}, u32[]{:S(2)}) %collective-permute-start.3) | collective-permute-done | bytes 127008 | tf_op jit(solution)/shard_map/ppermute | solution.py:511
  21.1 0.1 shard_map.72
  21.2 6.6 %collective-permute-start.4 = (f32[65,8,128]{2,1,0:T(8,128)S(1)}, f32[65,8,128]{2,1,0:T(8,128)S(1)}, u32[]{:S(2)}, u32[]{:S(2)}) collective-permute-start(f32[65,8,128]{2,1,0:T(8,128)S(1)} %get-tuple-element.24), channel_id=1, source_target_pairs={{32,64},{96,128},{160,192},{224,256},{288,320},{352,384},{416,448}... | collective-permute-start | bytes 798728 | tf_op jit(solution)/shard_map/ppermute | solution.py:552
  27.7 1.9 %collective-permute-start.5 = (f32[65,8,128]{2,1,0:T(8,128)S(1)}, f32[65,8,128]{2,1,0:T(8,128)S(1)}, u32[]{:S(2)}, u32[]{:S(2)}) collective-permute-start(f32[65,8,128]{2,1,0:T(8,128)S(1)} %get-tuple-element.25), channel_id=1, source_target_pairs={{0,32},{32,0},{1,33},{33,1},{2,34},{34,2},{3,35},{35,3},{4,36},{36... | collective-permute-start | bytes 798728 | tf_op jit(solution)/shard_map/ppermute | solution.py:553
  29.7 1.8 %shard_map.71 = (f32[16,7,8,128]{3,2,1,0:T(8,128)S(1)}, f32[20,14,8,128]{3,2,1,0:T(8,128)S(1)}) custom-call(f32[20,4,8,128]{3,2,1,0:T(8,128)S(1)} %shard_map.69.rotated, f32[5,4,8,128]{3,2,1,0:T(8,128)S(1)} %get-tuple-element.17.rest, f32[5,8,128]{2,1,0:T(8,128)S(1)} %get-tuple-element.19.halo, f32[31,8,128]{2,1,0:T(8,128)S(1)} %collective-permute-done.2.y_lo, ...), custom_call_target="tpu_custom_call" | custom-call | flops 1000000000 | bytes 100000 | tf_op jit(solution)/shard_map/pallas_call | solution.py:46
  31.5 0.4 collective-permute-done.4.off
  31.8 0.0 collective-permute-done.5.on
  31.8 2.7 %shard_map.73 = (f32[2048,128]{1,0:T(8,128)S(1)}, f32[16,16,128]{2,1,0:T(8,128)S(1)}) custom-call(f32[20,4,8,128]{3,2,1,0:T(8,128)S(1)} %shard_map.69.rotated, f32[5,4,8,128]{3,2,1,0:T(8,128)S(1)} %get-tuple-element.17.rest, f32[5,8,128]{2,1,0:T(8,128)S(1)} %get-tuple-element.19.halo, f32[31,8,128]{2,1,0:T(8,128)S(1)} %collective-permute-done.2.y_lo, ...), custom_call_target="tpu_custom_call" | custom-call | flops 100000 | bytes 100000 | tf_op jit(solution)/shard_map/pallas_call | solution.py:46
  34.5 14.4 %all_to_all.10.parts = f32[16,16,128]{2,1,0:T(8,128)S(1)} all-to-all(f32[16,16,128]{2,1,0:T(8,128)S(1)} %get-tuple-element.26), channel_id=1, replica_groups=mesh['gx_0'=8,'gx_1'=2,'gy'=4,'gz'=8] {'gx_1','gz'}, dimensions={0} | all-to-all | bytes 262144 | tf_op jit(solution)/shard_map/all_to_all | solution.py:422
  49.0 23.9 %all_to_all.11.parts = f32[32,16,128]{2,1,0:T(8,128)S(1)} all-to-all(f32[32,16,128]{2,1,0:T(8,128)S(1)} %shard_map.74), channel_id=1, replica_groups=mesh['gx_0'=8,'gx_1'=2,'gy'=4,'gz'=8] {'gx_0','gy'}, dimensions={0} | all-to-all | bytes 524288 | tf_op jit(solution)/shard_map/all_to_all | solution.py:422
  72.9 4.7 %all_gather.3.parts = f32[2,16,128]{2,1,0:T(8,128)S(1)} all-gather(f32[1,16,128]{2,1,0:T(8,128)S(1)} %shard_map.75), channel_id=1, replica_groups=mesh['gx_0'=8,'gx_1'=2,'gy'=4,'gz'=8] {'gx_1'}, dimensions={0}, use_global_device_ids=true | all-gather | bytes 24576 | tf_op jit(solution)/shard_map/all_gather | solution.py:582
  77.5 2.4 %shard_map.76 = (f32[24,4,8,128]{3,2,1,0:T(8,128)}, f32[3,24]{1,0:T(4,128)}) custom-call(f32[2,16,128]{2,1,0:T(8,128)S(1)} %all_gather.3.parts, f32[64,4,8,128]{3,2,1,0:T(8,128)S(1)} %bitcast.3), custom_call_target="tpu_custom_call" | custom-call | flops 100000 | bytes 100000 | tf_op jit(solution)/shard_map/pallas_call | solution.py:46
  (2 shorter events, 0.1 us)
Async XLA Ops:
  2.7 9.4 %collective-permute-start.1 = (f32[5,8,128]{2,1,0:T(8,128)S(1)}, f32[5,8,128]{2,1,0:T(8,128)S(1)}, u32[]{:S(2)}, u32[]{:S(2)}) collective-permute-start(f32[5,8,128]{2,1,0:T(8,128)S(1)} %get-tuple-element.18), channel_id=1, source_target_pairs={{1,0},{2,1},{3,2},{4,3},{5,4},{6,5},{7,6},{9,8},{10,9},{11,10},{12... | collective-permute-start | bytes 61448 | tf_op jit(solution)/shard_map/ppermute | solution.py:511
  4.0 8.1 %collective-permute-start = (f32[5,8,128]{2,1,0:T(8,128)S(1)}, f32[5,8,128]{2,1,0:T(8,128)S(1)}, u32[]{:S(2)}, u32[]{:S(2)}) collective-permute-start(f32[5,8,128]{2,1,0:T(8,128)S(1)} %get-tuple-element.18), channel_id=1, source_target_pairs={{0,1},{1,2},{2,3},{3,4},{4,5},{5,6},{6,7},{8,9},{9,10},{10,11},{11... | collective-permute-start | bytes 61448 | tf_op jit(solution)/shard_map/ppermute | solution.py:511
  8.6 0.7 copy-start
  12.2 5.2 %collective-permute-start.2 = (f32[31,8,128]{2,1,0:T(8,128)S(1)}, f32[31,8,128]{2,1,0:T(8,128)S(1)}, u32[]{:S(2)}, u32[]{:S(2)}) collective-permute-start(f32[31,8,128]{2,1,0:T(8,128)S(1)} %get-tuple-element.20), channel_id=1, source_target_pairs={{0,8},{8,16},{16,24},{1,9},{9,17},{17,25},{2,10},{10,18},{18,26},{... | collective-permute-start | bytes 380936 | tf_op jit(solution)/shard_map/ppermute | solution.py:511
  15.5 5.7 %collective-permute-start.3 = (f32[31,8,128]{2,1,0:T(8,128)S(1)}, f32[31,8,128]{2,1,0:T(8,128)S(1)}, u32[]{:S(2)}, u32[]{:S(2)}) collective-permute-start(f32[31,8,128]{2,1,0:T(8,128)S(1)} %get-tuple-element.21), channel_id=1, source_target_pairs={{8,0},{16,8},{24,16},{9,1},{17,9},{25,17},{10,2},{18,10},{26,18},{... | collective-permute-start | bytes 380936 | tf_op jit(solution)/shard_map/ppermute | solution.py:511
  21.2 10.6 %collective-permute-start.4 = (f32[65,8,128]{2,1,0:T(8,128)S(1)}, f32[65,8,128]{2,1,0:T(8,128)S(1)}, u32[]{:S(2)}, u32[]{:S(2)}) collective-permute-start(f32[65,8,128]{2,1,0:T(8,128)S(1)} %get-tuple-element.24), channel_id=1, source_target_pairs={{32,64},{96,128},{160,192},{224,256},{288,320},{352,384},{416,448}... | collective-permute-start | bytes 798728 | tf_op jit(solution)/shard_map/ppermute | solution.py:552
  27.7 4.1 %collective-permute-start.5 = (f32[65,8,128]{2,1,0:T(8,128)S(1)}, f32[65,8,128]{2,1,0:T(8,128)S(1)}, u32[]{:S(2)}, u32[]{:S(2)}) collective-permute-start(f32[65,8,128]{2,1,0:T(8,128)S(1)} %get-tuple-element.25), channel_id=1, source_target_pairs={{0,32},{32,0},{1,33},{33,1},{2,34},{34,2},{3,35},{35,3},{4,36},{36... | collective-permute-start | bytes 798728 | tf_op jit(solution)/shard_map/ppermute | solution.py:553

commit v6 on v5

--- a/solution.py
+++ b/solution.py
@@ -14,6 +14,7 @@
 FIELDS = 25
 SPAN = 64
 SIGMA = 7.125
+WIRE = 1280
 GX = ("gx_0", "gx_1")
 X, Y, Z = (4, 8, 128)
 TILE = (Y, Z)
@@ -201,8 +202,9 @@
 def region(radius):
     out = []
     for a, b in ((0, 0), (1, 0), (0, 1), (1, 1)):
-        for x in range(-radius + a + b, X + radius - a - b):
-            out.append((x, a, b))
+        reach = radius - a - b
+        if reach >= 0:
+            out.extend((x, a, b) for x in range(-reach, X + reach))
     return out
 
 
@@ -405,9 +407,25 @@
             precision=lax.Precision.HIGHEST,
             preferred_element_type=F32,
         )
-    packed = jnp.concatenate([total[:32], total[32:]], axis=1)
+    wide = jnp.concatenate([total, jnp.zeros((SPAN, Z - SPAN), F32)], axis=1)
+    lane = lax.broadcasted_iota(jnp.int32, (16, Z), 1)
+    main = jnp.where(
+        lane < 64,
+        wide[:16],
+        jnp.where(lane < 112, pltpu.roll(wide[16:32], 48, 1), pltpu.roll(wide[48:], 64, 1)),
+    )
+    lane = lanes_of()
+    extra = jnp.zeros(TILE, F32)
+    for g in range(4):
+        tile = shift_rows(wide[32 + 8 * (g // 2) : 40 + 8 * (g // 2)], -4 * (g % 2))
+        tile = tile if g == 1 else shift_lanes(tile, (32 * g - 32) % Z)
+        extra = jnp.where((lane >= 32 * g) & (lane < 32 * g + 32), tile, extra)
     for i in range(copies):
-        gram[i] = packed[:16] if i < copies // 2 else packed[16:]
+        c = i // (copies // 2)
+        for k in range(8):
+            gram[i, :, Z * k : Z * (k + 1)] = main[8 * c + k : 8 * c + k + 1]
+        for k in range(2):
+            gram[i, :, Z * (8 + k) : Z * (9 + k)] = extra[2 * c + k : 2 * c + k + 1]
 
 
 def sum_kernel(copies, parts, out):
@@ -431,12 +449,38 @@
         pltpu.make_async_copy(fresh.at[k], basis.at[KEEP + k], sems.at[1 + k])
         for k in range(ROWS - KEEP)
     ]
-    total = jnp.concatenate([parts[0], parts[1]], axis=0) * (1.0 / cell_count)
-    lane = lax.broadcasted_iota(jnp.int32, (32, Z), 1)
-    gram = jnp.concatenate(
-        [jnp.where(lane < SPAN, total, 0.0), jnp.where(lane < SPAN, pltpu.roll(total, 64, 1), 0.0)],
+    row = lax.broadcasted_iota(jnp.int32, (16, Z), 0)
+    lane = lax.broadcasted_iota(jnp.int32, (16, Z), 1)
+    main = jnp.zeros((16, Z), F32)
+    extra = jnp.zeros(TILE, F32)
+    for c in range(2):
+        for k in range(8):
+            main = jnp.where(row == 8 * c + k, parts[c, :, Z * k : Z * (k + 1)], main)
+        for k in range(2):
+            here = rows_of() == 2 * c + k
+            extra = jnp.where(here, parts[c, :, Z * (8 + k) : Z * (9 + k)], extra)
+    main, extra = main * (1.0 / cell_count), extra * (1.0 / cell_count)
+    upper = []
+    for g in (0, 2):
+        tile = jnp.where(
+            rows_of() < 4,
+            shift_lanes(extra, (32 - 32 * g) % Z),
+            shift_lanes(shift_rows(extra, 4), -32 * g % Z) if g else shift_rows(extra, 4),
+        )
+        upper.append(jnp.where((lanes_of() >= 32) & (lanes_of() < SPAN), tile, 0.0))
+    blocks = jnp.concatenate(
+        [
+            jnp.where(lane < SPAN, main, 0.0),
+            jnp.where((lane >= 16) & (lane < SPAN), pltpu.roll(main, Z - 48, 1), 0.0),
+            *upper,
+            jnp.where((lane >= 48) & (lane < SPAN), pltpu.roll(main, 64, 1), 0.0),
+            jnp.zeros((Z - SPAN, Z), F32),
+        ],
         axis=0,
     )
+    across = lax.broadcasted_iota(jnp.int32, (Z, Z), 1) // 16
+    down = lax.broadcasted_iota(jnp.int32, (Z, Z), 0) // 16
+    gram = (blocks + jnp.where(across < down, blocks.T, 0.0))[:SPAN]
     row64 = lax.broadcasted_iota(jnp.int32, (SPAN, Z), 0)
     lane64 = lax.broadcasted_iota(jnp.int32, (SPAN, Z), 1)
     eye = row64 == lane64
@@ -563,7 +607,7 @@
     )
     span, parts = call(
         functools.partial(stencil_kernel, sizes[0]),
-        [(SPAN * X * Y, Z), (sizes[0], 16, Z)],
+        [(SPAN * X * Y, Z), (sizes[0], 1, WIRE)],
         [rotated, rest, halo, y_lo, y_hi, coef_in, partial, off, on],
         scratch=[
             pltpu.VMEM((len(OUTER), 7, Y, Z), F32),
@@ -576,9 +620,9 @@
         limit=8,
     )
     parts = exchange(parts, stages[0])
-    (parts,) = call(functools.partial(sum_kernel, sizes[1]), [(sizes[1], 16, Z)], [parts])
+    (parts,) = call(functools.partial(sum_kernel, sizes[1]), [(sizes[1], 1, WIRE)], [parts])
     parts = exchange(parts, stages[1])
-    (half,) = call(functools.partial(sum_kernel, 1), [(1, 16, Z)], [parts])
+    (half,) = call(functools.partial(sum_kernel, 1), [(1, 1, WIRE)], [parts])
     whole = lax.all_gather(half, "gx_1", axis=0, tiled=True)
     basis, hessenberg = call(
         functools.partial(finish_kernel, cell_count),

time: 80.4 us -> 78.5 us (0.976)
  blocking collectives: 43 us -> 41.7 us
  transfers between devices with their start and end apart: 6 -> 6, of which waited for: 3 -> 3; matrix products, arithmetic and copies ran while one was open for 0% -> 0% of each run, Pallas kernels for 6% -> 5%
where the time goes in v6:
time: 78.5 us; the launch traced here: 78.1 us
  blocking collectives  41.7 us (53%)
  starting transfers between devices  19 us (24%)
  Pallas kernels  11.5 us (15%)
  waiting for transfers between devices  5.15 us (7%)
    all_to_all x2, blocking collectives, exchange(): return lax.all_to_all(parts, axis, 0, 0)  37.8 us
    pallas_call x9, Pallas kernels, call(): pl.pallas_call(kernel, out_shape=[jax.ShapeDtypeStruct(s, F32) for s in o...  11.5 us
    ppermute x4, starting transfers between devices, send(): return lax.ppermute(value, axis, up if forward else [(j, i) for i, j in up])  10.5 us
    ppermute x1, starting transfers between devices, per_device(): off = lax.ppermute(off, GX, swap + [(j, i) for i, j in swap])  6.55 us
    ppermute x4, waiting for transfers between devices, send(): return lax.ppermute(value, axis, up if forward else [(j, i) for i, j in up])  4.37 us
    all_gather x1, blocking collectives, per_device(): whole = lax.all_gather(half, 'gx_1', axis=0, tiled=True)  3.9 us
    ppermute x1, starting transfers between devices, per_device(): on = lax.ppermute(on, 'gx_1', [(0, 1), (1, 0)])  1.94 us
  transfers between devices with their start and end apart: 6, of which 3 were waited for; matrix products, arithmetic and copies ran while one was open for 0% of the time, Pallas kernels for 5%

profile of v6, /device:TPU:1, one launch (start us, length us, event | category | flops | bytes accessed | tf_op | source)
XLA Modules:
  0.0 78.1 jit_solution(2440691294243711226)
XLA Ops:
  0.6 0.0 copy-start
  0.6 2.1 %shard_map.68 = (f32[60,4,8,128]{3,2,1,0:T(8,128)S(1)}, f32[5,4,8,128]{3,2,1,0:T(8,128)S(1)}, f32[5,8,128]{2,1,0:T(8,128)S(1)}) custom-call(f32[60,4,8,128]{3,2,1,0:T(8,128)} %basis.1, f32[20,60]{1,0:T(8,128)} %bitcast.4, f32[4,8,128]{2,1,0:T(8,128)} %next_vector.1, f32[4,8,128]{2,1,0:T(8,128)} %diag.1, f32[3,4,8,128]{3,2,1,0:T(8,128)} %velocity.1), custom_call_target="tpu_custom_call" | custom-call | flops 100000 | bytes 100000 | tf_op jit(solution)/shard_map/pallas_call | solution.py:47
  2.7 1.3 %collective-permute-start.1 = (f32[5,8,128]{2,1,0:T(8,128)S(1)}, f32[5,8,128]{2,1,0:T(8,128)S(1)}, u32[]{:S(2)}, u32[]{:S(2)}) collective-permute-start(f32[5,8,128]{2,1,0:T(8,128)S(1)} %get-tuple-element.18), channel_id=1, source_target_pairs={{1,0},{2,1},{3,2},{4,3},{5,4},{6,5},{7,6},{9,8},{10,9},{11,10},{12... | collective-permute-start | bytes 61448 | tf_op jit(solution)/shard_map/ppermute | solution.py:555
  4.0 4.6 %collective-permute-start = (f32[5,8,128]{2,1,0:T(8,128)S(1)}, f32[5,8,128]{2,1,0:T(8,128)S(1)}, u32[]{:S(2)}, u32[]{:S(2)}) collective-permute-start(f32[5,8,128]{2,1,0:T(8,128)S(1)} %get-tuple-element.18), channel_id=1, source_target_pairs={{0,1},{1,2},{2,3},{3,4},{4,5},{5,6},{6,7},{8,9},{9,10},{10,11},{11... | collective-permute-start | bytes 61448 | tf_op jit(solution)/shard_map/ppermute | solution.py:555
  8.7 0.0 copy-done
  8.7 2.7 %shard_map.69.rotated = f32[20,4,8,128]{3,2,1,0:T(8,128)S(1)} custom-call(f32[60,4,8,128]{3,2,1,0:T(8,128)S(1)} %get-tuple-element.16.basis, f32[20,60]{1,0:T(8,128)S(1)} %bitcast.5), custom_call_target="tpu_custom_call" | custom-call | flops 1000000000 | bytes 100000 | tf_op jit(solution)/shard_map/pallas_call | solution.py:47
  11.4 0.0 collective-permute-done.1.from_hi
  11.4 0.0 collective-permute-done.from_lo
  11.4 0.1 shard_map.70
  11.5 3.3 %collective-permute-start.2 = (f32[31,8,128]{2,1,0:T(8,128)S(1)}, f32[31,8,128]{2,1,0:T(8,128)S(1)}, u32[]{:S(2)}, u32[]{:S(2)}) collective-permute-start(f32[31,8,128]{2,1,0:T(8,128)S(1)} %get-tuple-element.20), channel_id=1, source_target_pairs={{0,8},{8,16},{16,24},{1,9},{9,17},{17,25},{2,10},{10,18},{18,26},{... | collective-permute-start | bytes 380936 | tf_op jit(solution)/shard_map/ppermute | solution.py:555
  14.8 1.3 %collective-permute-start.3 = (f32[31,8,128]{2,1,0:T(8,128)S(1)}, f32[31,8,128]{2,1,0:T(8,128)S(1)}, u32[]{:S(2)}, u32[]{:S(2)}) collective-permute-start(f32[31,8,128]{2,1,0:T(8,128)S(1)} %get-tuple-element.21), channel_id=1, source_target_pairs={{8,0},{16,8},{24,16},{9,1},{17,9},{25,17},{10,2},{18,10},{26,18},{... | collective-permute-start | bytes 380936 | tf_op jit(solution)/shard_map/ppermute | solution.py:555
  16.1 0.6 collective-permute-done.2.y_lo
  16.7 3.8 %collective-permute-done.3.y_hi = f32[31,8,128]{2,1,0:T(8,128)S(1)} collective-permute-done((f32[31,8,128]{2,1,0:T(8,128)S(1)}, f32[31,8,128]{2,1,0:T(8,128)S(1)}, u32[]{:S(2)}, u32[]{:S(2)}) %collective-permute-start.3) | collective-permute-done | bytes 127008 | tf_op jit(solution)/shard_map/ppermute | solution.py:555
  20.5 0.1 shard_map.72
  20.5 6.6 %collective-permute-start.4 = (f32[65,8,128]{2,1,0:T(8,128)S(1)}, f32[65,8,128]{2,1,0:T(8,128)S(1)}, u32[]{:S(2)}, u32[]{:S(2)}) collective-permute-start(f32[65,8,128]{2,1,0:T(8,128)S(1)} %get-tuple-element.24), channel_id=1, source_target_pairs={{32,64},{96,128},{160,192},{224,256},{288,320},{352,384},{416,448}... | collective-permute-start | bytes 798728 | tf_op jit(solution)/shard_map/ppermute | solution.py:596
  27.1 1.9 %collective-permute-start.5 = (f32[65,8,128]{2,1,0:T(8,128)S(1)}, f32[65,8,128]{2,1,0:T(8,128)S(1)}, u32[]{:S(2)}, u32[]{:S(2)}) collective-permute-start(f32[65,8,128]{2,1,0:T(8,128)S(1)} %get-tuple-element.25), channel_id=1, source_target_pairs={{0,32},{32,0},{1,33},{33,1},{2,34},{34,2},{3,35},{35,3},{4,36},{36... | collective-permute-start | bytes 798728 | tf_op jit(solution)/shard_map/ppermute | solution.py:597
  29.0 1.4 %shard_map.71 = (f32[16,7,8,128]{3,2,1,0:T(8,128)S(1)}, f32[20,12,8,128]{3,2,1,0:T(8,128)S(1)}) custom-call(f32[20,4,8,128]{3,2,1,0:T(8,128)S(1)} %shard_map.69.rotated, f32[5,4,8,128]{3,2,1,0:T(8,128)S(1)} %get-tuple-element.17.rest, f32[5,8,128]{2,1,0:T(8,128)S(1)} %get-tuple-element.19.halo, f32[31,8,128]{2,1,0:T(8,128)S(1)} %collective-permute-done.2.y_lo, ...), custom_call_target="tpu_custom_call" | custom-call | flops 1000000000 | bytes 100000 | tf_op jit(solution)/shard_map/pallas_call | solution.py:47
  30.4 0.8 collective-permute-done.4.off
  31.2 0.0 collective-permute-done.5.on
  31.2 2.7 %shard_map.73 = (f32[2048,128]{1,0:T(8,128)S(1)}, f32[16,1,1280]{2,1,0:T(1,128)S(1)}) custom-call(f32[20,4,8,128]{3,2,1,0:T(8,128)S(1)} %shard_map.69.rotated, f32[5,4,8,128]{3,2,1,0:T(8,128)S(1)} %get-tuple-element.17.rest, f32[5,8,128]{2,1,0:T(8,128)S(1)} %get-tuple-element.19.halo, f32[31,8,128]{2,1,0:T(8,128)S(1)} %collective-permute-done.2.y_lo, ...), custom_call_target="tpu_custom_call" | custom-call | flops 100000 | bytes 100000 | tf_op jit(solution)/shard_map/pallas_call | solution.py:47
  33.9 15.0 %all_to_all.10.parts = f32[16,1,1280]{2,1,0:T(1,128)S(1)} all-to-all(f32[16,1,1280]{2,1,0:T(1,128)S(1)} %get-tuple-element.26), channel_id=1, replica_groups=mesh['gx_0'=8,'gx_1'=2,'gy'=4,'gz'=8] {'gx_1','gz'}, dimensions={0} | all-to-all | bytes 163840 | tf_op jit(solution)/shard_map/all_to_all | solution.py:440
  48.9 22.8 %all_to_all.11.parts = f32[32,1,1280]{2,1,0:T(1,128)S(1)} all-to-all(f32[32,1,1280]{2,1,0:T(1,128)S(1)} %shard_map.74), channel_id=1, replica_groups=mesh['gx_0'=8,'gx_1'=2,'gy'=4,'gz'=8] {'gx_0','gy'}, dimensions={0} | all-to-all | bytes 327680 | tf_op jit(solution)/shard_map/all_to_all | solution.py:440
  71.8 3.9 %all_gather.3.parts = f32[2,1,1280]{2,1,0:T(1,128)S(1)} all-gather(f32[1,1,1280]{2,1,0:T(1,128)S(1)} %shard_map.75), channel_id=1, replica_groups=mesh['gx_0'=8,'gx_1'=2,'gy'=4,'gz'=8] {'gx_1'}, dimensions={0}, use_global_device_ids=true | all-gather | bytes 15360 | tf_op jit(solution)/shard_map/all_gather | solution.py:626
  75.7 2.5 %shard_map.76 = (f32[24,4,8,128]{3,2,1,0:T(8,128)}, f32[3,24]{1,0:T(4,128)}) custom-call(f32[2,1,1280]{2,1,0:T(1,128)S(1)} %all_gather.3.parts, f32[64,4,8,128]{3,2,1,0:T(8,128)S(1)} %bitcast.3), custom_call_target="tpu_custom_call" | custom-call | flops 100000 | bytes 100000 | tf_op jit(solution)/shard_map/pallas_call | solution.py:47
  (2 shorter events, 0.1 us)
Async XLA Ops:
  0.6 8.1 %copy-start = (f32[60,20]{0,1:T(8,128)S(1)}, f32[60,20]{0,1:T(8,128)}, u32[]{:S(2)}) copy-start(f32[60,20]{0,1:T(8,128)} %param.6) | copy-start | bytes 14404
  2.7 8.7 %collective-permute-start.1 = (f32[5,8,128]{2,1,0:T(8,128)S(1)}, f32[5,8,128]{2,1,0:T(8,128)S(1)}, u32[]{:S(2)}, u32[]{:S(2)}) collective-permute-start(f32[5,8,128]{2,1,0:T(8,128)S(1)} %get-tuple-element.18), channel_id=1, source_target_pairs={{1,0},{2,1},{3,2},{4,3},{5,4},{6,5},{7,6},{9,8},{10,9},{11,10},{12... | collective-permute-start | bytes 61448 | tf_op jit(solution)/shard_map/ppermute | solution.py:555
  4.0 7.4 %collective-permute-start = (f32[5,8,128]{2,1,0:T(8,128)S(1)}, f32[5,8,128]{2,1,0:T(8,128)S(1)}, u32[]{:S(2)}, u32[]{:S(2)}) collective-permute-start(f32[5,8,128]{2,1,0:T(8,128)S(1)} %get-tuple-element.18), channel_id=1, source_target_pairs={{0,1},{1,2},{2,3},{3,4},{4,5},{5,6},{6,7},{8,9},{9,10},{10,11},{11... | collective-permute-start | bytes 61448 | tf_op jit(solution)/shard_map/ppermute | solution.py:555
  11.5 5.2 %collective-permute-start.2 = (f32[31,8,128]{2,1,0:T(8,128)S(1)}, f32[31,8,128]{2,1,0:T(8,128)S(1)}, u32[]{:S(2)}, u32[]{:S(2)}) collective-permute-start(f32[31,8,128]{2,1,0:T(8,128)S(1)} %get-tuple-element.20), channel_id=1, source_target_pairs={{0,8},{8,16},{16,24},{1,9},{9,17},{17,25},{2,10},{10,18},{18,26},{... | collective-permute-start | bytes 380936 | tf_op jit(solution)/shard_map/ppermute | solution.py:555
  14.8 5.7 %collective-permute-start.3 = (f32[31,8,128]{2,1,0:T(8,128)S(1)}, f32[31,8,128]{2,1,0:T(8,128)S(1)}, u32[]{:S(2)}, u32[]{:S(2)}) collective-permute-start(f32[31,8,128]{2,1,0:T(8,128)S(1)} %get-tuple-element.21), channel_id=1, source_target_pairs={{8,0},{16,8},{24,16},{9,1},{17,9},{25,17},{10,2},{18,10},{26,18},{... | collective-permute-start | bytes 380936 | tf_op jit(solution)/shard_map/ppermute | solution.py:555
  20.5 10.6 %collective-permute-start.4 = (f32[65,8,128]{2,1,0:T(8,128)S(1)}, f32[65,8,128]{2,1,0:T(8,128)S(1)}, u32[]{:S(2)}, u32[]{:S(2)}) collective-permute-start(f32[65,8,128]{2,1,0:T(8,128)S(1)} %get-tuple-element.24), channel_id=1, source_target_pairs={{32,64},{96,128},{160,192},{224,256},{288,320},{352,384},{416,448}... | collective-permute-start | bytes 798728 | tf_op jit(solution)/shard_map/ppermute | solution.py:596
  27.1 4.1 %collective-permute-start.5 = (f32[65,8,128]{2,1,0:T(8,128)S(1)}, f32[65,8,128]{2,1,0:T(8,128)S(1)}, u32[]{:S(2)}, u32[]{:S(2)}) collective-permute-start(f32[65,8,128]{2,1,0:T(8,128)S(1)} %get-tuple-element.25), channel_id=1, source_target_pairs={{0,32},{32,0},{1,33},{33,1},{2,34},{34,2},{3,35},{35,3},{4,36},{36... | collective-permute-start | bytes 798728 | tf_op jit(solution)/shard_map/ppermute | solution.py:597

commit v7 on v6

--- a/solution.py
+++ b/solution.py
@@ -159,11 +159,26 @@
         b = jnp.where(row == x, shift_rows(tile, x - 2), b)
     up[25] = a
     down[25] = b
+    a = jnp.zeros(TILE, F32)
+    b = a
     for p in range(5):
         merged = jnp.where(left, from_lo[p], from_hi[p])
         halo[p] = merged
-        up[26 + p] = merged
-        down[26 + p] = merged
+        a = jnp.where(row == p, shift_rows(merged, p - 7), a)
+        b = jnp.where(row == p, shift_rows(merged, p), b)
+    up[26] = jnp.where(row == 5, shift_rows(merged, -1), a)
+    down[26] = jnp.where(row == 5, shift_rows(merged, 4), b)
+
+
+def corner_of(p, y_lo, y_hi):
+    row = rows_of()
+    lo, hi = y_lo[26], y_hi[26]
+    tile = jnp.where(row == 0, shift_rows(hi, -p), jnp.zeros(TILE, F32))
+    tile = jnp.where(row == 7, shift_rows(lo, 7 - p), tile)
+    if p == 4:
+        tile = jnp.where(row == 1, shift_rows(hi, -4), tile)
+        tile = jnp.where(row == 6, shift_rows(lo, 1), tile)
+    return tile
 
 
 def pack_x_kernel(rotated, rest, halo, y_lo, y_hi, off, on):
@@ -192,11 +207,19 @@
             b = jnp.where(row == 2 * k, shift_rows(lo, 2 * k - 1), b)
             b = jnp.where(row == 2 * k + 1, shift_rows(hi, 2 * k + 1), b)
         put(52 + v, a, b)
-    for out in (off, on):
-        for p in range(5):
-            out[58 + p] = halo[p]
-        out[63] = y_lo[30]
-        out[64] = y_hi[30]
+    part = lax.rem(lanes_of(), 24)
+    a = jnp.zeros(TILE, F32)
+    b = a
+    for p in range(4):
+        tile = halo[p]
+        here = (part >= 18 - 6 * p) & (part < 24 - 6 * p)
+        a = jnp.where(here, shift_lanes(tile, -6 * p % Z) if p else tile, a)
+        here = (part >= 6 * p) & (part < 6 * p + 6)
+        b = jnp.where(here, shift_lanes(tile, 6 * p) if p else tile, b)
+    put(58, a, b)
+    corner = corner_of(4, y_lo, y_hi)
+    put(59, halo[4], halo[4])
+    put(60, corner, corner)
 
 
 def region(radius):
@@ -244,8 +267,11 @@
     p, q = (f // 5, f % 5) if isinstance(f, int) else (lax.div(f, 5), lax.rem(f, 5))
     place = x if 0 <= x < X else (x + X if x < 0 else x - X)
     by = 128 - 3 - 6 * (4 * q + place)
-    if a == 0:
-        packed = halo[p] if 0 <= x < X else (x_lo if x < 0 else x_hi)[58 + p]
+    if a == 0 and not 0 <= x < X and not (isinstance(f, int) and f >= KEEP):
+        packed = (x_lo if x < 0 else x_hi)[58]
+        by = 128 - 3 - 24 * q - (18 - 6 * p if x < 0 else 6 * p)
+    elif a == 0:
+        packed = halo[p] if 0 <= x < X else (x_lo if x < 0 else x_hi)[59]
     elif 0 <= x < X:
         packed = y_halo[p]
     else:
@@ -301,18 +327,21 @@
 
 
 def inner_kernel(rotated, rest, halo, y_lo, y_hi, coef_in, partial, y_halo):
-    first = rows_of() < 4
     for p in range(5):
-        y_halo[p] = jnp.where(first, y_hi[26 + p], y_lo[26 + p])
+        y_halo[p] = corner_of(p, y_lo, y_hi)
     refs = (Fields(rotated, rest), halo, y_lo, y_hi, None, None, y_halo, None)
     fill_coefficients(INNER, coef_in, refs)
     coef = lambda key, i: coef_in[INNER.index(key), i]
 
     def body(f, carry):
         get = cached(f, refs)
+        once = {}
         for at, key in enumerate(ONCE):
             skip = (SIDES[key[0]][0],) if key[0] in SIDES else ()
-            partial[f, at] = apply(get, key, coef, skip)
+            once[key] = apply(get, key, coef, skip)
+            partial[f, at] = once[key]
+        for x, skip in ((1, (2,)), (2, (1,))):
+            partial[f, len(ONCE) + x - 1] = apply(once.__getitem__, (x, 0, 0), coef, skip)
         return carry
 
     lax.fori_loop(0, KEEP, body, 0, unroll=4)
@@ -344,11 +373,10 @@
         x_lo[i] = jnp.where(upper, on[i], off[i])
         x_hi[i] = jnp.where(upper, off[i], on[i])
     refs = (fields, halo, y_lo, y_hi, x_lo, x_hi, y_halo, x_corner)
-    first = rows_of() < 4
     for p in range(5):
-        y_halo[p] = jnp.where(first, y_hi[26 + p], y_lo[26 + p])
-    x_corner[0] = jnp.where(first, x_lo[64], x_lo[63])
-    x_corner[1] = jnp.where(first, x_hi[64], x_hi[63])
+        y_halo[p] = corner_of(p, y_lo, y_hi)
+    x_corner[0] = x_lo[60]
+    x_corner[1] = x_hi[60]
     fill_coefficients(OUTER, coef_out, refs)
 
     def coef(key, i):
@@ -380,6 +408,8 @@
         once = {}
         for at, key in enumerate(ONCE):
             x, a, b = key
+            if x not in SIDES and (a or b):
+                continue
             tile = partial[f, at]
             if x in SIDES:
                 i, side = SIDES[x]
@@ -390,8 +420,11 @@
         for x in range(X):
             store(f, x, get((x, 0, 0)))
             store(f + 20, x, once[(x, 0, 0)])
-        for x in range(X):
+        for x in SIDES:
             store(f + 40, x, apply(once.__getitem__, (x, 0, 0), coef))
+        for x, i, near in ((1, 2, 0), (2, 1, 3)):
+            term = coef((x, 0, 0), i) * once[(near, 0, 0)]
+            store(f + 40, x, partial[f, len(ONCE) + x - 1] + term)
         return carry
 
     lax.fori_loop(0, KEEP, body, 0, unroll=4)
@@ -585,11 +618,11 @@
         flops=10**9,
     )
     up, down, halo = call(
-        pack_y_kernel, [(31, Y, Z), (31, Y, Z), (5, Y, Z)], [rotated, rest, z_lo, z_hi]
+        pack_y_kernel, [(27, Y, Z), (27, Y, Z), (5, Y, Z)], [rotated, rest, z_lo, z_hi]
     )
     y_lo, y_hi = send(up, "gy", True), send(down, "gy", False)
     off, on = call(
-        pack_x_kernel, [(65, Y, Z), (65, Y, Z)], [rotated, rest, halo, y_lo, y_hi]
+        pack_x_kernel, [(61, Y, Z), (61, Y, Z)], [rotated, rest, halo, y_lo, y_hi]
     )
     count = lax.axis_size(GX)
     swap = [(i, i + 1) for i in range(1, count - 1, 2)]
@@ -599,7 +632,7 @@
     sizes = [lax.axis_size(stage) for stage in stages]
     coef_in, partial = call(
         inner_kernel,
-        [(len(INNER), 7, Y, Z), (KEEP, len(ONCE), Y, Z)],
+        [(len(INNER), 7, Y, Z), (KEEP, len(ONCE) + 2, Y, Z)],
         [rotated, rest, halo, y_lo, y_hi],
         scratch=[pltpu.VMEM((5, Y, Z), F32)],
         limit=6,
@@ -614,8 +647,8 @@
             pltpu.VMEM((5, Y, Z), F32),
             pltpu.VMEM((2, Y, Z), F32),
             pltpu.VMEM((len(region(3)), Y, Z), F32),
-            pltpu.VMEM((65, Y, Z), F32),
-            pltpu.VMEM((65, Y, Z), F32),
+            pltpu.VMEM((61, Y, Z), F32),
+            pltpu.VMEM((61, Y, Z), F32),
         ],
         limit=8,
     )

time: 78.5 us -> 78.3 us (level)
  waiting for transfers between devices: 5.15 us -> 4.33 us
  transfers between devices with their start and end apart: 6 -> 6, of which waited for: 3 -> 3; matrix products, arithmetic and copies ran while one was open for 0% -> 0% of each run, Pallas kernels for 5% -> 6%
where the time goes in v7:
time: 78.3 us; the launch traced here: 77.8 us
  blocking collectives  41.1 us (52%)
  starting transfers between devices  19 us (24%)
  Pallas kernels  12 us (15%)
  waiting for transfers between devices  4.33 us (6%)
    all_to_all x2, blocking collectives, exchange(): return lax.all_to_all(parts, axis, 0, 0)  37.2 us
    pallas_call x9, Pallas kernels, call(): pl.pallas_call(kernel, out_shape=[jax.ShapeDtypeStruct(s, F32) for s in o...  12 us
    ppermute x4, starting transfers between devices, send(): return lax.ppermute(value, axis, up if forward else [(j, i) for i, j in up])  10.5 us
    ppermute x1, starting transfers between devices, per_device(): off = lax.ppermute(off, GX, swap + [(j, i) for i, j in swap])  6.55 us
    ppermute x4, waiting for transfers between devices, send(): return lax.ppermute(value, axis, up if forward else [(j, i) for i, j in up])  4.2 us
    all_gather x1, blocking collectives, per_device(): whole = lax.all_gather(half, 'gx_1', axis=0, tiled=True)  3.9 us
    ppermute x1, starting transfers between devices, per_device(): on = lax.ppermute(on, 'gx_1', [(0, 1), (1, 0)])  1.94 us
  transfers between devices with their start and end apart: 6, of which 3 were waited for; matrix products, arithmetic and copies ran while one was open for 0% of the time, Pallas kernels for 6%

profile of v7, /device:TPU:1, one launch (start us, length us, event | category | flops | bytes accessed | tf_op | source)
XLA Modules:
  0.0 77.8 jit_solution(17677551274392317069)
XLA Ops:
  0.6 2.0 %shard_map.68 = (f32[60,4,8,128]{3,2,1,0:T(8,128)S(1)}, f32[5,4,8,128]{3,2,1,0:T(8,128)S(1)}, f32[5,8,128]{2,1,0:T(8,128)S(1)}) custom-call(f32[60,4,8,128]{3,2,1,0:T(8,128)} %basis.1, f32[20,60]{1,0:T(8,128)} %bitcast.4, f32[4,8,128]{2,1,0:T(8,128)} %next_vector.1, f32[4,8,128]{2,1,0:T(8,128)} %diag.1, f32[3,4,8,128]{3,2,1,0:T(8,128)} %velocity.1), custom_call_target="tpu_custom_call" | custom-call | flops 100000 | bytes 100000 | tf_op jit(solution)/shard_map/pallas_call | solution.py:47
  2.7 1.3 %collective-permute-start.1 = (f32[5,8,128]{2,1,0:T(8,128)S(1)}, f32[5,8,128]{2,1,0:T(8,128)S(1)}, u32[]{:S(2)}, u32[]{:S(2)}) collective-permute-start(f32[5,8,128]{2,1,0:T(8,128)S(1)} %get-tuple-element.18), channel_id=1, source_target_pairs={{1,0},{2,1},{3,2},{4,3},{5,4},{6,5},{7,6},{9,8},{10,9},{11,10},{12... | collective-permute-start | bytes 61448 | tf_op jit(solution)/shard_map/ppermute | solution.py:588
  4.0 4.6 %collective-permute-start = (f32[5,8,128]{2,1,0:T(8,128)S(1)}, f32[5,8,128]{2,1,0:T(8,128)S(1)}, u32[]{:S(2)}, u32[]{:S(2)}) collective-permute-start(f32[5,8,128]{2,1,0:T(8,128)S(1)} %get-tuple-element.18), channel_id=1, source_target_pairs={{0,1},{1,2},{2,3},{3,4},{4,5},{5,6},{6,7},{8,9},{9,10},{10,11},{11... | collective-permute-start | bytes 61448 | tf_op jit(solution)/shard_map/ppermute | solution.py:588
  8.6 0.0 copy-start
  8.7 0.7 copy-done
  9.4 2.7 %shard_map.69.rotated = f32[20,4,8,128]{3,2,1,0:T(8,128)S(1)} custom-call(f32[60,4,8,128]{3,2,1,0:T(8,128)S(1)} %get-tuple-element.16.basis, f32[20,60]{1,0:T(8,128)S(1)} %bitcast.5), custom_call_target="tpu_custom_call" | custom-call | flops 1000000000 | bytes 100000 | tf_op jit(solution)/shard_map/pallas_call | solution.py:47
  12.1 0.0 collective-permute-done.1.from_hi
  12.1 0.0 collective-permute-done.from_lo
  12.1 0.1 shard_map.70
  12.2 3.3 %collective-permute-start.2 = (f32[27,8,128]{2,1,0:T(8,128)S(1)}, f32[27,8,128]{2,1,0:T(8,128)S(1)}, u32[]{:S(2)}, u32[]{:S(2)}) collective-permute-start(f32[27,8,128]{2,1,0:T(8,128)S(1)} %get-tuple-element.20), channel_id=1, source_target_pairs={{0,8},{8,16},{16,24},{1,9},{9,17},{17,25},{2,10},{10,18},{18,26},{... | collective-permute-start | bytes 331784 | tf_op jit(solution)/shard_map/ppermute | solution.py:588
  15.5 1.3 %collective-permute-start.3 = (f32[27,8,128]{2,1,0:T(8,128)S(1)}, f32[27,8,128]{2,1,0:T(8,128)S(1)}, u32[]{:S(2)}, u32[]{:S(2)}) collective-permute-start(f32[27,8,128]{2,1,0:T(8,128)S(1)} %get-tuple-element.21), channel_id=1, source_target_pairs={{8,0},{16,8},{24,16},{9,1},{17,9},{25,17},{10,2},{18,10},{26,18},{... | collective-permute-start | bytes 331784 | tf_op jit(solution)/shard_map/ppermute | solution.py:588
  16.8 0.4 collective-permute-done.2.y_lo
  17.2 3.8 %collective-permute-done.3.y_hi = f32[27,8,128]{2,1,0:T(8,128)S(1)} collective-permute-done((f32[27,8,128]{2,1,0:T(8,128)S(1)}, f32[27,8,128]{2,1,0:T(8,128)S(1)}, u32[]{:S(2)}, u32[]{:S(2)}) %collective-permute-start.3) | collective-permute-done | bytes 110624 | tf_op jit(solution)/shard_map/ppermute | solution.py:588
  20.9 0.1 shard_map.72
  21.0 6.5 %collective-permute-start.4 = (f32[61,8,128]{2,1,0:T(8,128)S(1)}, f32[61,8,128]{2,1,0:T(8,128)S(1)}, u32[]{:S(2)}, u32[]{:S(2)}) collective-permute-start(f32[61,8,128]{2,1,0:T(8,128)S(1)} %get-tuple-element.24), channel_id=1, source_target_pairs={{32,64},{96,128},{160,192},{224,256},{288,320},{352,384},{416,448}... | collective-permute-start | bytes 749576 | tf_op jit(solution)/shard_map/ppermute | solution.py:629
  27.6 1.9 %collective-permute-start.5 = (f32[61,8,128]{2,1,0:T(8,128)S(1)}, f32[61,8,128]{2,1,0:T(8,128)S(1)}, u32[]{:S(2)}, u32[]{:S(2)}) collective-permute-start(f32[61,8,128]{2,1,0:T(8,128)S(1)} %get-tuple-element.25), channel_id=1, source_target_pairs={{0,32},{32,0},{1,33},{33,1},{2,34},{34,2},{3,35},{35,3},{4,36},{36... | collective-permute-start | bytes 749576 | tf_op jit(solution)/shard_map/ppermute | solution.py:630
  29.5 1.8 %shard_map.71 = (f32[16,7,8,128]{3,2,1,0:T(8,128)S(1)}, f32[20,14,8,128]{3,2,1,0:T(8,128)S(1)}) custom-call(f32[20,4,8,128]{3,2,1,0:T(8,128)S(1)} %shard_map.69.rotated, f32[5,4,8,128]{3,2,1,0:T(8,128)S(1)} %get-tuple-element.17.rest, f32[5,8,128]{2,1,0:T(8,128)S(1)} %get-tuple-element.19.halo, f32[27,8,128]{2,1,0:T(8,128)S(1)} %collective-permute-done.2.y_lo, ...), custom_call_target="tpu_custom_call" | custom-call | flops 1000000000 | bytes 100000 | tf_op jit(solution)/shard_map/pallas_call | solution.py:47
  31.4 0.1 collective-permute-done.4.off
  31.5 0.0 collective-permute-done.5.on
  31.5 2.7 %shard_map.73 = (f32[2048,128]{1,0:T(8,128)S(1)}, f32[16,1,1280]{2,1,0:T(1,128)S(1)}) custom-call(f32[20,4,8,128]{3,2,1,0:T(8,128)S(1)} %shard_map.69.rotated, f32[5,4,8,128]{3,2,1,0:T(8,128)S(1)} %get-tuple-element.17.rest, f32[5,8,128]{2,1,0:T(8,128)S(1)} %get-tuple-element.19.halo, f32[27,8,128]{2,1,0:T(8,128)S(1)} %collective-permute-done.2.y_lo, ...), custom_call_target="tpu_custom_call" | custom-call | flops 100000 | bytes 100000 | tf_op jit(solution)/shard_map/pallas_call | solution.py:47
  34.2 14.6 %all_to_all.10.parts = f32[16,1,1280]{2,1,0:T(1,128)S(1)} all-to-all(f32[16,1,1280]{2,1,0:T(1,128)S(1)} %get-tuple-element.26), channel_id=1, replica_groups=mesh['gx_0'=8,'gx_1'=2,'gy'=4,'gz'=8] {'gx_1','gz'}, dimensions={0} | all-to-all | bytes 163840 | tf_op jit(solution)/shard_map/all_to_all | solution.py:473
  48.8 22.6 %all_to_all.11.parts = f32[32,1,1280]{2,1,0:T(1,128)S(1)} all-to-all(f32[32,1,1280]{2,1,0:T(1,128)S(1)} %shard_map.74), channel_id=1, replica_groups=mesh['gx_0'=8,'gx_1'=2,'gy'=4,'gz'=8] {'gx_0','gy'}, dimensions={0} | all-to-all | bytes 327680 | tf_op jit(solution)/shard_map/all_to_all | solution.py:473
  71.4 3.9 %all_gather.3.parts = f32[2,1,1280]{2,1,0:T(1,128)S(1)} all-gather(f32[1,1,1280]{2,1,0:T(1,128)S(1)} %shard_map.75), channel_id=1, replica_groups=mesh['gx_0'=8,'gx_1'=2,'gy'=4,'gz'=8] {'gx_1'}, dimensions={0}, use_global_device_ids=true | all-gather | bytes 15360 | tf_op jit(solution)/shard_map/all_gather | solution.py:659
  75.3 2.5 %shard_map.76 = (f32[24,4,8,128]{3,2,1,0:T(8,128)}, f32[3,24]{1,0:T(4,128)}) custom-call(f32[2,1,1280]{2,1,0:T(1,128)S(1)} %all_gather.3.parts, f32[64,4,8,128]{3,2,1,0:T(8,128)S(1)} %bitcast.3), custom_call_target="tpu_custom_call" | custom-call | flops 100000 | bytes 100000 | tf_op jit(solution)/shard_map/pallas_call | solution.py:47
  (2 shorter events, 0.1 us)
Async XLA Ops:
  2.7 9.4 %collective-permute-start.1 = (f32[5,8,128]{2,1,0:T(8,128)S(1)}, f32[5,8,128]{2,1,0:T(8,128)S(1)}, u32[]{:S(2)}, u32[]{:S(2)}) collective-permute-start(f32[5,8,128]{2,1,0:T(8,128)S(1)} %get-tuple-element.18), channel_id=1, source_target_pairs={{1,0},{2,1},{3,2},{4,3},{5,4},{6,5},{7,6},{9,8},{10,9},{11,10},{12... | collective-permute-start | bytes 61448 | tf_op jit(solution)/shard_map/ppermute | solution.py:588
  4.0 8.1 %collective-permute-start = (f32[5,8,128]{2,1,0:T(8,128)S(1)}, f32[5,8,128]{2,1,0:T(8,128)S(1)}, u32[]{:S(2)}, u32[]{:S(2)}) collective-permute-start(f32[5,8,128]{2,1,0:T(8,128)S(1)} %get-tuple-element.18), channel_id=1, source_target_pairs={{0,1},{1,2},{2,3},{3,4},{4,5},{5,6},{6,7},{8,9},{9,10},{10,11},{11... | collective-permute-start | bytes 61448 | tf_op jit(solution)/shard_map/ppermute | solution.py:588
  8.6 0.7 copy-start
  12.2 5.0 %collective-permute-start.2 = (f32[27,8,128]{2,1,0:T(8,128)S(1)}, f32[27,8,128]{2,1,0:T(8,128)S(1)}, u32[]{:S(2)}, u32[]{:S(2)}) collective-permute-start(f32[27,8,128]{2,1,0:T(8,128)S(1)} %get-tuple-element.20), channel_id=1, source_target_pairs={{0,8},{8,16},{16,24},{1,9},{9,17},{17,25},{2,10},{10,18},{18,26},{... | collective-permute-start | bytes 331784 | tf_op jit(solution)/shard_map/ppermute | solution.py:588
  15.5 5.5 %collective-permute-start.3 = (f32[27,8,128]{2,1,0:T(8,128)S(1)}, f32[27,8,128]{2,1,0:T(8,128)S(1)}, u32[]{:S(2)}, u32[]{:S(2)}) collective-permute-start(f32[27,8,128]{2,1,0:T(8,128)S(1)} %get-tuple-element.21), channel_id=1, source_target_pairs={{8,0},{16,8},{24,16},{9,1},{17,9},{25,17},{10,2},{18,10},{26,18},{... | collective-permute-start | bytes 331784 | tf_op jit(solution)/shard_map/ppermute | solution.py:588
  21.0 10.5 %collective-permute-start.4 = (f32[61,8,128]{2,1,0:T(8,128)S(1)}, f32[61,8,128]{2,1,0:T(8,128)S(1)}, u32[]{:S(2)}, u32[]{:S(2)}) collective-permute-start(f32[61,8,128]{2,1,0:T(8,128)S(1)} %get-tuple-element.24), channel_id=1, source_target_pairs={{32,64},{96,128},{160,192},{224,256},{288,320},{352,384},{416,448}... | collective-permute-start | bytes 749576 | tf_op jit(solution)/shard_map/ppermute | solution.py:629
  27.6 3.9 %collective-permute-start.5 = (f32[61,8,128]{2,1,0:T(8,128)S(1)}, f32[61,8,128]{2,1,0:T(8,128)S(1)}, u32[]{:S(2)}, u32[]{:S(2)}) collective-permute-start(f32[61,8,128]{2,1,0:T(8,128)S(1)} %get-tuple-element.25), channel_id=1, source_target_pairs={{0,32},{32,0},{1,33},{33,1},{2,34},{34,2},{3,35},{35,3},{4,36},{36... | collective-permute-start | bytes 749576 | tf_op jit(solution)/shard_map/ppermute | solution.py:630

commit v8 on v7

--- a/solution.py
+++ b/solution.py
@@ -14,6 +14,7 @@
 FIELDS = 25
 SPAN = 64
 SIGMA = 7.125
+PLANES = 51
 WIRE = 1280
 GX = ("gx_0", "gx_1")
 X, Y, Z = (4, 8, 128)
@@ -181,13 +182,27 @@
     return tile
 
 
+def planes_kernel(rotated, rest, early):
+    fields = Fields(rotated, rest)
+    upper = lax.axis_index("gx_1") == 1
+    for f in range(FIELDS):
+        early[2 * f] = jnp.where(upper, fields[f, 2], fields[f, 0])
+        early[2 * f + 1] = jnp.where(upper, fields[f, 3], fields[f, 1])
+    early[PLANES - 1] = jnp.where(upper, fields[20, 1], fields[20, 2])
+
+
+def keep_kernel(source, out):
+    out[...] = source[...]
+
+
 def pack_x_kernel(rotated, rest, halo, y_lo, y_hi, off, on):
     fields = Fields(rotated, rest)
     first, row = rows_of() < 4, rows_of()
     upper = lax.axis_index("gx_1") == 1
 
     def put(at, up, down):
-        off[at] = jnp.where(upper, up, down)
+        if at >= PLANES:
+            off[at - PLANES] = jnp.where(upper, up, down)
         on[at] = jnp.where(upper, down, up)
 
     for f in range(FIELDS):
@@ -356,6 +371,7 @@
     y_hi,
     coef_in,
     partial,
+    early,
     off,
     on,
     span,
@@ -369,9 +385,10 @@
 ):
     fields = Fields(rotated, rest)
     upper = lax.axis_index("gx_1") == 1
-    for i in range(off.shape[0]):
-        x_lo[i] = jnp.where(upper, on[i], off[i])
-        x_hi[i] = jnp.where(upper, off[i], on[i])
+    for i in range(on.shape[0]):
+        far = early[i] if i < PLANES else off[i - PLANES]
+        x_lo[i] = jnp.where(upper, on[i], far)
+        x_hi[i] = jnp.where(upper, far, on[i])
     refs = (fields, halo, y_lo, y_hi, x_lo, x_hi, y_halo, x_corner)
     for p in range(5):
         y_halo[p] = corner_of(p, y_lo, y_hi)
@@ -620,13 +637,18 @@
     up, down, halo = call(
         pack_y_kernel, [(27, Y, Z), (27, Y, Z), (5, Y, Z)], [rotated, rest, z_lo, z_hi]
     )
-    y_lo, y_hi = send(up, "gy", True), send(down, "gy", False)
-    off, on = call(
-        pack_x_kernel, [(61, Y, Z), (61, Y, Z)], [rotated, rest, halo, y_lo, y_hi]
-    )
     count = lax.axis_size(GX)
     swap = [(i, i + 1) for i in range(1, count - 1, 2)]
-    off = lax.ppermute(off, GX, swap + [(j, i) for i, j in swap])
+    swap = swap + [(j, i) for i, j in swap]
+    y_lo = send(up, "gy", True)
+    y_hi = send(down, "gy", False)
+    (early,) = call(planes_kernel, [(PLANES, Y, Z)], [rotated, rest])
+    early = lax.ppermute(early, GX, swap)
+    (rest,) = call(keep_kernel, [rest.shape], [rest])
+    off, on = call(
+        pack_x_kernel, [(61 - PLANES, Y, Z), (61, Y, Z)], [rotated, rest, halo, y_lo, y_hi]
+    )
+    off = lax.ppermute(off, GX, swap)
     on = lax.ppermute(on, "gx_1", [(0, 1), (1, 0)])
     stages = (("gx_1", "gz"), ("gx_0", "gy"))
     sizes = [lax.axis_size(stage) for stage in stages]
@@ -641,7 +663,7 @@
     span, parts = call(
         functools.partial(stencil_kernel, sizes[0]),
         [(SPAN * X * Y, Z), (sizes[0], 1, WIRE)],
-        [rotated, rest, halo, y_lo, y_hi, coef_in, partial, off, on],
+        [rotated, rest, halo, y_lo, y_hi, coef_in, partial, early, off, on],
         scratch=[
             pltpu.VMEM((len(OUTER), 7, Y, Z), F32),
             pltpu.VMEM((5, Y, Z), F32),

time: 78.3 us -> 80.2 us (1.024)
  starting transfers between devices: 19 us -> 23.9 us
  blocking collectives: 41.1 us -> 38.1 us
    ppermute x1, starting transfers between devices: 1.94 us -> 7.8 us  [per_device(): on = lax.ppermute(on, 'gx_1', [(0, 1), (1, 0)])]
    all_to_all x2, blocking collectives: 37.2 us -> 34.2 us  [exchange(): return lax.all_to_all(parts, axis, 0, 0)]
    ppermute x1 -> x2, starting transfers between devices: 6.55 us -> 5.56 us  [the longest x1 3.64 us: per_device(): off = lax.ppermute(off, GX, swap)]
    pallas_call x9 -> x11, Pallas kernels: 12 us -> 12 us  [call(): pl.pallas_call(kernel, out_shape=[jax.ShapeDtypeStruct(s, F32) for s in o...]
  transfers between devices with their start and end apart: 6 -> 7, of which waited for: 3 -> 3; matrix products, arithmetic and copies ran while one was open for 0% -> 0% of each run, Pallas kernels for 6% -> 6%
where the time goes in v8:
time: 80.2 us; the launch traced here: 79.8 us
  blocking collectives  38.1 us (48%)
  starting transfers between devices  23.9 us (30%)
  Pallas kernels  12 us (15%)
  waiting for transfers between devices  4.34 us (5%)
    all_to_all x2, blocking collectives, exchange(): return lax.all_to_all(parts, axis, 0, 0)  34.2 us
    pallas_call x11, Pallas kernels, call(): pl.pallas_call(kernel, out_shape=[jax.ShapeDtypeStruct(s, F32) for s in o...  12 us
    ppermute x4, starting transfers between devices, send(): return lax.ppermute(value, axis, up if forward else [(j, i) for i, j in up])  10.5 us
    ppermute x1, starting transfers between devices, per_device(): on = lax.ppermute(on, 'gx_1', [(0, 1), (1, 0)])  7.8 us
    ppermute x4, waiting for transfers between devices, send(): return lax.ppermute(value, axis, up if forward else [(j, i) for i, j in up])  4.18 us
    all_gather x1, blocking collectives, per_device(): whole = lax.all_gather(half, 'gx_1', axis=0, tiled=True)  3.9 us
    ppermute x1, starting transfers between devices, per_device(): off = lax.ppermute(off, GX, swap)  3.64 us
    ppermute x1, starting transfers between devices, per_device(): early = lax.ppermute(early, GX, swap)  1.92 us
  transfers between devices with their start and end apart: 7, of which 3 were waited for; matrix products, arithmetic and copies ran while one was open for 0% of the time, Pallas kernels for 6%

profile of v8, /device:TPU:1, one launch (start us, length us, event | category | flops | bytes accessed | tf_op | source)
XLA Modules:
  0.0 79.8 jit_solution(12569338538202446407)
XLA Ops:
  0.6 2.0 %shard_map.68 = (f32[60,4,8,128]{3,2,1,0:T(8,128)S(1)}, f32[5,4,8,128]{3,2,1,0:T(8,128)S(1)}, f32[5,8,128]{2,1,0:T(8,128)S(1)}) custom-call(f32[60,4,8,128]{3,2,1,0:T(8,128)} %basis.1, f32[20,60]{1,0:T(8,128)} %bitcast.4, f32[4,8,128]{2,1,0:T(8,128)} %next_vector.1, f32[4,8,128]{2,1,0:T(8,128)} %diag.1, f32[3,4,8,128]{3,2,1,0:T(8,128)} %velocity.1), custom_call_target="tpu_custom_call" | custom-call | flops 100000 | bytes 100000 | tf_op jit(solution)/shard_map/pallas_call | solution.py:48
  2.7 1.3 %collective-permute-start.1 = (f32[5,8,128]{2,1,0:T(8,128)S(1)}, f32[5,8,128]{2,1,0:T(8,128)S(1)}, u32[]{:S(2)}, u32[]{:S(2)}) collective-permute-start(f32[5,8,128]{2,1,0:T(8,128)S(1)} %get-tuple-element.18), channel_id=1, source_target_pairs={{1,0},{2,1},{3,2},{4,3},{5,4},{6,5},{7,6},{9,8},{10,9},{11,10},{12... | collective-permute-start | bytes 61448 | tf_op jit(solution)/shard_map/ppermute | solution.py:605
  4.0 4.6 %collective-permute-start = (f32[5,8,128]{2,1,0:T(8,128)S(1)}, f32[5,8,128]{2,1,0:T(8,128)S(1)}, u32[]{:S(2)}, u32[]{:S(2)}) collective-permute-start(f32[5,8,128]{2,1,0:T(8,128)S(1)} %get-tuple-element.18), channel_id=1, source_target_pairs={{0,1},{1,2},{2,3},{3,4},{4,5},{5,6},{6,7},{8,9},{9,10},{10,11},{11... | collective-permute-start | bytes 61448 | tf_op jit(solution)/shard_map/ppermute | solution.py:605
  8.6 0.0 copy-start
  8.7 0.7 copy-done
  9.4 2.7 %shard_map.69.rotated = f32[20,4,8,128]{3,2,1,0:T(8,128)S(1)} custom-call(f32[60,4,8,128]{3,2,1,0:T(8,128)S(1)} %get-tuple-element.16.basis, f32[20,60]{1,0:T(8,128)S(1)} %bitcast.5), custom_call_target="tpu_custom_call" | custom-call | flops 1000000000 | bytes 100000 | tf_op jit(solution)/shard_map/pallas_call | solution.py:48
  12.1 0.0 collective-permute-done.1.from_hi
  12.1 0.0 collective-permute-done.from_lo
  12.1 0.1 shard_map.71
  12.2 3.3 %collective-permute-start.2 = (f32[27,8,128]{2,1,0:T(8,128)S(1)}, f32[27,8,128]{2,1,0:T(8,128)S(1)}, u32[]{:S(2)}, u32[]{:S(2)}) collective-permute-start(f32[27,8,128]{2,1,0:T(8,128)S(1)} %get-tuple-element.20), channel_id=1, source_target_pairs={{0,8},{8,16},{16,24},{1,9},{9,17},{17,25},{2,10},{10,18},{18,26},{... | collective-permute-start | bytes 331784 | tf_op jit(solution)/shard_map/ppermute | solution.py:605
  15.5 1.3 %collective-permute-start.3 = (f32[27,8,128]{2,1,0:T(8,128)S(1)}, f32[27,8,128]{2,1,0:T(8,128)S(1)}, u32[]{:S(2)}, u32[]{:S(2)}) collective-permute-start(f32[27,8,128]{2,1,0:T(8,128)S(1)} %get-tuple-element.21), channel_id=1, source_target_pairs={{8,0},{16,8},{24,16},{9,1},{17,9},{25,17},{10,2},{18,10},{26,18},{... | collective-permute-start | bytes 331784 | tf_op jit(solution)/shard_map/ppermute | solution.py:605
  16.8 0.4 collective-permute-done.2.y_lo
  17.2 3.8 %collective-permute-done.3.y_hi = f32[27,8,128]{2,1,0:T(8,128)S(1)} collective-permute-done((f32[27,8,128]{2,1,0:T(8,128)S(1)}, f32[27,8,128]{2,1,0:T(8,128)S(1)}, u32[]{:S(2)}, u32[]{:S(2)}) %collective-permute-start.3) | collective-permute-done | bytes 110624 | tf_op jit(solution)/shard_map/ppermute | solution.py:605
  20.9 0.1 shard_map.74
  21.0 7.8 %collective-permute-start.6 = (f32[61,8,128]{2,1,0:T(8,128)S(1)}, f32[61,8,128]{2,1,0:T(8,128)S(1)}, u32[]{:S(2)}, u32[]{:S(2)}) collective-permute-start(f32[61,8,128]{2,1,0:T(8,128)S(1)} %get-tuple-element.25), channel_id=1, source_target_pairs={{0,32},{32,0},{1,33},{33,1},{2,34},{34,2},{3,35},{35,3},{4,36},{36... | collective-permute-start | bytes 749576 | tf_op jit(solution)/shard_map/ppermute | solution.py:652
  28.9 1.9 %collective-permute-start.4 = (f32[51,8,128]{2,1,0:T(8,128)S(1)}, f32[51,8,128]{2,1,0:T(8,128)S(1)}, u32[]{:S(2)}, u32[]{:S(2)}) collective-permute-start(f32[51,8,128]{2,1,0:T(8,128)S(1)} %shard_map.73), channel_id=1, source_target_pairs={{32,64},{96,128},{160,192},{224,256},{288,320},{352,384},{416,448}... | collective-permute-start | bytes 626696 | tf_op jit(solution)/shard_map/ppermute | solution.py:646
  30.8 3.6 %collective-permute-start.5 = (f32[10,8,128]{2,1,0:T(8,128)S(1)}, f32[10,8,128]{2,1,0:T(8,128)S(1)}, u32[]{:S(2)}, u32[]{:S(2)}) collective-permute-start(f32[10,8,128]{2,1,0:T(8,128)S(1)} %get-tuple-element.24), channel_id=1, source_target_pairs={{32,64},{96,128},{160,192},{224,256},{288,320},{352,384},{416,448}... | collective-permute-start | bytes 122888 | tf_op jit(solution)/shard_map/ppermute | solution.py:651
  34.4 1.8 %shard_map.72 = (f32[16,7,8,128]{3,2,1,0:T(8,128)S(1)}, f32[20,14,8,128]{3,2,1,0:T(8,128)S(1)}) custom-call(f32[20,4,8,128]{3,2,1,0:T(8,128)S(1)} %shard_map.69.rotated, f32[5,4,8,128]{3,2,1,0:T(8,128)S(1)} %shard_map.70.rest, f32[5,8,128]{2,1,0:T(8,128)S(1)} %get-tuple-element.19.halo, f32[27,8,128]{2,1,0:T(8,128)S(1)} %collective-permute-done.2.y_lo, ...), custom_call_target="tpu_custom_call" | custom-call | flops 1000000000 | bytes 100000 | tf_op jit(solution)/shard_map/pallas_call | solution.py:48
  36.3 0.2 collective-permute-done.5.off
  36.4 0.0 collective-permute-done.4.early
  36.4 0.0 collective-permute-done.6.on
  36.4 2.7 %shard_map.75 = (f32[2048,128]{1,0:T(8,128)S(1)}, f32[16,1,1280]{2,1,0:T(1,128)S(1)}) custom-call(f32[20,4,8,128]{3,2,1,0:T(8,128)S(1)} %shard_map.69.rotated, f32[5,4,8,128]{3,2,1,0:T(8,128)S(1)} %shard_map.70.rest, f32[5,8,128]{2,1,0:T(8,128)S(1)} %get-tuple-element.19.halo, f32[27,8,128]{2,1,0:T(8,128)S(1)} %collective-permute-done.2.y_lo, ...), custom_call_target="tpu_custom_call" | custom-call | flops 100000 | bytes 100000 | tf_op jit(solution)/shard_map/pallas_call | solution.py:48
  39.1 12.8 %all_to_all.10.parts = f32[16,1,1280]{2,1,0:T(1,128)S(1)} all-to-all(f32[16,1,1280]{2,1,0:T(1,128)S(1)} %get-tuple-element.26), channel_id=1, replica_groups=mesh['gx_0'=8,'gx_1'=2,'gy'=4,'gz'=8] {'gx_1','gz'}, dimensions={0} | all-to-all | bytes 163840 | tf_op jit(solution)/shard_map/all_to_all | solution.py:490
  52.0 21.4 %all_to_all.11.parts = f32[32,1,1280]{2,1,0:T(1,128)S(1)} all-to-all(f32[32,1,1280]{2,1,0:T(1,128)S(1)} %shard_map.76), channel_id=1, replica_groups=mesh['gx_0'=8,'gx_1'=2,'gy'=4,'gz'=8] {'gx_0','gy'}, dimensions={0} | all-to-all | bytes 327680 | tf_op jit(solution)/shard_map/all_to_all | solution.py:490
  73.4 3.9 %all_gather.3.parts = f32[2,1,1280]{2,1,0:T(1,128)S(1)} all-gather(f32[1,1,1280]{2,1,0:T(1,128)S(1)} %shard_map.77), channel_id=1, replica_groups=mesh['gx_0'=8,'gx_1'=2,'gy'=4,'gz'=8] {'gx_1'}, dimensions={0}, use_global_device_ids=true | all-gather | bytes 15360 | tf_op jit(solution)/shard_map/all_gather | solution.py:681
  77.3 2.5 %shard_map.78 = (f32[24,4,8,128]{3,2,1,0:T(8,128)}, f32[3,24]{1,0:T(4,128)}) custom-call(f32[2,1,1280]{2,1,0:T(1,128)S(1)} %all_gather.3.parts, f32[64,4,8,128]{3,2,1,0:T(8,128)S(1)} %bitcast.3), custom_call_target="tpu_custom_call" | custom-call | flops 100000 | bytes 100000 | tf_op jit(solution)/shard_map/pallas_call | solution.py:48
  (4 shorter events, 0.1 us)
Async XLA Ops:
  2.7 9.4 %collective-permute-start.1 = (f32[5,8,128]{2,1,0:T(8,128)S(1)}, f32[5,8,128]{2,1,0:T(8,128)S(1)}, u32[]{:S(2)}, u32[]{:S(2)}) collective-permute-start(f32[5,8,128]{2,1,0:T(8,128)S(1)} %get-tuple-element.18), channel_id=1, source_target_pairs={{1,0},{2,1},{3,2},{4,3},{5,4},{6,5},{7,6},{9,8},{10,9},{11,10},{12... | collective-permute-start | bytes 61448 | tf_op jit(solution)/shard_map/ppermute | solution.py:605
  4.0 8.1 %collective-permute-start = (f32[5,8,128]{2,1,0:T(8,128)S(1)}, f32[5,8,128]{2,1,0:T(8,128)S(1)}, u32[]{:S(2)}, u32[]{:S(2)}) collective-permute-start(f32[5,8,128]{2,1,0:T(8,128)S(1)} %get-tuple-element.18), channel_id=1, source_target_pairs={{0,1},{1,2},{2,3},{3,4},{4,5},{5,6},{6,7},{8,9},{9,10},{10,11},{11... | collective-permute-start | bytes 61448 | tf_op jit(solution)/shard_map/ppermute | solution.py:605
  8.6 0.7 copy-start
  12.2 5.0 %collective-permute-start.2 = (f32[27,8,128]{2,1,0:T(8,128)S(1)}, f32[27,8,128]{2,1,0:T(8,128)S(1)}, u32[]{:S(2)}, u32[]{:S(2)}) collective-permute-start(f32[27,8,128]{2,1,0:T(8,128)S(1)} %get-tuple-element.20), channel_id=1, source_target_pairs={{0,8},{8,16},{16,24},{1,9},{9,17},{17,25},{2,10},{10,18},{18,26},{... | collective-permute-start | bytes 331784 | tf_op jit(solution)/shard_map/ppermute | solution.py:605
  15.5 5.5 %collective-permute-start.3 = (f32[27,8,128]{2,1,0:T(8,128)S(1)}, f32[27,8,128]{2,1,0:T(8,128)S(1)}, u32[]{:S(2)}, u32[]{:S(2)}) collective-permute-start(f32[27,8,128]{2,1,0:T(8,128)S(1)} %get-tuple-element.21), channel_id=1, source_target_pairs={{8,0},{16,8},{24,16},{9,1},{17,9},{25,17},{10,2},{18,10},{26,18},{... | collective-permute-start | bytes 331784 | tf_op jit(solution)/shard_map/ppermute | solution.py:605
  21.0 15.4 %collective-permute-start.6 = (f32[61,8,128]{2,1,0:T(8,128)S(1)}, f32[61,8,128]{2,1,0:T(8,128)S(1)}, u32[]{:S(2)}, u32[]{:S(2)}) collective-permute-start(f32[61,8,128]{2,1,0:T(8,128)S(1)} %get-tuple-element.25), channel_id=1, source_target_pairs={{0,32},{32,0},{1,33},{33,1},{2,34},{34,2},{3,35},{35,3},{4,36},{36... | collective-permute-start | bytes 749576 | tf_op jit(solution)/shard_map/ppermute | solution.py:652
  28.9 7.6 %collective-permute-start.4 = (f32[51,8,128]{2,1,0:T(8,128)S(1)}, f32[51,8,128]{2,1,0:T(8,128)S(1)}, u32[]{:S(2)}, u32[]{:S(2)}) collective-permute-start(f32[51,8,128]{2,1,0:T(8,128)S(1)} %shard_map.73), channel_id=1, source_target_pairs={{32,64},{96,128},{160,192},{224,256},{288,320},{352,384},{416,448}... | collective-permute-start | bytes 626696 | tf_op jit(solution)/shard_map/ppermute | solution.py:646
  30.8 5.6 %collective-permute-start.5 = (f32[10,8,128]{2,1,0:T(8,128)S(1)}, f32[10,8,128]{2,1,0:T(8,128)S(1)}, u32[]{:S(2)}, u32[]{:S(2)}) collective-permute-start(f32[10,8,128]{2,1,0:T(8,128)S(1)} %get-tuple-element.24), channel_id=1, source_target_pairs={{32,64},{96,128},{160,192},{224,256},{288,320},{352,384},{416,448}... | collective-permute-start | bytes 122888 | tf_op jit(solution)/shard_map/ppermute | solution.py:651

commit v9 on v8

--- a/solution.py
+++ b/solution.py
@@ -191,10 +191,6 @@
     early[PLANES - 1] = jnp.where(upper, fields[20, 1], fields[20, 2])
 
 
-def keep_kernel(source, out):
-    out[...] = source[...]
-
-
 def pack_x_kernel(rotated, rest, halo, y_lo, y_hi, off, on):
     fields = Fields(rotated, rest)
     first, row = rows_of() < 4, rows_of()
@@ -294,18 +290,24 @@
     return shift_lanes(packed, by)
 
 
-def apply(get, key, coef, skip=()):
+def along_y(get, key, coef):
     x, a, b = key
-    row, lane = rows_of(), lanes_of()
-    centre = get((x, a, b))
-    y_other = get((x, 1 - a, b))
-    z_other = get((x, a, 1 - b))
-    y_ahead = shift_rows(jnp.where(row == 0, y_other, centre), 7)
-    y_behind = shift_rows(jnp.where(row == 7, y_other, centre), 1)
-    z_ahead = shift_lanes(jnp.where(lane == 0, z_other, centre), 127)
-    z_behind = shift_lanes(jnp.where(lane == 127, z_other, centre), 1)
-    total = coef(key, 3) * y_ahead + coef(key, 4) * y_behind
-    total = total + (coef(key, 5) * z_ahead + coef(key, 6) * z_behind)
+    row = rows_of()
+    centre, other = get(key), get((x, 1 - a, b))
+    ahead = shift_rows(jnp.where(row == 0, other, centre), 7)
+    behind = shift_rows(jnp.where(row == 7, other, centre), 1)
+    return coef(key, 3) * ahead + coef(key, 4) * behind
+
+
+def apply(get, key, coef, skip=(), with_y=True):
+    x, a, b = key
+    lane = lanes_of()
+    centre, other = get(key), get((x, a, 1 - b))
+    ahead = shift_lanes(jnp.where(lane == 0, other, centre), 127)
+    behind = shift_lanes(jnp.where(lane == 127, other, centre), 1)
+    total = coef(key, 5) * ahead + coef(key, 6) * behind
+    if with_y:
+        total = along_y(get, key, coef) + total
     total = total + coef(key, 0) * centre
     for i, at in ((1, (x + 1, a, b)), (2, (x - 1, a, b))):
         if i not in skip:
@@ -336,24 +338,52 @@
 
 
 INNER = [key for key in COEF if 0 <= key[0] < X]
+LEVEL = [key for key in INNER if not key[1]]
+BESIDE = [key for key in INNER if key[1]]
 OUTER = [key for key in COEF if not 0 <= key[0] < X]
 ONCE = [key for key in region(1) if 0 <= key[0] < X]
 SIDES = {0: (2, -1), X - 1: (1, X)}
 
 
-def inner_kernel(rotated, rest, halo, y_lo, y_hi, coef_in, partial, y_halo):
+def skip_of(key):
+    return (SIDES[key[0]][0],) if key[0] in SIDES else ()
+
+
+def level_kernel(rotated, rest, halo, coef_level, partial):
+    refs = (Fields(rotated, rest), halo, None, None, None, None, None, None)
+    fill_coefficients(LEVEL, coef_level, refs)
+    coef = lambda key, i: coef_level[LEVEL.index(key), i]
+
+    def body(f, carry):
+        get = cached(f, refs)
+        for at, key in enumerate(LEVEL):
+            partial[f, at] = apply(get, key, coef, skip_of(key), with_y=False)
+        return carry
+
+    lax.fori_loop(0, KEEP, body, 0, unroll=4)
+
+
+def inner_kernel(
+    rotated, rest, halo, y_lo, y_hi, coef_level, level, coef_beside, partial, y_halo
+):
     for p in range(5):
         y_halo[p] = corner_of(p, y_lo, y_hi)
     refs = (Fields(rotated, rest), halo, y_lo, y_hi, None, None, y_halo, None)
-    fill_coefficients(INNER, coef_in, refs)
-    coef = lambda key, i: coef_in[INNER.index(key), i]
+    fill_coefficients(BESIDE, coef_beside, refs)
+
+    def coef(key, i):
+        if key in LEVEL:
+            return coef_level[LEVEL.index(key), i]
+        return coef_beside[BESIDE.index(key), i]
 
     def body(f, carry):
         get = cached(f, refs)
         once = {}
         for at, key in enumerate(ONCE):
-            skip = (SIDES[key[0]][0],) if key[0] in SIDES else ()
-            once[key] = apply(get, key, coef, skip)
+            if key in LEVEL:
+                once[key] = level[f, LEVEL.index(key)] + along_y(get, key, coef)
+            else:
+                once[key] = apply(get, key, coef, skip_of(key))
             partial[f, at] = once[key]
         for x, skip in ((1, (2,)), (2, (1,))):
             partial[f, len(ONCE) + x - 1] = apply(once.__getitem__, (x, 0, 0), coef, skip)
@@ -369,7 +399,8 @@
     halo,
     y_lo,
     y_hi,
-    coef_in,
+    coef_level,
+    coef_beside,
     partial,
     early,
     off,
@@ -397,8 +428,10 @@
     fill_coefficients(OUTER, coef_out, refs)
 
     def coef(key, i):
-        if key in INNER:
-            return coef_in[INNER.index(key), i]
+        if key in LEVEL:
+            return coef_level[LEVEL.index(key), i]
+        if key in BESIDE:
+            return coef_beside[BESIDE.index(key), i]
         return coef_out[OUTER.index(key), i]
 
     def store(f, x, tile):
@@ -644,7 +677,12 @@
     y_hi = send(down, "gy", False)
     (early,) = call(planes_kernel, [(PLANES, Y, Z)], [rotated, rest])
     early = lax.ppermute(early, GX, swap)
-    (rest,) = call(keep_kernel, [rest.shape], [rest])
+    coef_level, level = call(
+        level_kernel,
+        [(len(LEVEL), 7, Y, Z), (KEEP, len(LEVEL), Y, Z)],
+        [rotated, rest, halo],
+        limit=4,
+    )
     off, on = call(
         pack_x_kernel, [(61 - PLANES, Y, Z), (61, Y, Z)], [rotated, rest, halo, y_lo, y_hi]
     )
@@ -652,10 +690,10 @@
     on = lax.ppermute(on, "gx_1", [(0, 1), (1, 0)])
     stages = (("gx_1", "gz"), ("gx_0", "gy"))
     sizes = [lax.axis_size(stage) for stage in stages]
-    coef_in, partial = call(
+    coef_beside, partial = call(
         inner_kernel,
-        [(len(INNER), 7, Y, Z), (KEEP, len(ONCE) + 2, Y, Z)],
-        [rotated, rest, halo, y_lo, y_hi],
+        [(len(BESIDE), 7, Y, Z), (KEEP, len(ONCE) + 2, Y, Z)],
+        [rotated, rest, halo, y_lo, y_hi, coef_level, level],
         scratch=[pltpu.VMEM((5, Y, Z), F32)],
         limit=6,
         flops=10**9,
@@ -663,7 +701,7 @@
     span, parts = call(
         functools.partial(stencil_kernel, sizes[0]),
         [(SPAN * X * Y, Z), (sizes[0], 1, WIRE)],
-        [rotated, rest, halo, y_lo, y_hi, coef_in, partial, early, off, on],
+        [rotated, rest, halo, y_lo, y_hi, coef_level, coef_beside, partial, early, off, on],
         scratch=[
             pltpu.VMEM((len(OUTER), 7, Y, Z), F32),
             pltpu.VMEM((5, Y, Z), F32),

time: 80.2 us -> 81.4 us (1.015)
  no operation moved by 1% of the time
where the time goes in v9:
time: 81.4 us; the launch traced here: 80.9 us
  blocking collectives  38.3 us (47%)
  starting transfers between devices  23.9 us (29%)
  Pallas kernels  12.6 us (15%)
  waiting for transfers between devices  4.65 us (6%)
    all_to_all x2, blocking collectives, exchange(): return lax.all_to_all(parts, axis, 0, 0)  34.4 us
    pallas_call x11, Pallas kernels, call(): pl.pallas_call(kernel, out_shape=[jax.ShapeDtypeStruct(s, F32) for s in o...  12.6 us
    ppermute x4, starting transfers between devices, send(): return lax.ppermute(value, axis, up if forward else [(j, i) for i, j in up])  10.5 us
    ppermute x1, starting transfers between devices, per_device(): on = lax.ppermute(on, 'gx_1', [(0, 1), (1, 0)])  7.8 us
    ppermute x4, waiting for transfers between devices, send(): return lax.ppermute(value, axis, up if forward else [(j, i) for i, j in up])  4.2 us
    all_gather x1, blocking collectives, per_device(): whole = lax.all_gather(half, 'gx_1', axis=0, tiled=True)  3.9 us
    ppermute x1, starting transfers between devices, per_device(): off = lax.ppermute(off, GX, swap)  3.64 us
    ppermute x1, starting transfers between devices, per_device(): early = lax.ppermute(early, GX, swap)  1.92 us
  transfers between devices with their start and end apart: 7, of which 3 were waited for; matrix products, arithmetic and copies ran while one was open for 0% of the time, Pallas kernels for 6%

profile of v9, /device:TPU:1, one launch (start us, length us, event | category | flops | bytes accessed | tf_op | source)
XLA Modules:
  0.0 80.9 jit_solution(8961108335955379788)
XLA Ops:
  0.6 2.0 %shard_map.68 = (f32[60,4,8,128]{3,2,1,0:T(8,128)S(1)}, f32[5,4,8,128]{3,2,1,0:T(8,128)S(1)}, f32[5,8,128]{2,1,0:T(8,128)S(1)}) custom-call(f32[60,4,8,128]{3,2,1,0:T(8,128)} %basis.1, f32[20,60]{1,0:T(8,128)} %bitcast.4, f32[4,8,128]{2,1,0:T(8,128)} %next_vector.1, f32[4,8,128]{2,1,0:T(8,128)} %diag.1, f32[3,4,8,128]{3,2,1,0:T(8,128)} %velocity.1), custom_call_target="tpu_custom_call" | custom-call | flops 100000 | bytes 100000 | tf_op jit(solution)/shard_map/pallas_call | solution.py:48
  2.7 1.3 %collective-permute-start.1 = (f32[5,8,128]{2,1,0:T(8,128)S(1)}, f32[5,8,128]{2,1,0:T(8,128)S(1)}, u32[]{:S(2)}, u32[]{:S(2)}) collective-permute-start(f32[5,8,128]{2,1,0:T(8,128)S(1)} %get-tuple-element.20), channel_id=1, source_target_pairs={{1,0},{2,1},{3,2},{4,3},{5,4},{6,5},{7,6},{9,8},{10,9},{11,10},{12... | collective-permute-start | bytes 61448 | tf_op jit(solution)/shard_map/ppermute | solution.py:638
  4.0 4.6 %collective-permute-start = (f32[5,8,128]{2,1,0:T(8,128)S(1)}, f32[5,8,128]{2,1,0:T(8,128)S(1)}, u32[]{:S(2)}, u32[]{:S(2)}) collective-permute-start(f32[5,8,128]{2,1,0:T(8,128)S(1)} %get-tuple-element.20), channel_id=1, source_target_pairs={{0,1},{1,2},{2,3},{3,4},{4,5},{5,6},{6,7},{8,9},{9,10},{10,11},{11... | collective-permute-start | bytes 61448 | tf_op jit(solution)/shard_map/ppermute | solution.py:638
  8.6 0.0 copy-start
  8.7 0.7 copy-done
  9.4 2.7 %shard_map.69.rotated = f32[20,4,8,128]{3,2,1,0:T(8,128)S(1)} custom-call(f32[60,4,8,128]{3,2,1,0:T(8,128)S(1)} %get-tuple-element.18.basis, f32[20,60]{1,0:T(8,128)S(1)} %bitcast.5), custom_call_target="tpu_custom_call" | custom-call | flops 1000000000 | bytes 100000 | tf_op jit(solution)/shard_map/pallas_call | solution.py:48
  12.1 0.0 collective-permute-done.1.from_hi
  12.1 0.0 collective-permute-done.from_lo
  12.1 0.1 shard_map.70
  12.2 3.3 %collective-permute-start.2 = (f32[27,8,128]{2,1,0:T(8,128)S(1)}, f32[27,8,128]{2,1,0:T(8,128)S(1)}, u32[]{:S(2)}, u32[]{:S(2)}) collective-permute-start(f32[27,8,128]{2,1,0:T(8,128)S(1)} %get-tuple-element.22), channel_id=1, source_target_pairs={{0,8},{8,16},{16,24},{1,9},{9,17},{17,25},{2,10},{10,18},{18,26},{... | collective-permute-start | bytes 331784 | tf_op jit(solution)/shard_map/ppermute | solution.py:638
  15.5 1.3 %collective-permute-start.3 = (f32[27,8,128]{2,1,0:T(8,128)S(1)}, f32[27,8,128]{2,1,0:T(8,128)S(1)}, u32[]{:S(2)}, u32[]{:S(2)}) collective-permute-start(f32[27,8,128]{2,1,0:T(8,128)S(1)} %get-tuple-element.23), channel_id=1, source_target_pairs={{8,0},{16,8},{24,16},{9,1},{17,9},{25,17},{10,2},{18,10},{26,18},{... | collective-permute-start | bytes 331784 | tf_op jit(solution)/shard_map/ppermute | solution.py:638
  16.8 0.4 collective-permute-done.2.y_lo
  17.2 3.8 %collective-permute-done.3.y_hi = f32[27,8,128]{2,1,0:T(8,128)S(1)} collective-permute-done((f32[27,8,128]{2,1,0:T(8,128)S(1)}, f32[27,8,128]{2,1,0:T(8,128)S(1)}, u32[]{:S(2)}, u32[]{:S(2)}) %collective-permute-start.3) | collective-permute-done | bytes 110624 | tf_op jit(solution)/shard_map/ppermute | solution.py:638
  20.9 0.1 shard_map.74
  21.0 7.8 %collective-permute-start.6 = (f32[61,8,128]{2,1,0:T(8,128)S(1)}, f32[61,8,128]{2,1,0:T(8,128)S(1)}, u32[]{:S(2)}, u32[]{:S(2)}) collective-permute-start(f32[61,8,128]{2,1,0:T(8,128)S(1)} %get-tuple-element.29), channel_id=1, source_target_pairs={{0,32},{32,0},{1,33},{33,1},{2,34},{34,2},{3,35},{35,3},{4,36},{36... | collective-permute-start | bytes 749576 | tf_op jit(solution)/shard_map/ppermute | solution.py:690
  28.9 1.9 %collective-permute-start.4 = (f32[51,8,128]{2,1,0:T(8,128)S(1)}, f32[51,8,128]{2,1,0:T(8,128)S(1)}, u32[]{:S(2)}, u32[]{:S(2)}) collective-permute-start(f32[51,8,128]{2,1,0:T(8,128)S(1)} %shard_map.73), channel_id=1, source_target_pairs={{32,64},{96,128},{160,192},{224,256},{288,320},{352,384},{416,448}... | collective-permute-start | bytes 626696 | tf_op jit(solution)/shard_map/ppermute | solution.py:679
  30.8 1.2 %shard_map.71 = (f32[8,7,8,128]{3,2,1,0:T(8,128)S(1)}, f32[20,8,8,128]{3,2,1,0:T(8,128)S(1)}) custom-call(f32[20,4,8,128]{3,2,1,0:T(8,128)S(1)} %shard_map.69.rotated, f32[5,4,8,128]{3,2,1,0:T(8,128)S(1)} %get-tuple-element.19.rest, f32[5,8,128]{2,1,0:T(8,128)S(1)} %get-tuple-element.21.halo), custom_call_target="tpu_custom_call" | custom-call | flops 100000 | bytes 100000 | tf_op jit(solution)/shard_map/pallas_call | solution.py:48
  32.0 3.6 %collective-permute-start.5 = (f32[10,8,128]{2,1,0:T(8,128)S(1)}, f32[10,8,128]{2,1,0:T(8,128)S(1)}, u32[]{:S(2)}, u32[]{:S(2)}) collective-permute-start(f32[10,8,128]{2,1,0:T(8,128)S(1)} %get-tuple-element.28), channel_id=1, source_target_pairs={{32,64},{96,128},{160,192},{224,256},{288,320},{352,384},{416,448}... | collective-permute-start | bytes 122888 | tf_op jit(solution)/shard_map/ppermute | solution.py:689
  35.6 1.2 %shard_map.72 = (f32[8,7,8,128]{3,2,1,0:T(8,128)S(1)}, f32[20,14,8,128]{3,2,1,0:T(8,128)S(1)}) custom-call(f32[20,4,8,128]{3,2,1,0:T(8,128)S(1)} %shard_map.69.rotated, f32[5,4,8,128]{3,2,1,0:T(8,128)S(1)} %get-tuple-element.19.rest, f32[5,8,128]{2,1,0:T(8,128)S(1)} %get-tuple-element.21.halo, f32[27,8,128]{2,1,0:T(8,128)S(1)} %collective-permute-done.2.y_lo, ...), custom_call_target="tpu_custom_call" | custom-call | flops 1000000000 | bytes 100000 | tf_op jit(solution)/shard_map/pallas_call | solution.py:48
  36.9 0.5 collective-permute-done.5.off
  37.3 0.0 collective-permute-done.4.early
  37.3 0.0 collective-permute-done.6.on
  37.3 2.7 %shard_map.75 = (f32[2048,128]{1,0:T(8,128)S(1)}, f32[16,1,1280]{2,1,0:T(1,128)S(1)}) custom-call(f32[20,4,8,128]{3,2,1,0:T(8,128)S(1)} %shard_map.69.rotated, f32[5,4,8,128]{3,2,1,0:T(8,128)S(1)} %get-tuple-element.19.rest, f32[5,8,128]{2,1,0:T(8,128)S(1)} %get-tuple-element.21.halo, f32[27,8,128]{2,1,0:T(8,128)S(1)} %collective-permute-done.2.y_lo, ...), custom_call_target="tpu_custom_call" | custom-call | flops 100000 | bytes 100000 | tf_op jit(solution)/shard_map/pallas_call | solution.py:48
  40.0 13.1 %all_to_all.10.parts = f32[16,1,1280]{2,1,0:T(1,128)S(1)} all-to-all(f32[16,1,1280]{2,1,0:T(1,128)S(1)} %get-tuple-element.30), channel_id=1, replica_groups=mesh['gx_0'=8,'gx_1'=2,'gy'=4,'gz'=8] {'gx_1','gz'}, dimensions={0} | all-to-all | bytes 163840 | tf_op jit(solution)/shard_map/all_to_all | solution.py:523
  53.1 21.4 %all_to_all.11.parts = f32[32,1,1280]{2,1,0:T(1,128)S(1)} all-to-all(f32[32,1,1280]{2,1,0:T(1,128)S(1)} %shard_map.76), channel_id=1, replica_groups=mesh['gx_0'=8,'gx_1'=2,'gy'=4,'gz'=8] {'gx_0','gy'}, dimensions={0} | all-to-all | bytes 327680 | tf_op jit(solution)/shard_map/all_to_all | solution.py:523
  74.5 3.9 %all_gather.3.parts = f32[2,1,1280]{2,1,0:T(1,128)S(1)} all-gather(f32[1,1,1280]{2,1,0:T(1,128)S(1)} %shard_map.77), channel_id=1, replica_groups=mesh['gx_0'=8,'gx_1'=2,'gy'=4,'gz'=8] {'gx_1'}, dimensions={0}, use_global_device_ids=true | all-gather | bytes 15360 | tf_op jit(solution)/shard_map/all_gather | solution.py:719
  78.4 2.5 %shard_map.78 = (f32[24,4,8,128]{3,2,1,0:T(8,128)}, f32[3,24]{1,0:T(4,128)}) custom-call(f32[2,1,1280]{2,1,0:T(1,128)S(1)} %all_gather.3.parts, f32[64,4,8,128]{3,2,1,0:T(8,128)S(1)} %bitcast.3), custom_call_target="tpu_custom_call" | custom-call | flops 100000 | bytes 100000 | tf_op jit(solution)/shard_map/pallas_call | solution.py:48
  (3 shorter events, 0.1 us)
Async XLA Ops:
  2.7 9.4 %collective-permute-start.1 = (f32[5,8,128]{2,1,0:T(8,128)S(1)}, f32[5,8,128]{2,1,0:T(8,128)S(1)}, u32[]{:S(2)}, u32[]{:S(2)}) collective-permute-start(f32[5,8,128]{2,1,0:T(8,128)S(1)} %get-tuple-element.20), channel_id=1, source_target_pairs={{1,0},{2,1},{3,2},{4,3},{5,4},{6,5},{7,6},{9,8},{10,9},{11,10},{12... | collective-permute-start | bytes 61448 | tf_op jit(solution)/shard_map/ppermute | solution.py:638
  4.0 8.1 %collective-permute-start = (f32[5,8,128]{2,1,0:T(8,128)S(1)}, f32[5,8,128]{2,1,0:T(8,128)S(1)}, u32[]{:S(2)}, u32[]{:S(2)}) collective-permute-start(f32[5,8,128]{2,1,0:T(8,128)S(1)} %get-tuple-element.20), channel_id=1, source_target_pairs={{0,1},{1,2},{2,3},{3,4},{4,5},{5,6},{6,7},{8,9},{9,10},{10,11},{11... | collective-permute-start | bytes 61448 | tf_op jit(solution)/shard_map/ppermute | solution.py:638
  8.6 0.7 copy-start
  12.2 5.0 %collective-permute-start.2 = (f32[27,8,128]{2,1,0:T(8,128)S(1)}, f32[27,8,128]{2,1,0:T(8,128)S(1)}, u32[]{:S(2)}, u32[]{:S(2)}) collective-permute-start(f32[27,8,128]{2,1,0:T(8,128)S(1)} %get-tuple-element.22), channel_id=1, source_target_pairs={{0,8},{8,16},{16,24},{1,9},{9,17},{17,25},{2,10},{10,18},{18,26},{... | collective-permute-start | bytes 331784 | tf_op jit(solution)/shard_map/ppermute | solution.py:638
  15.5 5.5 %collective-permute-start.3 = (f32[27,8,128]{2,1,0:T(8,128)S(1)}, f32[27,8,128]{2,1,0:T(8,128)S(1)}, u32[]{:S(2)}, u32[]{:S(2)}) collective-permute-start(f32[27,8,128]{2,1,0:T(8,128)S(1)} %get-tuple-element.23), channel_id=1, source_target_pairs={{8,0},{16,8},{24,16},{9,1},{17,9},{25,17},{10,2},{18,10},{26,18},{... | collective-permute-start | bytes 331784 | tf_op jit(solution)/shard_map/ppermute | solution.py:638
  21.0 16.3 %collective-permute-start.6 = (f32[61,8,128]{2,1,0:T(8,128)S(1)}, f32[61,8,128]{2,1,0:T(8,128)S(1)}, u32[]{:S(2)}, u32[]{:S(2)}) collective-permute-start(f32[61,8,128]{2,1,0:T(8,128)S(1)} %get-tuple-element.29), channel_id=1, source_target_pairs={{0,32},{32,0},{1,33},{33,1},{2,34},{34,2},{3,35},{35,3},{4,36},{36... | collective-permute-start | bytes 749576 | tf_op jit(solution)/shard_map/ppermute | solution.py:690
  28.9 8.4 %collective-permute-start.4 = (f32[51,8,128]{2,1,0:T(8,128)S(1)}, f32[51,8,128]{2,1,0:T(8,128)S(1)}, u32[]{:S(2)}, u32[]{:S(2)}) collective-permute-start(f32[51,8,128]{2,1,0:T(8,128)S(1)} %shard_map.73), channel_id=1, source_target_pairs={{32,64},{96,128},{160,192},{224,256},{288,320},{352,384},{416,448}... | collective-permute-start | bytes 626696 | tf_op jit(solution)/shard_map/ppermute | solution.py:679
  32.0 5.3 %collective-permute-start.5 = (f32[10,8,128]{2,1,0:T(8,128)S(1)}, f32[10,8,128]{2,1,0:T(8,128)S(1)}, u32[]{:S(2)}, u32[]{:S(2)}) collective-permute-start(f32[10,8,128]{2,1,0:T(8,128)S(1)} %get-tuple-element.28), channel_id=1, source_target_pairs={{32,64},{96,128},{160,192},{224,256},{288,320},{352,384},{416,448}... | collective-permute-start | bytes 122888 | tf_op jit(solution)/shard_map/ppermute | solution.py:689

commit v10 on v9

--- a/solution.py
+++ b/solution.py
@@ -60,7 +60,7 @@
 
 
 def edge_kernel(
-    basis, schur, next_vector, diag, velocity, held, rest, packed, weights, small, sems
+    basis, schur, next_vector, diag, velocity, held, rest, packed, passed, weights, small, sems
 ):
     chunks = basis.shape[0] // CHUNK
     copies = [
@@ -74,10 +74,25 @@
         pltpu.make_async_copy(next_vector, rest.at[0], sems.at[1 + chunks]),
         pltpu.make_async_copy(diag, small.at[0], sems.at[2 + chunks]),
         pltpu.make_async_copy(velocity, small.at[pl.ds(1, 3)], sems.at[3 + chunks]),
+        pltpu.make_async_copy(schur, passed, sems.at[4 + chunks]),
     ]
-    for copy in copies:
+    for copy in copies[1 + chunks : 4 + chunks]:
         copy.start()
+    for copy in copies[: 1 + chunks]:
+        copy.start()
+    copies[4 + chunks].start()
     lane = lanes_of()
+    for copy in copies[1 + chunks : 4 + chunks]:
+        copy.wait()
+    for x in range(X):
+        rest[1, x] = 6.0 + small[0, x]
+        for d in range(3):
+            rest[2 + d, x] = 0.5 * small[1 + d, x]
+    total = jnp.zeros(TILE, F32)
+    for j in range(20):
+        moved = shift_lanes(rest[j // 4, j % 4], 6 * j + 3)
+        total = jnp.where((lane >= 6 * j) & (lane < 6 * j + 6), moved, total)
+    packed[4] = total
     copies[0].wait()
     acc = [jnp.zeros(TILE, F32) for _ in range(KEEP)]
     for c in range(chunks):
@@ -94,17 +109,7 @@
         for q in range(1, 5):
             total = jnp.where(lane < 24 * q, total, shift_lanes(acc[5 * p + q], 24 * q))
         packed[p] = total
-    for copy in copies[1 + chunks :]:
-        copy.wait()
-    for x in range(X):
-        rest[1, x] = 6.0 + small[0, x]
-        for d in range(3):
-            rest[2 + d, x] = 0.5 * small[1 + d, x]
-    total = jnp.zeros(TILE, F32)
-    for j in range(20):
-        moved = shift_lanes(rest[j // 4, j % 4], 6 * j + 3)
-        total = jnp.where((lane >= 6 * j) & (lane < 6 * j + 6), moved, total)
-    packed[4] = total
+    copies[4 + chunks].wait()
 
 
 def rotate_kernel(basis, schur, rotated):
@@ -392,6 +397,10 @@
     lax.fori_loop(0, KEEP, body, 0, unroll=4)
 
 
+def inner(a, b):
+    return lax.dot_general(a, b, (((1,), (1,)), ((), ())), preferred_element_type=F32)
+
+
 def stencil_kernel(
     copies,
     rotated,
@@ -477,19 +486,22 @@
             store(f + 40, x, partial[f, len(ONCE) + x - 1] + term)
         return carry
 
-    lax.fori_loop(0, KEEP, body, 0, unroll=4)
-
-    total = jnp.zeros((SPAN, SPAN), F32)
+    lax.fori_loop(0, KEEP, body, 0, unroll=5)
+
+    even = jnp.zeros((SPAN, SPAN), F32)
+    mixed = even
     for r in range(0, X * Y, 2):
         pair = [span[pl.ds(r + i, SPAN, stride=X * Y), :] for i in range(2)]
         rows = jnp.concatenate(pair, axis=1)
-        total = total + lax.dot_general(
-            rows,
-            rows,
-            (((1,), (1,)), ((), ())),
-            precision=lax.Precision.HIGHEST,
-            preferred_element_type=F32,
-        )
+        high = rows.astype(jnp.bfloat16)
+        left = rows - high.astype(F32)
+        middle = left.astype(jnp.bfloat16)
+        low = (left - middle.astype(F32)).astype(jnp.bfloat16)
+        even = even + (inner(high, high) + inner(middle, middle))
+        mixed = mixed + (inner(high, middle) + inner(high, low))
+    square = jnp.concatenate([mixed, jnp.zeros((SPAN, Z - SPAN), F32)], axis=1)
+    square = jnp.concatenate([square, jnp.zeros((Z - SPAN, Z), F32)], axis=0)
+    total = even + (mixed + square.T[:SPAN, :SPAN])
     wide = jnp.concatenate([total, jnp.zeros((SPAN, Z - SPAN), F32)], axis=1)
     lane = lax.broadcasted_iota(jnp.int32, (16, Z), 1)
     main = jnp.where(
@@ -643,9 +655,14 @@
     cell_count = next_vector.size
     for axis in axes:
         cell_count *= lax.axis_size(axis)
-    held, rest, packed = call(
+    held, rest, packed, passed = call(
         edge_kernel,
-        [krylov_basis.shape, (FIELDS - KEEP, X, Y, Z), (5, Y, Z)],
+        [
+            krylov_basis.shape,
+            (FIELDS - KEEP, X, Y, Z),
+            (5, Y, Z),
+            (KEEP, krylov_basis.shape[0]),
+        ],
         [
             pltpu.with_memory_space_constraint(value, pltpu.HBM)
             for value in (krylov_basis, schur_vectors.T, next_vector, diag_shift, velocity)
@@ -653,7 +670,7 @@
         scratch=[
             pltpu.SMEM((KEEP, krylov_basis.shape[0]), F32),
             pltpu.VMEM((4, X, Y, Z), F32),
-            pltpu.SemaphoreType.DMA((4 + krylov_basis.shape[0] // CHUNK,)),
+            pltpu.SemaphoreType.DMA((5 + krylov_basis.shape[0] // CHUNK,)),
         ],
         ins="hhhhh",
         limit=4,
@@ -662,7 +679,7 @@
     (rotated,) = call(
         rotate_kernel,
         [(KEEP, X, Y, Z)],
-        [held, schur_vectors.T],
+        [held, passed],
         ins="vs",
         limit=4,
         flops=10**9,

time: 81.4 us -> 80.8 us (level)
  no operation moved by 1% of the time
where the time goes in v10:
time: 80.8 us; the launch traced here: 80.4 us
  blocking collectives  39 us (48%)
  starting transfers between devices  23.9 us (30%)
  Pallas kernels  12.1 us (15%)
  waiting for transfers between devices  4.65 us (6%)
    all_to_all x2, blocking collectives, exchange(): return lax.all_to_all(parts, axis, 0, 0)  35.1 us
    pallas_call x11, Pallas kernels, call(): pl.pallas_call(kernel, out_shape=[jax.ShapeDtypeStruct(s, F32) for s in o...  12.1 us
    ppermute x4, starting transfers between devices, send(): return lax.ppermute(value, axis, up if forward else [(j, i) for i, j in up])  10.5 us
    ppermute x1, starting transfers between devices, per_device(): on = lax.ppermute(on, 'gx_1', [(0, 1), (1, 0)])  7.8 us
    ppermute x4, waiting for transfers between devices, send(): return lax.ppermute(value, axis, up if forward else [(j, i) for i, j in up])  4.2 us
    all_gather x1, blocking collectives, per_device(): whole = lax.all_gather(half, 'gx_1', axis=0, tiled=True)  3.9 us
    ppermute x1, starting transfers between devices, per_device(): off = lax.ppermute(off, GX, swap)  3.64 us
    ppermute x1, starting transfers between devices, per_device(): early = lax.ppermute(early, GX, swap)  1.92 us
  transfers between devices with their start and end apart: 7, of which 3 were waited for; matrix products, arithmetic and copies ran while one was open for 0% of the time, Pallas kernels for 6%

profile of v10, /device:TPU:1, one launch (start us, length us, event | category | flops | bytes accessed | tf_op | source)
XLA Modules:
  0.0 80.4 jit_solution(8250342468991169524)
XLA Ops:
  0.6 2.0 %shard_map.68 = (f32[60,4,8,128]{3,2,1,0:T(8,128)S(1)}, f32[5,4,8,128]{3,2,1,0:T(8,128)S(1)}, f32[5,8,128]{2,1,0:T(8,128)S(1)}, f32[20,60]{1,0:T(8,128)S(1)}) custom-call(f32[60,4,8,128]{3,2,1,0:T(8,128)} %basis.1, f32[20,60]{1,0:T(8,128)} %bitcast.4, f32[4,8,128]{2,1,0:T(8,128)} %next_vector.1, f32[4,8,128]{2,1,0:T(8,128)} %diag.1, f32[3,4,8,128]{3,2,1,0:T(8,128)} %velocity.1), custom_call_target="tpu_custom_call" | custom-call | flops 100000 | bytes 100000 | tf_op jit(solution)/shard_map/pallas_call | solution.py:48
  2.7 1.3 %collective-permute-start.1 = (f32[5,8,128]{2,1,0:T(8,128)S(1)}, f32[5,8,128]{2,1,0:T(8,128)S(1)}, u32[]{:S(2)}, u32[]{:S(2)}) collective-permute-start(f32[5,8,128]{2,1,0:T(8,128)S(1)} %get-tuple-element.22), channel_id=1, source_target_pairs={{1,0},{2,1},{3,2},{4,3},{5,4},{6,5},{7,6},{9,8},{10,9},{11,10},{12... | collective-permute-start | bytes 61448 | tf_op jit(solution)/shard_map/ppermute | solution.py:650
  4.0 4.6 %collective-permute-start = (f32[5,8,128]{2,1,0:T(8,128)S(1)}, f32[5,8,128]{2,1,0:T(8,128)S(1)}, u32[]{:S(2)}, u32[]{:S(2)}) collective-permute-start(f32[5,8,128]{2,1,0:T(8,128)S(1)} %get-tuple-element.22), channel_id=1, source_target_pairs={{0,1},{1,2},{2,3},{3,4},{4,5},{5,6},{6,7},{8,9},{9,10},{10,11},{11... | collective-permute-start | bytes 61448 | tf_op jit(solution)/shard_map/ppermute | solution.py:650
  8.6 2.7 %shard_map.69.rotated = f32[20,4,8,128]{3,2,1,0:T(8,128)S(1)} custom-call(f32[60,4,8,128]{3,2,1,0:T(8,128)S(1)} %get-tuple-element.19.basis, f32[20,60]{1,0:T(8,128)S(1)} %get-tuple-element.20.schur), custom_call_target="tpu_custom_call" | custom-call | flops 1000000000 | bytes 100000 | tf_op jit(solution)/shard_map/pallas_call | solution.py:48
  11.3 0.0 collective-permute-done.1.from_hi
  11.4 0.0 collective-permute-done.from_lo
  11.4 0.1 shard_map.70
  11.4 3.3 %collective-permute-start.2 = (f32[27,8,128]{2,1,0:T(8,128)S(1)}, f32[27,8,128]{2,1,0:T(8,128)S(1)}, u32[]{:S(2)}, u32[]{:S(2)}) collective-permute-start(f32[27,8,128]{2,1,0:T(8,128)S(1)} %get-tuple-element.24), channel_id=1, source_target_pairs={{0,8},{8,16},{16,24},{1,9},{9,17},{17,25},{2,10},{10,18},{18,26},{... | collective-permute-start | bytes 331784 | tf_op jit(solution)/shard_map/ppermute | solution.py:650
  14.7 1.3 %collective-permute-start.3 = (f32[27,8,128]{2,1,0:T(8,128)S(1)}, f32[27,8,128]{2,1,0:T(8,128)S(1)}, u32[]{:S(2)}, u32[]{:S(2)}) collective-permute-start(f32[27,8,128]{2,1,0:T(8,128)S(1)} %get-tuple-element.25), channel_id=1, source_target_pairs={{8,0},{16,8},{24,16},{9,1},{17,9},{25,17},{10,2},{18,10},{26,18},{... | collective-permute-start | bytes 331784 | tf_op jit(solution)/shard_map/ppermute | solution.py:650
  16.0 0.4 collective-permute-done.2.y_lo
  16.5 3.8 %collective-permute-done.3.y_hi = f32[27,8,128]{2,1,0:T(8,128)S(1)} collective-permute-done((f32[27,8,128]{2,1,0:T(8,128)S(1)}, f32[27,8,128]{2,1,0:T(8,128)S(1)}, u32[]{:S(2)}, u32[]{:S(2)}) %collective-permute-start.3) | collective-permute-done | bytes 110624 | tf_op jit(solution)/shard_map/ppermute | solution.py:650
  20.2 0.1 shard_map.74
  20.3 7.8 %collective-permute-start.6 = (f32[61,8,128]{2,1,0:T(8,128)S(1)}, f32[61,8,128]{2,1,0:T(8,128)S(1)}, u32[]{:S(2)}, u32[]{:S(2)}) collective-permute-start(f32[61,8,128]{2,1,0:T(8,128)S(1)} %get-tuple-element.31), channel_id=1, source_target_pairs={{0,32},{32,0},{1,33},{33,1},{2,34},{34,2},{3,35},{35,3},{4,36},{36... | collective-permute-start | bytes 749576 | tf_op jit(solution)/shard_map/ppermute | solution.py:707
  28.1 1.9 %collective-permute-start.4 = (f32[51,8,128]{2,1,0:T(8,128)S(1)}, f32[51,8,128]{2,1,0:T(8,128)S(1)}, u32[]{:S(2)}, u32[]{:S(2)}) collective-permute-start(f32[51,8,128]{2,1,0:T(8,128)S(1)} %shard_map.73), channel_id=1, source_target_pairs={{32,64},{96,128},{160,192},{224,256},{288,320},{352,384},{416,448}... | collective-permute-start | bytes 626696 | tf_op jit(solution)/shard_map/ppermute | solution.py:696
  30.1 1.2 %shard_map.71 = (f32[8,7,8,128]{3,2,1,0:T(8,128)S(1)}, f32[20,8,8,128]{3,2,1,0:T(8,128)S(1)}) custom-call(f32[20,4,8,128]{3,2,1,0:T(8,128)S(1)} %shard_map.69.rotated, f32[5,4,8,128]{3,2,1,0:T(8,128)S(1)} %get-tuple-element.21.rest, f32[5,8,128]{2,1,0:T(8,128)S(1)} %get-tuple-element.23.halo), custom_call_target="tpu_custom_call" | custom-call | flops 100000 | bytes 100000 | tf_op jit(solution)/shard_map/pallas_call | solution.py:48
  31.2 3.6 %collective-permute-start.5 = (f32[10,8,128]{2,1,0:T(8,128)S(1)}, f32[10,8,128]{2,1,0:T(8,128)S(1)}, u32[]{:S(2)}, u32[]{:S(2)}) collective-permute-start(f32[10,8,128]{2,1,0:T(8,128)S(1)} %get-tuple-element.30), channel_id=1, source_target_pairs={{32,64},{96,128},{160,192},{224,256},{288,320},{352,384},{416,448}... | collective-permute-start | bytes 122888 | tf_op jit(solution)/shard_map/ppermute | solution.py:706
  34.9 1.2 %shard_map.72 = (f32[8,7,8,128]{3,2,1,0:T(8,128)S(1)}, f32[20,14,8,128]{3,2,1,0:T(8,128)S(1)}) custom-call(f32[20,4,8,128]{3,2,1,0:T(8,128)S(1)} %shard_map.69.rotated, f32[5,4,8,128]{3,2,1,0:T(8,128)S(1)} %get-tuple-element.21.rest, f32[5,8,128]{2,1,0:T(8,128)S(1)} %get-tuple-element.23.halo, f32[27,8,128]{2,1,0:T(8,128)S(1)} %collective-permute-done.2.y_lo, ...), custom_call_target="tpu_custom_call" | custom-call | flops 1000000000 | bytes 100000 | tf_op jit(solution)/shard_map/pallas_call | solution.py:48
  36.1 0.5 collective-permute-done.5.off
  36.6 0.0 collective-permute-done.4.early
  36.6 0.0 collective-permute-done.6.on
  36.6 2.3 %shard_map.75 = (f32[2048,128]{1,0:T(8,128)S(1)}, f32[16,1,1280]{2,1,0:T(1,128)S(1)}) custom-call(f32[20,4,8,128]{3,2,1,0:T(8,128)S(1)} %shard_map.69.rotated, f32[5,4,8,128]{3,2,1,0:T(8,128)S(1)} %get-tuple-element.21.rest, f32[5,8,128]{2,1,0:T(8,128)S(1)} %get-tuple-element.23.halo, f32[27,8,128]{2,1,0:T(8,128)S(1)} %collective-permute-done.2.y_lo, ...), custom_call_target="tpu_custom_call" | custom-call | flops 100000 | bytes 100000 | tf_op jit(solution)/shard_map/pallas_call | solution.py:48
  38.8 13.7 %all_to_all.10.parts = f32[16,1,1280]{2,1,0:T(1,128)S(1)} all-to-all(f32[16,1,1280]{2,1,0:T(1,128)S(1)} %get-tuple-element.32), channel_id=1, replica_groups=mesh['gx_0'=8,'gx_1'=2,'gy'=4,'gz'=8] {'gx_1','gz'}, dimensions={0} | all-to-all | bytes 163840 | tf_op jit(solution)/shard_map/all_to_all | solution.py:535
  52.6 21.4 %all_to_all.11.parts = f32[32,1,1280]{2,1,0:T(1,128)S(1)} all-to-all(f32[32,1,1280]{2,1,0:T(1,128)S(1)} %shard_map.76), channel_id=1, replica_groups=mesh['gx_0'=8,'gx_1'=2,'gy'=4,'gz'=8] {'gx_0','gy'}, dimensions={0} | all-to-all | bytes 327680 | tf_op jit(solution)/shard_map/all_to_all | solution.py:535
  74.0 3.9 %all_gather.3.parts = f32[2,1,1280]{2,1,0:T(1,128)S(1)} all-gather(f32[1,1,1280]{2,1,0:T(1,128)S(1)} %shard_map.77), channel_id=1, replica_groups=mesh['gx_0'=8,'gx_1'=2,'gy'=4,'gz'=8] {'gx_1'}, dimensions={0}, use_global_device_ids=true | all-gather | bytes 15360 | tf_op jit(solution)/shard_map/all_gather | solution.py:736
  77.9 2.5 %shard_map.78 = (f32[24,4,8,128]{3,2,1,0:T(8,128)}, f32[3,24]{1,0:T(4,128)}) custom-call(f32[2,1,1280]{2,1,0:T(1,128)S(1)} %all_gather.3.parts, f32[64,4,8,128]{3,2,1,0:T(8,128)S(1)} %bitcast.3), custom_call_target="tpu_custom_call" | custom-call | flops 100000 | bytes 100000 | tf_op jit(solution)/shard_map/pallas_call | solution.py:48
  (3 shorter events, 0.1 us)
Async XLA Ops:
  2.7 8.7 %collective-permute-start.1 = (f32[5,8,128]{2,1,0:T(8,128)S(1)}, f32[5,8,128]{2,1,0:T(8,128)S(1)}, u32[]{:S(2)}, u32[]{:S(2)}) collective-permute-start(f32[5,8,128]{2,1,0:T(8,128)S(1)} %get-tuple-element.22), channel_id=1, source_target_pairs={{1,0},{2,1},{3,2},{4,3},{5,4},{6,5},{7,6},{9,8},{10,9},{11,10},{12... | collective-permute-start | bytes 61448 | tf_op jit(solution)/shard_map/ppermute | solution.py:650
  4.0 7.4 %collective-permute-start = (f32[5,8,128]{2,1,0:T(8,128)S(1)}, f32[5,8,128]{2,1,0:T(8,128)S(1)}, u32[]{:S(2)}, u32[]{:S(2)}) collective-permute-start(f32[5,8,128]{2,1,0:T(8,128)S(1)} %get-tuple-element.22), channel_id=1, source_target_pairs={{0,1},{1,2},{2,3},{3,4},{4,5},{5,6},{6,7},{8,9},{9,10},{10,11},{11... | collective-permute-start | bytes 61448 | tf_op jit(solution)/shard_map/ppermute | solution.py:650
  11.4 5.0 %collective-permute-start.2 = (f32[27,8,128]{2,1,0:T(8,128)S(1)}, f32[27,8,128]{2,1,0:T(8,128)S(1)}, u32[]{:S(2)}, u32[]{:S(2)}) collective-permute-start(f32[27,8,128]{2,1,0:T(8,128)S(1)} %get-tuple-element.24), channel_id=1, source_target_pairs={{0,8},{8,16},{16,24},{1,9},{9,17},{17,25},{2,10},{10,18},{18,26},{... | collective-permute-start | bytes 331784 | tf_op jit(solution)/shard_map/ppermute | solution.py:650
  14.7 5.5 %collective-permute-start.3 = (f32[27,8,128]{2,1,0:T(8,128)S(1)}, f32[27,8,128]{2,1,0:T(8,128)S(1)}, u32[]{:S(2)}, u32[]{:S(2)}) collective-permute-start(f32[27,8,128]{2,1,0:T(8,128)S(1)} %get-tuple-element.25), channel_id=1, source_target_pairs={{8,0},{16,8},{24,16},{9,1},{17,9},{25,17},{10,2},{18,10},{26,18},{... | collective-permute-start | bytes 331784 | tf_op jit(solution)/shard_map/ppermute | solution.py:650
  20.3 16.3 %collective-permute-start.6 = (f32[61,8,128]{2,1,0:T(8,128)S(1)}, f32[61,8,128]{2,1,0:T(8,128)S(1)}, u32[]{:S(2)}, u32[]{:S(2)}) collective-permute-start(f32[61,8,128]{2,1,0:T(8,128)S(1)} %get-tuple-element.31), channel_id=1, source_target_pairs={{0,32},{32,0},{1,33},{33,1},{2,34},{34,2},{3,35},{35,3},{4,36},{36... | collective-permute-start | bytes 749576 | tf_op jit(solution)/shard_map/ppermute | solution.py:707
  28.1 8.4 %collective-permute-start.4 = (f32[51,8,128]{2,1,0:T(8,128)S(1)}, f32[51,8,128]{2,1,0:T(8,128)S(1)}, u32[]{:S(2)}, u32[]{:S(2)}) collective-permute-start(f32[51,8,128]{2,1,0:T(8,128)S(1)} %shard_map.73), channel_id=1, source_target_pairs={{32,64},{96,128},{160,192},{224,256},{288,320},{352,384},{416,448}... | collective-permute-start | bytes 626696 | tf_op jit(solution)/shard_map/ppermute | solution.py:696
  31.2 5.3 %collective-permute-start.5 = (f32[10,8,128]{2,1,0:T(8,128)S(1)}, f32[10,8,128]{2,1,0:T(8,128)S(1)}, u32[]{:S(2)}, u32[]{:S(2)}) collective-permute-start(f32[10,8,128]{2,1,0:T(8,128)S(1)} %get-tuple-element.30), channel_id=1, source_target_pairs={{32,64},{96,128},{160,192},{224,256},{288,320},{352,384},{416,448}... | collective-permute-start | bytes 122888 | tf_op jit(solution)/shard_map/ppermute | solution.py:706

commit v11 on v10

--- a/solution.py
+++ b/solution.py
@@ -15,7 +15,7 @@
 SPAN = 64
 SIGMA = 7.125
 PLANES = 51
-WIRE = 1280
+WIRE = 1152
 GX = ("gx_0", "gx_1")
 X, Y, Z = (4, 8, 128)
 TILE = (Y, Z)
@@ -365,7 +365,7 @@
             partial[f, at] = apply(get, key, coef, skip_of(key), with_y=False)
         return carry
 
-    lax.fori_loop(0, KEEP, body, 0, unroll=4)
+    lax.fori_loop(0, KEEP, body, 0, unroll=5)
 
 
 def inner_kernel(
@@ -394,7 +394,7 @@
             partial[f, len(ONCE) + x - 1] = apply(once.__getitem__, (x, 0, 0), coef, skip)
         return carry
 
-    lax.fori_loop(0, KEEP, body, 0, unroll=4)
+    lax.fori_loop(0, KEEP, body, 0, unroll=5)
 
 
 def inner(a, b):
@@ -503,24 +503,28 @@
     square = jnp.concatenate([square, jnp.zeros((Z - SPAN, Z), F32)], axis=0)
     total = even + (mixed + square.T[:SPAN, :SPAN])
     wide = jnp.concatenate([total, jnp.zeros((SPAN, Z - SPAN), F32)], axis=1)
-    lane = lax.broadcasted_iota(jnp.int32, (16, Z), 1)
-    main = jnp.where(
-        lane < 64,
-        wide[:16],
-        jnp.where(lane < 112, pltpu.roll(wide[16:32], 48, 1), pltpu.roll(wide[48:], 64, 1)),
-    )
     lane = lanes_of()
+    tiles = []
+    for pieces in PIECES:
+        tile = jnp.zeros(TILE, F32)
+        for i, at in pieces:
+            moved = wide[Y * i : Y * (i + 1)]
+            moved = shift_lanes(moved, (at - Y * i) % Z) if at != Y * i else moved
+            tile = jnp.where((lane >= at) & (lane < at + SPAN - Y * i), moved, tile)
+        tiles.append(tile)
     extra = jnp.zeros(TILE, F32)
     for g in range(4):
-        tile = shift_rows(wide[32 + 8 * (g // 2) : 40 + 8 * (g // 2)], -4 * (g % 2))
-        tile = tile if g == 1 else shift_lanes(tile, (32 * g - 32) % Z)
+        tile = shift_rows(wide[32:40], -2 * g)
+        tile = shift_lanes(tile, (32 * g - 32) % Z) if g != 1 else tile
         extra = jnp.where((lane >= 32 * g) & (lane < 32 * g + 32), tile, extra)
     for i in range(copies):
         c = i // (copies // 2)
-        for k in range(8):
-            gram[i, :, Z * k : Z * (k + 1)] = main[8 * c + k : 8 * c + k + 1]
-        for k in range(2):
-            gram[i, :, Z * (8 + k) : Z * (9 + k)] = extra[2 * c + k : 2 * c + k + 1]
+        for k in range(Y):
+            gram[i, :, Z * k : Z * (k + 1)] = tiles[c][k : k + 1]
+        gram[i, :, Z * Y :] = extra[c : c + 1]
+
+
+PIECES = (((0, 0), (1, 64), (7, 120)), ((2, 0), (3, 48), (5, 88), (6, 112)))
 
 
 def sum_kernel(copies, parts, out):
@@ -544,37 +548,27 @@
         pltpu.make_async_copy(fresh.at[k], basis.at[KEEP + k], sems.at[1 + k])
         for k in range(ROWS - KEEP)
     ]
-    row = lax.broadcasted_iota(jnp.int32, (16, Z), 0)
-    lane = lax.broadcasted_iota(jnp.int32, (16, Z), 1)
-    main = jnp.zeros((16, Z), F32)
+    row, lane = rows_of(), lanes_of()
+    rows = [None] * 8
     extra = jnp.zeros(TILE, F32)
     for c in range(2):
-        for k in range(8):
-            main = jnp.where(row == 8 * c + k, parts[c, :, Z * k : Z * (k + 1)], main)
-        for k in range(2):
-            here = rows_of() == 2 * c + k
-            extra = jnp.where(here, parts[c, :, Z * (8 + k) : Z * (9 + k)], extra)
-    main, extra = main * (1.0 / cell_count), extra * (1.0 / cell_count)
-    upper = []
-    for g in (0, 2):
-        tile = jnp.where(
-            rows_of() < 4,
-            shift_lanes(extra, (32 - 32 * g) % Z),
-            shift_lanes(shift_rows(extra, 4), -32 * g % Z) if g else shift_rows(extra, 4),
-        )
-        upper.append(jnp.where((lanes_of() >= 32) & (lanes_of() < SPAN), tile, 0.0))
-    blocks = jnp.concatenate(
-        [
-            jnp.where(lane < SPAN, main, 0.0),
-            jnp.where((lane >= 16) & (lane < SPAN), pltpu.roll(main, Z - 48, 1), 0.0),
-            *upper,
-            jnp.where((lane >= 48) & (lane < SPAN), pltpu.roll(main, 64, 1), 0.0),
-            jnp.zeros((Z - SPAN, Z), F32),
-        ],
-        axis=0,
-    )
-    across = lax.broadcasted_iota(jnp.int32, (Z, Z), 1) // 16
-    down = lax.broadcasted_iota(jnp.int32, (Z, Z), 0) // 16
+        tile = jnp.zeros(TILE, F32)
+        for k in range(Y):
+            tile = jnp.where(row == k, parts[c, :, Z * k : Z * (k + 1)], tile)
+        tile = tile * (1.0 / cell_count)
+        for i, at in PIECES[c]:
+            moved = shift_lanes(tile, (Y * i - at) % Z) if at != Y * i else tile
+            rows[i] = jnp.where((lane >= Y * i) & (lane < SPAN), moved, 0.0)
+        extra = jnp.where(row == c, parts[c, :, Z * Y :], extra)
+    extra = extra * (1.0 / cell_count)
+    tile = jnp.zeros(TILE, F32)
+    for g in range(4):
+        moved = shift_lanes(extra, (32 - 32 * g) % Z) if g != 1 else extra
+        tile = jnp.where((row >= 2 * g) & (row < 2 * g + 2), shift_rows(moved, 2 * g), tile)
+    rows[4] = jnp.where((lane >= 32) & (lane < SPAN), tile, 0.0)
+    blocks = jnp.concatenate([*rows, jnp.zeros((Z - SPAN, Z), F32)], axis=0)
+    across = lax.broadcasted_iota(jnp.int32, (Z, Z), 1) // Y
+    down = lax.broadcasted_iota(jnp.int32, (Z, Z), 0) // Y
     gram = (blocks + jnp.where(across < down, blocks.T, 0.0))[:SPAN]
     row64 = lax.broadcasted_iota(jnp.int32, (SPAN, Z), 0)
     lane64 = lax.broadcasted_iota(jnp.int32, (SPAN, Z), 1)

time: 80.8 us -> 80.5 us (level)
  no operation moved by 1% of the time
where the time goes in v11:
time: 80.5 us; the launch traced here: 80 us
  blocking collectives  38.7 us (48%)
  starting transfers between devices  23.9 us (30%)
  Pallas kernels  11.9 us (15%)
  waiting for transfers between devices  4.77 us (6%)
    all_to_all x2, blocking collectives, exchange(): return lax.all_to_all(parts, axis, 0, 0)  34.9 us
    pallas_call x11, Pallas kernels, call(): pl.pallas_call(kernel, out_shape=[jax.ShapeDtypeStruct(s, F32) for s in o...  11.9 us
    ppermute x4, starting transfers between devices, send(): return lax.ppermute(value, axis, up if forward else [(j, i) for i, j in up])  10.5 us
    ppermute x1, starting transfers between devices, per_device(): on = lax.ppermute(on, 'gx_1', [(0, 1), (1, 0)])  7.8 us
    ppermute x4, waiting for transfers between devices, send(): return lax.ppermute(value, axis, up if forward else [(j, i) for i, j in up])  4.2 us
    all_gather x1, blocking collectives, per_device(): whole = lax.all_gather(half, 'gx_1', axis=0, tiled=True)  3.84 us
    ppermute x1, starting transfers between devices, per_device(): off = lax.ppermute(off, GX, swap)  3.64 us
    ppermute x1, starting transfers between devices, per_device(): early = lax.ppermute(early, GX, swap)  1.92 us
  transfers between devices with their start and end apart: 7, of which 3 were waited for; matrix products, arithmetic and copies ran while one was open for 0% of the time, Pallas kernels for 6%

profile of v11, /device:TPU:1, one launch (start us, length us, event | category | flops | bytes accessed | tf_op | source)
XLA Modules:
  0.0 80.0 jit_solution(13936306957891657203)
XLA Ops:
  0.6 2.0 %shard_map.68 = (f32[60,4,8,128]{3,2,1,0:T(8,128)S(1)}, f32[5,4,8,128]{3,2,1,0:T(8,128)S(1)}, f32[5,8,128]{2,1,0:T(8,128)S(1)}, f32[20,60]{1,0:T(8,128)S(1)}) custom-call(f32[60,4,8,128]{3,2,1,0:T(8,128)} %basis.1, f32[20,60]{1,0:T(8,128)} %bitcast.4, f32[4,8,128]{2,1,0:T(8,128)} %next_vector.1, f32[4,8,128]{2,1,0:T(8,128)} %diag.1, f32[3,4,8,128]{3,2,1,0:T(8,128)} %velocity.1), custom_call_target="tpu_custom_call" | custom-call | flops 100000 | bytes 100000 | tf_op jit(solution)/shard_map/pallas_call | solution.py:48
  2.7 1.3 %collective-permute-start.1 = (f32[5,8,128]{2,1,0:T(8,128)S(1)}, f32[5,8,128]{2,1,0:T(8,128)S(1)}, u32[]{:S(2)}, u32[]{:S(2)}) collective-permute-start(f32[5,8,128]{2,1,0:T(8,128)S(1)} %get-tuple-element.22), channel_id=1, source_target_pairs={{1,0},{2,1},{3,2},{4,3},{5,4},{6,5},{7,6},{9,8},{10,9},{11,10},{12... | collective-permute-start | bytes 61448 | tf_op jit(solution)/shard_map/ppermute | solution.py:644
  4.0 4.6 %collective-permute-start = (f32[5,8,128]{2,1,0:T(8,128)S(1)}, f32[5,8,128]{2,1,0:T(8,128)S(1)}, u32[]{:S(2)}, u32[]{:S(2)}) collective-permute-start(f32[5,8,128]{2,1,0:T(8,128)S(1)} %get-tuple-element.22), channel_id=1, source_target_pairs={{0,1},{1,2},{2,3},{3,4},{4,5},{5,6},{6,7},{8,9},{9,10},{10,11},{11... | collective-permute-start | bytes 61448 | tf_op jit(solution)/shard_map/ppermute | solution.py:644
  8.6 2.7 %shard_map.69.rotated = f32[20,4,8,128]{3,2,1,0:T(8,128)S(1)} custom-call(f32[60,4,8,128]{3,2,1,0:T(8,128)S(1)} %get-tuple-element.19.basis, f32[20,60]{1,0:T(8,128)S(1)} %get-tuple-element.20.schur), custom_call_target="tpu_custom_call" | custom-call | flops 1000000000 | bytes 100000 | tf_op jit(solution)/shard_map/pallas_call | solution.py:48
  11.3 0.0 collective-permute-done.1.from_hi
  11.4 0.0 collective-permute-done.from_lo
  11.4 0.1 shard_map.70
  11.4 3.3 %collective-permute-start.2 = (f32[27,8,128]{2,1,0:T(8,128)S(1)}, f32[27,8,128]{2,1,0:T(8,128)S(1)}, u32[]{:S(2)}, u32[]{:S(2)}) collective-permute-start(f32[27,8,128]{2,1,0:T(8,128)S(1)} %get-tuple-element.24), channel_id=1, source_target_pairs={{0,8},{8,16},{16,24},{1,9},{9,17},{17,25},{2,10},{10,18},{18,26},{... | collective-permute-start | bytes 331784 | tf_op jit(solution)/shard_map/ppermute | solution.py:644
  14.7 1.3 %collective-permute-start.3 = (f32[27,8,128]{2,1,0:T(8,128)S(1)}, f32[27,8,128]{2,1,0:T(8,128)S(1)}, u32[]{:S(2)}, u32[]{:S(2)}) collective-permute-start(f32[27,8,128]{2,1,0:T(8,128)S(1)} %get-tuple-element.25), channel_id=1, source_target_pairs={{8,0},{16,8},{24,16},{9,1},{17,9},{25,17},{10,2},{18,10},{26,18},{... | collective-permute-start | bytes 331784 | tf_op jit(solution)/shard_map/ppermute | solution.py:644
  16.0 0.4 collective-permute-done.2.y_lo
  16.5 3.8 %collective-permute-done.3.y_hi = f32[27,8,128]{2,1,0:T(8,128)S(1)} collective-permute-done((f32[27,8,128]{2,1,0:T(8,128)S(1)}, f32[27,8,128]{2,1,0:T(8,128)S(1)}, u32[]{:S(2)}, u32[]{:S(2)}) %collective-permute-start.3) | collective-permute-done | bytes 110624 | tf_op jit(solution)/shard_map/ppermute | solution.py:644
  20.2 0.1 shard_map.74
  20.3 7.8 %collective-permute-start.6 = (f32[61,8,128]{2,1,0:T(8,128)S(1)}, f32[61,8,128]{2,1,0:T(8,128)S(1)}, u32[]{:S(2)}, u32[]{:S(2)}) collective-permute-start(f32[61,8,128]{2,1,0:T(8,128)S(1)} %get-tuple-element.31), channel_id=1, source_target_pairs={{0,32},{32,0},{1,33},{33,1},{2,34},{34,2},{3,35},{35,3},{4,36},{36... | collective-permute-start | bytes 749576 | tf_op jit(solution)/shard_map/ppermute | solution.py:701
  28.1 1.9 %collective-permute-start.4 = (f32[51,8,128]{2,1,0:T(8,128)S(1)}, f32[51,8,128]{2,1,0:T(8,128)S(1)}, u32[]{:S(2)}, u32[]{:S(2)}) collective-permute-start(f32[51,8,128]{2,1,0:T(8,128)S(1)} %shard_map.73), channel_id=1, source_target_pairs={{32,64},{96,128},{160,192},{224,256},{288,320},{352,384},{416,448}... | collective-permute-start | bytes 626696 | tf_op jit(solution)/shard_map/ppermute | solution.py:690
  30.1 1.1 %shard_map.71 = (f32[8,7,8,128]{3,2,1,0:T(8,128)S(1)}, f32[20,8,8,128]{3,2,1,0:T(8,128)S(1)}) custom-call(f32[20,4,8,128]{3,2,1,0:T(8,128)S(1)} %shard_map.69.rotated, f32[5,4,8,128]{3,2,1,0:T(8,128)S(1)} %get-tuple-element.21.rest, f32[5,8,128]{2,1,0:T(8,128)S(1)} %get-tuple-element.23.halo), custom_call_target="tpu_custom_call" | custom-call | flops 100000 | bytes 100000 | tf_op jit(solution)/shard_map/pallas_call | solution.py:48
  31.1 3.6 %collective-permute-start.5 = (f32[10,8,128]{2,1,0:T(8,128)S(1)}, f32[10,8,128]{2,1,0:T(8,128)S(1)}, u32[]{:S(2)}, u32[]{:S(2)}) collective-permute-start(f32[10,8,128]{2,1,0:T(8,128)S(1)} %get-tuple-element.30), channel_id=1, source_target_pairs={{32,64},{96,128},{160,192},{224,256},{288,320},{352,384},{416,448}... | collective-permute-start | bytes 122888 | tf_op jit(solution)/shard_map/ppermute | solution.py:700
  34.8 1.1 %shard_map.72 = (f32[8,7,8,128]{3,2,1,0:T(8,128)S(1)}, f32[20,14,8,128]{3,2,1,0:T(8,128)S(1)}) custom-call(f32[20,4,8,128]{3,2,1,0:T(8,128)S(1)} %shard_map.69.rotated, f32[5,4,8,128]{3,2,1,0:T(8,128)S(1)} %get-tuple-element.21.rest, f32[5,8,128]{2,1,0:T(8,128)S(1)} %get-tuple-element.23.halo, f32[27,8,128]{2,1,0:T(8,128)S(1)} %collective-permute-done.2.y_lo, ...), custom_call_target="tpu_custom_call" | custom-call | flops 1000000000 | bytes 100000 | tf_op jit(solution)/shard_map/pallas_call | solution.py:48
  35.9 0.6 collective-permute-done.5.off
  36.5 0.0 collective-permute-done.4.early
  36.5 0.0 collective-permute-done.6.on
  36.5 2.3 %shard_map.75 = (f32[2048,128]{1,0:T(8,128)S(1)}, f32[16,1,1152]{2,1,0:T(1,128)S(1)}) custom-call(f32[20,4,8,128]{3,2,1,0:T(8,128)S(1)} %shard_map.69.rotated, f32[5,4,8,128]{3,2,1,0:T(8,128)S(1)} %get-tuple-element.21.rest, f32[5,8,128]{2,1,0:T(8,128)S(1)} %get-tuple-element.23.halo, f32[27,8,128]{2,1,0:T(8,128)S(1)} %collective-permute-done.2.y_lo, ...), custom_call_target="tpu_custom_call" | custom-call | flops 100000 | bytes 100000 | tf_op jit(solution)/shard_map/pallas_call | solution.py:48
  38.7 13.6 %all_to_all.10.parts = f32[16,1,1152]{2,1,0:T(1,128)S(1)} all-to-all(f32[16,1,1152]{2,1,0:T(1,128)S(1)} %get-tuple-element.32), channel_id=1, replica_groups=mesh['gx_0'=8,'gx_1'=2,'gy'=4,'gz'=8] {'gx_1','gz'}, dimensions={0} | all-to-all | bytes 147456 | tf_op jit(solution)/shard_map/all_to_all | solution.py:539
  52.4 21.2 %all_to_all.11.parts = f32[32,1,1152]{2,1,0:T(1,128)S(1)} all-to-all(f32[32,1,1152]{2,1,0:T(1,128)S(1)} %shard_map.76), channel_id=1, replica_groups=mesh['gx_0'=8,'gx_1'=2,'gy'=4,'gz'=8] {'gx_0','gy'}, dimensions={0} | all-to-all | bytes 294912 | tf_op jit(solution)/shard_map/all_to_all | solution.py:539
  73.7 3.8 %all_gather.3.parts = f32[2,1,1152]{2,1,0:T(1,128)S(1)} all-gather(f32[1,1,1152]{2,1,0:T(1,128)S(1)} %shard_map.77), channel_id=1, replica_groups=mesh['gx_0'=8,'gx_1'=2,'gy'=4,'gz'=8] {'gx_1'}, dimensions={0}, use_global_device_ids=true | all-gather | bytes 13824 | tf_op jit(solution)/shard_map/all_gather | solution.py:730
  77.5 2.5 %shard_map.78 = (f32[24,4,8,128]{3,2,1,0:T(8,128)}, f32[3,24]{1,0:T(4,128)}) custom-call(f32[2,1,1152]{2,1,0:T(1,128)S(1)} %all_gather.3.parts, f32[64,4,8,128]{3,2,1,0:T(8,128)S(1)} %bitcast.3), custom_call_target="tpu_custom_call" | custom-call | flops 100000 | bytes 100000 | tf_op jit(solution)/shard_map/pallas_call | solution.py:48
  (3 shorter events, 0.1 us)
Async XLA Ops:
  2.7 8.7 %collective-permute-start.1 = (f32[5,8,128]{2,1,0:T(8,128)S(1)}, f32[5,8,128]{2,1,0:T(8,128)S(1)}, u32[]{:S(2)}, u32[]{:S(2)}) collective-permute-start(f32[5,8,128]{2,1,0:T(8,128)S(1)} %get-tuple-element.22), channel_id=1, source_target_pairs={{1,0},{2,1},{3,2},{4,3},{5,4},{6,5},{7,6},{9,8},{10,9},{11,10},{12... | collective-permute-start | bytes 61448 | tf_op jit(solution)/shard_map/ppermute | solution.py:644
  4.0 7.4 %collective-permute-start = (f32[5,8,128]{2,1,0:T(8,128)S(1)}, f32[5,8,128]{2,1,0:T(8,128)S(1)}, u32[]{:S(2)}, u32[]{:S(2)}) collective-permute-start(f32[5,8,128]{2,1,0:T(8,128)S(1)} %get-tuple-element.22), channel_id=1, source_target_pairs={{0,1},{1,2},{2,3},{3,4},{4,5},{5,6},{6,7},{8,9},{9,10},{10,11},{11... | collective-permute-start | bytes 61448 | tf_op jit(solution)/shard_map/ppermute | solution.py:644
  11.4 5.0 %collective-permute-start.2 = (f32[27,8,128]{2,1,0:T(8,128)S(1)}, f32[27,8,128]{2,1,0:T(8,128)S(1)}, u32[]{:S(2)}, u32[]{:S(2)}) collective-permute-start(f32[27,8,128]{2,1,0:T(8,128)S(1)} %get-tuple-element.24), channel_id=1, source_target_pairs={{0,8},{8,16},{16,24},{1,9},{9,17},{17,25},{2,10},{10,18},{18,26},{... | collective-permute-start | bytes 331784 | tf_op jit(solution)/shard_map/ppermute | solution.py:644
  14.7 5.5 %collective-permute-start.3 = (f32[27,8,128]{2,1,0:T(8,128)S(1)}, f32[27,8,128]{2,1,0:T(8,128)S(1)}, u32[]{:S(2)}, u32[]{:S(2)}) collective-permute-start(f32[27,8,128]{2,1,0:T(8,128)S(1)} %get-tuple-element.25), channel_id=1, source_target_pairs={{8,0},{16,8},{24,16},{9,1},{17,9},{25,17},{10,2},{18,10},{26,18},{... | collective-permute-start | bytes 331784 | tf_op jit(solution)/shard_map/ppermute | solution.py:644
  20.3 16.2 %collective-permute-start.6 = (f32[61,8,128]{2,1,0:T(8,128)S(1)}, f32[61,8,128]{2,1,0:T(8,128)S(1)}, u32[]{:S(2)}, u32[]{:S(2)}) collective-permute-start(f32[61,8,128]{2,1,0:T(8,128)S(1)} %get-tuple-element.31), channel_id=1, source_target_pairs={{0,32},{32,0},{1,33},{33,1},{2,34},{34,2},{3,35},{35,3},{4,36},{36... | collective-permute-start | bytes 749576 | tf_op jit(solution)/shard_map/ppermute | solution.py:701
  28.1 8.3 %collective-permute-start.4 = (f32[51,8,128]{2,1,0:T(8,128)S(1)}, f32[51,8,128]{2,1,0:T(8,128)S(1)}, u32[]{:S(2)}, u32[]{:S(2)}) collective-permute-start(f32[51,8,128]{2,1,0:T(8,128)S(1)} %shard_map.73), channel_id=1, source_target_pairs={{32,64},{96,128},{160,192},{224,256},{288,320},{352,384},{416,448}... | collective-permute-start | bytes 626696 | tf_op jit(solution)/shard_map/ppermute | solution.py:690
  31.1 5.3 %collective-permute-start.5 = (f32[10,8,128]{2,1,0:T(8,128)S(1)}, f32[10,8,128]{2,1,0:T(8,128)S(1)}, u32[]{:S(2)}, u32[]{:S(2)}) collective-permute-start(f32[10,8,128]{2,1,0:T(8,128)S(1)} %get-tuple-element.30), channel_id=1, source_target_pairs={{32,64},{96,128},{160,192},{224,256},{288,320},{352,384},{416,448}... | collective-permute-start | bytes 122888 | tf_op jit(solution)/shard_map/ppermute | solution.py:700

commit v12 on v11

--- a/solution.py
+++ b/solution.py
@@ -56,7 +56,7 @@
     )(*args)
 
 
-CHUNK = 10
+CHUNK = 20
 
 
 def edge_kernel(
@@ -343,8 +343,8 @@
 
 
 INNER = [key for key in COEF if 0 <= key[0] < X]
-LEVEL = [key for key in INNER if not key[1]]
-BESIDE = [key for key in INNER if key[1]]
+LEVEL = [key for key in INNER if not key[1] and not key[2]]
+BESIDE = [key for key in INNER if key[1] or key[2]]
 OUTER = [key for key in COEF if not 0 <= key[0] < X]
 ONCE = [key for key in region(1) if 0 <= key[0] < X]
 SIDES = {0: (2, -1), X - 1: (1, X)}

time: 80.5 us -> 80.1 us (level)
  no operation moved by 1% of the time
where the time goes in v12:
time: 80.1 us; the launch traced here: 79.6 us
  blocking collectives  38.7 us (48%)
  starting transfers between devices  23.9 us (30%)
  Pallas kernels  11.9 us (15%)
  waiting for transfers between devices  4.39 us (5%)
    all_to_all x2, blocking collectives, exchange(): return lax.all_to_all(parts, axis, 0, 0)  34.9 us
    pallas_call x11, Pallas kernels, call(): pl.pallas_call(kernel, out_shape=[jax.ShapeDtypeStruct(s, F32) for s in o...  11.9 us
    ppermute x4, starting transfers between devices, send(): return lax.ppermute(value, axis, up if forward else [(j, i) for i, j in up])  10.5 us
    ppermute x1, starting transfers between devices, per_device(): on = lax.ppermute(on, 'gx_1', [(0, 1), (1, 0)])  7.8 us
    ppermute x4, waiting for transfers between devices, send(): return lax.ppermute(value, axis, up if forward else [(j, i) for i, j in up])  4.2 us
    all_gather x1, blocking collectives, per_device(): whole = lax.all_gather(half, 'gx_1', axis=0, tiled=True)  3.84 us
    ppermute x1, starting transfers between devices, per_device(): off = lax.ppermute(off, GX, swap)  3.64 us
    ppermute x1, starting transfers between devices, per_device(): early = lax.ppermute(early, GX, swap)  1.92 us
  transfers between devices with their start and end apart: 7, of which 3 were waited for; matrix products, arithmetic and copies ran while one was open for 0% of the time, Pallas kernels for 6%

profile of v12, /device:TPU:1, one launch (start us, length us, event | category | flops | bytes accessed | tf_op | source)
XLA Modules:
  0.0 79.6 jit_solution(5932928894285360612)
XLA Ops:
  0.6 1.9 %shard_map.68 = (f32[60,4,8,128]{3,2,1,0:T(8,128)S(1)}, f32[5,4,8,128]{3,2,1,0:T(8,128)S(1)}, f32[5,8,128]{2,1,0:T(8,128)S(1)}, f32[20,60]{1,0:T(8,128)S(1)}) custom-call(f32[60,4,8,128]{3,2,1,0:T(8,128)} %basis.1, f32[20,60]{1,0:T(8,128)} %bitcast.4, f32[4,8,128]{2,1,0:T(8,128)} %next_vector.1, f32[4,8,128]{2,1,0:T(8,128)} %diag.1, f32[3,4,8,128]{3,2,1,0:T(8,128)} %velocity.1), custom_call_target="tpu_custom_call" | custom-call | flops 100000 | bytes 100000 | tf_op jit(solution)/shard_map/pallas_call | solution.py:48
  2.5 1.3 %collective-permute-start.1 = (f32[5,8,128]{2,1,0:T(8,128)S(1)}, f32[5,8,128]{2,1,0:T(8,128)S(1)}, u32[]{:S(2)}, u32[]{:S(2)}) collective-permute-start(f32[5,8,128]{2,1,0:T(8,128)S(1)} %get-tuple-element.22), channel_id=1, source_target_pairs={{1,0},{2,1},{3,2},{4,3},{5,4},{6,5},{7,6},{9,8},{10,9},{11,10},{12... | collective-permute-start | bytes 61448 | tf_op jit(solution)/shard_map/ppermute | solution.py:644
  3.8 4.6 %collective-permute-start = (f32[5,8,128]{2,1,0:T(8,128)S(1)}, f32[5,8,128]{2,1,0:T(8,128)S(1)}, u32[]{:S(2)}, u32[]{:S(2)}) collective-permute-start(f32[5,8,128]{2,1,0:T(8,128)S(1)} %get-tuple-element.22), channel_id=1, source_target_pairs={{0,1},{1,2},{2,3},{3,4},{4,5},{5,6},{6,7},{8,9},{9,10},{10,11},{11... | collective-permute-start | bytes 61448 | tf_op jit(solution)/shard_map/ppermute | solution.py:644
  8.5 2.7 %shard_map.69.rotated = f32[20,4,8,128]{3,2,1,0:T(8,128)S(1)} custom-call(f32[60,4,8,128]{3,2,1,0:T(8,128)S(1)} %get-tuple-element.19.basis, f32[20,60]{1,0:T(8,128)S(1)} %get-tuple-element.20.schur), custom_call_target="tpu_custom_call" | custom-call | flops 1000000000 | bytes 100000 | tf_op jit(solution)/shard_map/pallas_call | solution.py:48
  11.2 0.0 collective-permute-done.1.from_hi
  11.2 0.0 collective-permute-done.from_lo
  11.2 0.1 shard_map.70
  11.3 3.3 %collective-permute-start.2 = (f32[27,8,128]{2,1,0:T(8,128)S(1)}, f32[27,8,128]{2,1,0:T(8,128)S(1)}, u32[]{:S(2)}, u32[]{:S(2)}) collective-permute-start(f32[27,8,128]{2,1,0:T(8,128)S(1)} %get-tuple-element.24), channel_id=1, source_target_pairs={{0,8},{8,16},{16,24},{1,9},{9,17},{17,25},{2,10},{10,18},{18,26},{... | collective-permute-start | bytes 331784 | tf_op jit(solution)/shard_map/ppermute | solution.py:644
  14.6 1.3 %collective-permute-start.3 = (f32[27,8,128]{2,1,0:T(8,128)S(1)}, f32[27,8,128]{2,1,0:T(8,128)S(1)}, u32[]{:S(2)}, u32[]{:S(2)}) collective-permute-start(f32[27,8,128]{2,1,0:T(8,128)S(1)} %get-tuple-element.25), channel_id=1, source_target_pairs={{8,0},{16,8},{24,16},{9,1},{17,9},{25,17},{10,2},{18,10},{26,18},{... | collective-permute-start | bytes 331784 | tf_op jit(solution)/shard_map/ppermute | solution.py:644
  15.9 0.4 collective-permute-done.2.y_lo
  16.3 3.8 %collective-permute-done.3.y_hi = f32[27,8,128]{2,1,0:T(8,128)S(1)} collective-permute-done((f32[27,8,128]{2,1,0:T(8,128)S(1)}, f32[27,8,128]{2,1,0:T(8,128)S(1)}, u32[]{:S(2)}, u32[]{:S(2)}) %collective-permute-start.3) | collective-permute-done | bytes 110624 | tf_op jit(solution)/shard_map/ppermute | solution.py:644
  20.1 0.1 shard_map.74
  20.1 7.8 %collective-permute-start.6 = (f32[61,8,128]{2,1,0:T(8,128)S(1)}, f32[61,8,128]{2,1,0:T(8,128)S(1)}, u32[]{:S(2)}, u32[]{:S(2)}) collective-permute-start(f32[61,8,128]{2,1,0:T(8,128)S(1)} %get-tuple-element.31), channel_id=1, source_target_pairs={{0,32},{32,0},{1,33},{33,1},{2,34},{34,2},{3,35},{35,3},{4,36},{36... | collective-permute-start | bytes 749576 | tf_op jit(solution)/shard_map/ppermute | solution.py:701
  28.0 1.9 %collective-permute-start.4 = (f32[51,8,128]{2,1,0:T(8,128)S(1)}, f32[51,8,128]{2,1,0:T(8,128)S(1)}, u32[]{:S(2)}, u32[]{:S(2)}) collective-permute-start(f32[51,8,128]{2,1,0:T(8,128)S(1)} %shard_map.73), channel_id=1, source_target_pairs={{32,64},{96,128},{160,192},{224,256},{288,320},{352,384},{416,448}... | collective-permute-start | bytes 626696 | tf_op jit(solution)/shard_map/ppermute | solution.py:690
  29.9 0.8 %shard_map.71 = (f32[4,7,8,128]{3,2,1,0:T(8,128)S(1)}, f32[20,4,8,128]{3,2,1,0:T(8,128)S(1)}) custom-call(f32[20,4,8,128]{3,2,1,0:T(8,128)S(1)} %shard_map.69.rotated, f32[5,4,8,128]{3,2,1,0:T(8,128)S(1)} %get-tuple-element.21.rest, f32[5,8,128]{2,1,0:T(8,128)S(1)} %get-tuple-element.23.halo), custom_call_target="tpu_custom_call" | custom-call | flops 100000 | bytes 100000 | tf_op jit(solution)/shard_map/pallas_call | solution.py:48
  30.7 3.6 %collective-permute-start.5 = (f32[10,8,128]{2,1,0:T(8,128)S(1)}, f32[10,8,128]{2,1,0:T(8,128)S(1)}, u32[]{:S(2)}, u32[]{:S(2)}) collective-permute-start(f32[10,8,128]{2,1,0:T(8,128)S(1)} %get-tuple-element.30), channel_id=1, source_target_pairs={{32,64},{96,128},{160,192},{224,256},{288,320},{352,384},{416,448}... | collective-permute-start | bytes 122888 | tf_op jit(solution)/shard_map/ppermute | solution.py:700
  34.4 1.5 %shard_map.72 = (f32[12,7,8,128]{3,2,1,0:T(8,128)S(1)}, f32[20,14,8,128]{3,2,1,0:T(8,128)S(1)}) custom-call(f32[20,4,8,128]{3,2,1,0:T(8,128)S(1)} %shard_map.69.rotated, f32[5,4,8,128]{3,2,1,0:T(8,128)S(1)} %get-tuple-element.21.rest, f32[5,8,128]{2,1,0:T(8,128)S(1)} %get-tuple-element.23.halo, f32[27,8,128]{2,1,0:T(8,128)S(1)} %collective-permute-done.2.y_lo, ...), custom_call_target="tpu_custom_call" | custom-call | flops 1000000000 | bytes 100000 | tf_op jit(solution)/shard_map/pallas_call | solution.py:48
  35.9 0.2 collective-permute-done.5.off
  36.1 0.0 collective-permute-done.4.early
  36.1 0.0 collective-permute-done.6.on
  36.1 2.3 %shard_map.75 = (f32[2048,128]{1,0:T(8,128)S(1)}, f32[16,1,1152]{2,1,0:T(1,128)S(1)}) custom-call(f32[20,4,8,128]{3,2,1,0:T(8,128)S(1)} %shard_map.69.rotated, f32[5,4,8,128]{3,2,1,0:T(8,128)S(1)} %get-tuple-element.21.rest, f32[5,8,128]{2,1,0:T(8,128)S(1)} %get-tuple-element.23.halo, f32[27,8,128]{2,1,0:T(8,128)S(1)} %collective-permute-done.2.y_lo, ...), custom_call_target="tpu_custom_call" | custom-call | flops 100000 | bytes 100000 | tf_op jit(solution)/shard_map/pallas_call | solution.py:48
  38.3 13.6 %all_to_all.10.parts = f32[16,1,1152]{2,1,0:T(1,128)S(1)} all-to-all(f32[16,1,1152]{2,1,0:T(1,128)S(1)} %get-tuple-element.32), channel_id=1, replica_groups=mesh['gx_0'=8,'gx_1'=2,'gy'=4,'gz'=8] {'gx_1','gz'}, dimensions={0} | all-to-all | bytes 147456 | tf_op jit(solution)/shard_map/all_to_all | solution.py:539
  52.0 21.2 %all_to_all.11.parts = f32[32,1,1152]{2,1,0:T(1,128)S(1)} all-to-all(f32[32,1,1152]{2,1,0:T(1,128)S(1)} %shard_map.76), channel_id=1, replica_groups=mesh['gx_0'=8,'gx_1'=2,'gy'=4,'gz'=8] {'gx_0','gy'}, dimensions={0} | all-to-all | bytes 294912 | tf_op jit(solution)/shard_map/all_to_all | solution.py:539
  73.3 3.8 %all_gather.3.parts = f32[2,1,1152]{2,1,0:T(1,128)S(1)} all-gather(f32[1,1,1152]{2,1,0:T(1,128)S(1)} %shard_map.77), channel_id=1, replica_groups=mesh['gx_0'=8,'gx_1'=2,'gy'=4,'gz'=8] {'gx_1'}, dimensions={0}, use_global_device_ids=true | all-gather | bytes 13824 | tf_op jit(solution)/shard_map/all_gather | solution.py:730
  77.1 2.5 %shard_map.78 = (f32[24,4,8,128]{3,2,1,0:T(8,128)}, f32[3,24]{1,0:T(4,128)}) custom-call(f32[2,1,1152]{2,1,0:T(1,128)S(1)} %all_gather.3.parts, f32[64,4,8,128]{3,2,1,0:T(8,128)S(1)} %bitcast.3), custom_call_target="tpu_custom_call" | custom-call | flops 100000 | bytes 100000 | tf_op jit(solution)/shard_map/pallas_call | solution.py:48
  (3 shorter events, 0.1 us)
Async XLA Ops:
  2.5 8.7 %collective-permute-start.1 = (f32[5,8,128]{2,1,0:T(8,128)S(1)}, f32[5,8,128]{2,1,0:T(8,128)S(1)}, u32[]{:S(2)}, u32[]{:S(2)}) collective-permute-start(f32[5,8,128]{2,1,0:T(8,128)S(1)} %get-tuple-element.22), channel_id=1, source_target_pairs={{1,0},{2,1},{3,2},{4,3},{5,4},{6,5},{7,6},{9,8},{10,9},{11,10},{12... | collective-permute-start | bytes 61448 | tf_op jit(solution)/shard_map/ppermute | solution.py:644
  3.8 7.4 %collective-permute-start = (f32[5,8,128]{2,1,0:T(8,128)S(1)}, f32[5,8,128]{2,1,0:T(8,128)S(1)}, u32[]{:S(2)}, u32[]{:S(2)}) collective-permute-start(f32[5,8,128]{2,1,0:T(8,128)S(1)} %get-tuple-element.22), channel_id=1, source_target_pairs={{0,1},{1,2},{2,3},{3,4},{4,5},{5,6},{6,7},{8,9},{9,10},{10,11},{11... | collective-permute-start | bytes 61448 | tf_op jit(solution)/shard_map/ppermute | solution.py:644
  11.3 5.0 %collective-permute-start.2 = (f32[27,8,128]{2,1,0:T(8,128)S(1)}, f32[27,8,128]{2,1,0:T(8,128)S(1)}, u32[]{:S(2)}, u32[]{:S(2)}) collective-permute-start(f32[27,8,128]{2,1,0:T(8,128)S(1)} %get-tuple-element.24), channel_id=1, source_target_pairs={{0,8},{8,16},{16,24},{1,9},{9,17},{17,25},{2,10},{10,18},{18,26},{... | collective-permute-start | bytes 331784 | tf_op jit(solution)/shard_map/ppermute | solution.py:644
  14.6 5.5 %collective-permute-start.3 = (f32[27,8,128]{2,1,0:T(8,128)S(1)}, f32[27,8,128]{2,1,0:T(8,128)S(1)}, u32[]{:S(2)}, u32[]{:S(2)}) collective-permute-start(f32[27,8,128]{2,1,0:T(8,128)S(1)} %get-tuple-element.25), channel_id=1, source_target_pairs={{8,0},{16,8},{24,16},{9,1},{17,9},{25,17},{10,2},{18,10},{26,18},{... | collective-permute-start | bytes 331784 | tf_op jit(solution)/shard_map/ppermute | solution.py:644
  20.1 15.9 %collective-permute-start.6 = (f32[61,8,128]{2,1,0:T(8,128)S(1)}, f32[61,8,128]{2,1,0:T(8,128)S(1)}, u32[]{:S(2)}, u32[]{:S(2)}) collective-permute-start(f32[61,8,128]{2,1,0:T(8,128)S(1)} %get-tuple-element.31), channel_id=1, source_target_pairs={{0,32},{32,0},{1,33},{33,1},{2,34},{34,2},{3,35},{35,3},{4,36},{36... | collective-permute-start | bytes 749576 | tf_op jit(solution)/shard_map/ppermute | solution.py:701
  28.0 8.1 %collective-permute-start.4 = (f32[51,8,128]{2,1,0:T(8,128)S(1)}, f32[51,8,128]{2,1,0:T(8,128)S(1)}, u32[]{:S(2)}, u32[]{:S(2)}) collective-permute-start(f32[51,8,128]{2,1,0:T(8,128)S(1)} %shard_map.73), channel_id=1, source_target_pairs={{32,64},{96,128},{160,192},{224,256},{288,320},{352,384},{416,448}... | collective-permute-start | bytes 626696 | tf_op jit(solution)/shard_map/ppermute | solution.py:690
  30.7 5.3 %collective-permute-start.5 = (f32[10,8,128]{2,1,0:T(8,128)S(1)}, f32[10,8,128]{2,1,0:T(8,128)S(1)}, u32[]{:S(2)}, u32[]{:S(2)}) collective-permute-start(f32[10,8,128]{2,1,0:T(8,128)S(1)} %get-tuple-element.30), channel_id=1, source_target_pairs={{32,64},{96,128},{160,192},{224,256},{288,320},{352,384},{416,448}... | collective-permute-start | bytes 122888 | tf_op jit(solution)/shard_map/ppermute | solution.py:700

commit v13 on v12

--- a/solution.py
+++ b/solution.py
@@ -304,15 +304,14 @@
     return coef(key, 3) * ahead + coef(key, 4) * behind
 
 
-def apply(get, key, coef, skip=(), with_y=True):
+def apply(get, key, coef, skip=()):
     x, a, b = key
     lane = lanes_of()
     centre, other = get(key), get((x, a, 1 - b))
     ahead = shift_lanes(jnp.where(lane == 0, other, centre), 127)
     behind = shift_lanes(jnp.where(lane == 127, other, centre), 1)
     total = coef(key, 5) * ahead + coef(key, 6) * behind
-    if with_y:
-        total = along_y(get, key, coef) + total
+    total = along_y(get, key, coef) + total
     total = total + coef(key, 0) * centre
     for i, at in ((1, (x + 1, a, b)), (2, (x - 1, a, b))):
         if i not in skip:
@@ -354,23 +353,12 @@
     return (SIDES[key[0]][0],) if key[0] in SIDES else ()
 
 
-def level_kernel(rotated, rest, halo, coef_level, partial):
-    refs = (Fields(rotated, rest), halo, None, None, None, None, None, None)
+def level_kernel(rest, coef_level):
+    refs = (Fields(None, rest), None, None, None, None, None, None, None)
     fill_coefficients(LEVEL, coef_level, refs)
-    coef = lambda key, i: coef_level[LEVEL.index(key), i]
-
-    def body(f, carry):
-        get = cached(f, refs)
-        for at, key in enumerate(LEVEL):
-            partial[f, at] = apply(get, key, coef, skip_of(key), with_y=False)
-        return carry
-
-    lax.fori_loop(0, KEEP, body, 0, unroll=5)
-
-
-def inner_kernel(
-    rotated, rest, halo, y_lo, y_hi, coef_level, level, coef_beside, partial, y_halo
-):
+
+
+def inner_kernel(rotated, rest, halo, y_lo, y_hi, coef_level, coef_beside, partial, y_halo):
     for p in range(5):
         y_halo[p] = corner_of(p, y_lo, y_hi)
     refs = (Fields(rotated, rest), halo, y_lo, y_hi, None, None, y_halo, None)
@@ -385,10 +373,7 @@
         get = cached(f, refs)
         once = {}
         for at, key in enumerate(ONCE):
-            if key in LEVEL:
-                once[key] = level[f, LEVEL.index(key)] + along_y(get, key, coef)
-            else:
-                once[key] = apply(get, key, coef, skip_of(key))
+            once[key] = apply(get, key, coef, skip_of(key))
             partial[f, at] = once[key]
         for x, skip in ((1, (2,)), (2, (1,))):
             partial[f, len(ONCE) + x - 1] = apply(once.__getitem__, (x, 0, 0), coef, skip)
@@ -688,12 +673,7 @@
     y_hi = send(down, "gy", False)
     (early,) = call(planes_kernel, [(PLANES, Y, Z)], [rotated, rest])
     early = lax.ppermute(early, GX, swap)
-    coef_level, level = call(
-        level_kernel,
-        [(len(LEVEL), 7, Y, Z), (KEEP, len(LEVEL), Y, Z)],
-        [rotated, rest, halo],
-        limit=4,
-    )
+    (coef_level,) = call(level_kernel, [(len(LEVEL), 7, Y, Z)], [rest])
     off, on = call(
         pack_x_kernel, [(61 - PLANES, Y, Z), (61, Y, Z)], [rotated, rest, halo, y_lo, y_hi]
     )
@@ -704,7 +684,7 @@
     coef_beside, partial = call(
         inner_kernel,
         [(len(BESIDE), 7, Y, Z), (KEEP, len(ONCE) + 2, Y, Z)],
-        [rotated, rest, halo, y_lo, y_hi, coef_level, level],
+        [rotated, rest, halo, y_lo, y_hi, coef_level],
         scratch=[pltpu.VMEM((5, Y, Z), F32)],
         limit=6,
         flops=10**9,

time: 80.1 us -> 80 us (level)
  transfers between devices with their start and end apart: 7 -> 7, of which waited for: 3 -> 2; matrix products, arithmetic and copies ran while one was open for 0% -> 0% of each run, Pallas kernels for 6% -> 7%
where the time goes in v13:
time: 80 us; the launch traced here: 79.6 us
  blocking collectives  38.5 us (48%)
  starting transfers between devices  23.9 us (30%)
  Pallas kernels  12.2 us (15%)
  waiting for transfers between devices  4.21 us (5%)
    all_to_all x2, blocking collectives, exchange(): return lax.all_to_all(parts, axis, 0, 0)  34.6 us
    pallas_call x11, Pallas kernels, call(): pl.pallas_call(kernel, out_shape=[jax.ShapeDtypeStruct(s, F32) for s in o...  12.2 us
    ppermute x4, starting transfers between devices, send(): return lax.ppermute(value, axis, up if forward else [(j, i) for i, j in up])  10.5 us
    ppermute x1, starting transfers between devices, per_device(): on = lax.ppermute(on, 'gx_1', [(0, 1), (1, 0)])  7.8 us
    ppermute x4, waiting for transfers between devices, send(): return lax.ppermute(value, axis, up if forward else [(j, i) for i, j in up])  4.2 us
    all_gather x1, blocking collectives, per_device(): whole = lax.all_gather(half, 'gx_1', axis=0, tiled=True)  3.84 us
    ppermute x1, starting transfers between devices, per_device(): off = lax.ppermute(off, GX, swap)  3.64 us
    ppermute x1, starting transfers between devices, per_device(): early = lax.ppermute(early, GX, swap)  1.92 us
  transfers between devices with their start and end apart: 7, of which 2 were waited for; matrix products, arithmetic and copies ran while one was open for 0% of the time, Pallas kernels for 7%

profile of v13, /device:TPU:1, one launch (start us, length us, event | category | flops | bytes accessed | tf_op | source)
XLA Modules:
  0.0 79.6 jit_solution(2495271373422043564)
XLA Ops:
  0.6 1.9 %shard_map.68 = (f32[60,4,8,128]{3,2,1,0:T(8,128)S(1)}, f32[5,4,8,128]{3,2,1,0:T(8,128)S(1)}, f32[5,8,128]{2,1,0:T(8,128)S(1)}, f32[20,60]{1,0:T(8,128)S(1)}) custom-call(f32[60,4,8,128]{3,2,1,0:T(8,128)} %basis.1, f32[20,60]{1,0:T(8,128)} %bitcast.4, f32[4,8,128]{2,1,0:T(8,128)} %next_vector.1, f32[4,8,128]{2,1,0:T(8,128)} %diag.1, f32[3,4,8,128]{3,2,1,0:T(8,128)} %velocity.1), custom_call_target="tpu_custom_call" | custom-call | flops 100000 | bytes 100000 | tf_op jit(solution)/shard_map/pallas_call | solution.py:48
  2.5 1.3 %collective-permute-start.1 = (f32[5,8,128]{2,1,0:T(8,128)S(1)}, f32[5,8,128]{2,1,0:T(8,128)S(1)}, u32[]{:S(2)}, u32[]{:S(2)}) collective-permute-start(f32[5,8,128]{2,1,0:T(8,128)S(1)} %get-tuple-element.20), channel_id=1, source_target_pairs={{1,0},{2,1},{3,2},{4,3},{5,4},{6,5},{7,6},{9,8},{10,9},{11,10},{12... | collective-permute-start | bytes 61448 | tf_op jit(solution)/shard_map/ppermute | solution.py:629
  3.8 4.6 %collective-permute-start = (f32[5,8,128]{2,1,0:T(8,128)S(1)}, f32[5,8,128]{2,1,0:T(8,128)S(1)}, u32[]{:S(2)}, u32[]{:S(2)}) collective-permute-start(f32[5,8,128]{2,1,0:T(8,128)S(1)} %get-tuple-element.20), channel_id=1, source_target_pairs={{0,1},{1,2},{2,3},{3,4},{4,5},{5,6},{6,7},{8,9},{9,10},{10,11},{11... | collective-permute-start | bytes 61448 | tf_op jit(solution)/shard_map/ppermute | solution.py:629
  8.5 2.7 %shard_map.69.rotated = f32[20,4,8,128]{3,2,1,0:T(8,128)S(1)} custom-call(f32[60,4,8,128]{3,2,1,0:T(8,128)S(1)} %get-tuple-element.17.basis, f32[20,60]{1,0:T(8,128)S(1)} %get-tuple-element.18.schur), custom_call_target="tpu_custom_call" | custom-call | flops 1000000000 | bytes 100000 | tf_op jit(solution)/shard_map/pallas_call | solution.py:48
  11.2 0.0 collective-permute-done.1.from_hi
  11.2 0.0 collective-permute-done.from_lo
  11.2 0.1 shard_map.70
  11.3 3.3 %collective-permute-start.2 = (f32[27,8,128]{2,1,0:T(8,128)S(1)}, f32[27,8,128]{2,1,0:T(8,128)S(1)}, u32[]{:S(2)}, u32[]{:S(2)}) collective-permute-start(f32[27,8,128]{2,1,0:T(8,128)S(1)} %get-tuple-element.22), channel_id=1, source_target_pairs={{0,8},{8,16},{16,24},{1,9},{9,17},{17,25},{2,10},{10,18},{18,26},{... | collective-permute-start | bytes 331784 | tf_op jit(solution)/shard_map/ppermute | solution.py:629
  14.6 1.3 %collective-permute-start.3 = (f32[27,8,128]{2,1,0:T(8,128)S(1)}, f32[27,8,128]{2,1,0:T(8,128)S(1)}, u32[]{:S(2)}, u32[]{:S(2)}) collective-permute-start(f32[27,8,128]{2,1,0:T(8,128)S(1)} %get-tuple-element.23), channel_id=1, source_target_pairs={{8,0},{16,8},{24,16},{9,1},{17,9},{25,17},{10,2},{18,10},{26,18},{... | collective-permute-start | bytes 331784 | tf_op jit(solution)/shard_map/ppermute | solution.py:629
  15.9 0.4 collective-permute-done.2.y_lo
  16.3 3.8 %collective-permute-done.3.y_hi = f32[27,8,128]{2,1,0:T(8,128)S(1)} collective-permute-done((f32[27,8,128]{2,1,0:T(8,128)S(1)}, f32[27,8,128]{2,1,0:T(8,128)S(1)}, u32[]{:S(2)}, u32[]{:S(2)}) %collective-permute-start.3) | collective-permute-done | bytes 110624 | tf_op jit(solution)/shard_map/ppermute | solution.py:629
  20.1 0.1 shard_map.74
  20.1 7.8 %collective-permute-start.6 = (f32[61,8,128]{2,1,0:T(8,128)S(1)}, f32[61,8,128]{2,1,0:T(8,128)S(1)}, u32[]{:S(2)}, u32[]{:S(2)}) collective-permute-start(f32[61,8,128]{2,1,0:T(8,128)S(1)} %get-tuple-element.27), channel_id=1, source_target_pairs={{0,32},{32,0},{1,33},{33,1},{2,34},{34,2},{3,35},{35,3},{4,36},{36... | collective-permute-start | bytes 749576 | tf_op jit(solution)/shard_map/ppermute | solution.py:681
  28.0 1.9 %collective-permute-start.4 = (f32[51,8,128]{2,1,0:T(8,128)S(1)}, f32[51,8,128]{2,1,0:T(8,128)S(1)}, u32[]{:S(2)}, u32[]{:S(2)}) collective-permute-start(f32[51,8,128]{2,1,0:T(8,128)S(1)} %shard_map.73), channel_id=1, source_target_pairs={{32,64},{96,128},{160,192},{224,256},{288,320},{352,384},{416,448}... | collective-permute-start | bytes 626696 | tf_op jit(solution)/shard_map/ppermute | solution.py:675
  29.9 3.6 %collective-permute-start.5 = (f32[10,8,128]{2,1,0:T(8,128)S(1)}, f32[10,8,128]{2,1,0:T(8,128)S(1)}, u32[]{:S(2)}, u32[]{:S(2)}) collective-permute-start(f32[10,8,128]{2,1,0:T(8,128)S(1)} %get-tuple-element.26), channel_id=1, source_target_pairs={{32,64},{96,128},{160,192},{224,256},{288,320},{352,384},{416,448}... | collective-permute-start | bytes 122888 | tf_op jit(solution)/shard_map/ppermute | solution.py:680
  33.6 2.6 %shard_map.72 = (f32[12,7,8,128]{3,2,1,0:T(8,128)S(1)}, f32[20,14,8,128]{3,2,1,0:T(8,128)S(1)}) custom-call(f32[20,4,8,128]{3,2,1,0:T(8,128)S(1)} %shard_map.69.rotated, f32[5,4,8,128]{3,2,1,0:T(8,128)S(1)} %get-tuple-element.19.rest, f32[5,8,128]{2,1,0:T(8,128)S(1)} %get-tuple-element.21.halo, f32[27,8,128]{2,1,0:T(8,128)S(1)} %collective-permute-done.2.y_lo, ...), custom_call_target="tpu_custom_call" | custom-call | flops 1000000000 | bytes 100000 | tf_op jit(solution)/shard_map/pallas_call | solution.py:48
  36.2 0.0 collective-permute-done.5.off
  36.2 0.0 collective-permute-done.4.early
  36.3 0.0 collective-permute-done.6.on
  36.3 2.3 %shard_map.75 = (f32[2048,128]{1,0:T(8,128)S(1)}, f32[16,1,1152]{2,1,0:T(1,128)S(1)}) custom-call(f32[20,4,8,128]{3,2,1,0:T(8,128)S(1)} %shard_map.69.rotated, f32[5,4,8,128]{3,2,1,0:T(8,128)S(1)} %get-tuple-element.19.rest, f32[5,8,128]{2,1,0:T(8,128)S(1)} %get-tuple-element.21.halo, f32[27,8,128]{2,1,0:T(8,128)S(1)} %collective-permute-done.2.y_lo, ...), custom_call_target="tpu_custom_call" | custom-call | flops 100000 | bytes 100000 | tf_op jit(solution)/shard_map/pallas_call | solution.py:48
  38.5 12.6 %all_to_all.10.parts = f32[16,1,1152]{2,1,0:T(1,128)S(1)} all-to-all(f32[16,1,1152]{2,1,0:T(1,128)S(1)} %get-tuple-element.28), channel_id=1, replica_groups=mesh['gx_0'=8,'gx_1'=2,'gy'=4,'gz'=8] {'gx_1','gz'}, dimensions={0} | all-to-all | bytes 147456 | tf_op jit(solution)/shard_map/all_to_all | solution.py:524
  51.2 22.0 %all_to_all.11.parts = f32[32,1,1152]{2,1,0:T(1,128)S(1)} all-to-all(f32[32,1,1152]{2,1,0:T(1,128)S(1)} %shard_map.76), channel_id=1, replica_groups=mesh['gx_0'=8,'gx_1'=2,'gy'=4,'gz'=8] {'gx_0','gy'}, dimensions={0} | all-to-all | bytes 294912 | tf_op jit(solution)/shard_map/all_to_all | solution.py:524
  73.2 3.8 %all_gather.3.parts = f32[2,1,1152]{2,1,0:T(1,128)S(1)} all-gather(f32[1,1,1152]{2,1,0:T(1,128)S(1)} %shard_map.77), channel_id=1, replica_groups=mesh['gx_0'=8,'gx_1'=2,'gy'=4,'gz'=8] {'gx_1'}, dimensions={0}, use_global_device_ids=true | all-gather | bytes 13824 | tf_op jit(solution)/shard_map/all_gather | solution.py:710
  77.1 2.5 %shard_map.78 = (f32[24,4,8,128]{3,2,1,0:T(8,128)}, f32[3,24]{1,0:T(4,128)}) custom-call(f32[2,1,1152]{2,1,0:T(1,128)S(1)} %all_gather.3.parts, f32[64,4,8,128]{3,2,1,0:T(8,128)S(1)} %bitcast.3), custom_call_target="tpu_custom_call" | custom-call | flops 100000 | bytes 100000 | tf_op jit(solution)/shard_map/pallas_call | solution.py:48
  (4 shorter events, 0.1 us)
Async XLA Ops:
  2.5 8.7 %collective-permute-start.1 = (f32[5,8,128]{2,1,0:T(8,128)S(1)}, f32[5,8,128]{2,1,0:T(8,128)S(1)}, u32[]{:S(2)}, u32[]{:S(2)}) collective-permute-start(f32[5,8,128]{2,1,0:T(8,128)S(1)} %get-tuple-element.20), channel_id=1, source_target_pairs={{1,0},{2,1},{3,2},{4,3},{5,4},{6,5},{7,6},{9,8},{10,9},{11,10},{12... | collective-permute-start | bytes 61448 | tf_op jit(solution)/shard_map/ppermute | solution.py:629
  3.8 7.4 %collective-permute-start = (f32[5,8,128]{2,1,0:T(8,128)S(1)}, f32[5,8,128]{2,1,0:T(8,128)S(1)}, u32[]{:S(2)}, u32[]{:S(2)}) collective-permute-start(f32[5,8,128]{2,1,0:T(8,128)S(1)} %get-tuple-element.20), channel_id=1, source_target_pairs={{0,1},{1,2},{2,3},{3,4},{4,5},{5,6},{6,7},{8,9},{9,10},{10,11},{11... | collective-permute-start | bytes 61448 | tf_op jit(solution)/shard_map/ppermute | solution.py:629
  11.3 5.0 %collective-permute-start.2 = (f32[27,8,128]{2,1,0:T(8,128)S(1)}, f32[27,8,128]{2,1,0:T(8,128)S(1)}, u32[]{:S(2)}, u32[]{:S(2)}) collective-permute-start(f32[27,8,128]{2,1,0:T(8,128)S(1)} %get-tuple-element.22), channel_id=1, source_target_pairs={{0,8},{8,16},{16,24},{1,9},{9,17},{17,25},{2,10},{10,18},{18,26},{... | collective-permute-start | bytes 331784 | tf_op jit(solution)/shard_map/ppermute | solution.py:629
  14.6 5.5 %collective-permute-start.3 = (f32[27,8,128]{2,1,0:T(8,128)S(1)}, f32[27,8,128]{2,1,0:T(8,128)S(1)}, u32[]{:S(2)}, u32[]{:S(2)}) collective-permute-start(f32[27,8,128]{2,1,0:T(8,128)S(1)} %get-tuple-element.23), channel_id=1, source_target_pairs={{8,0},{16,8},{24,16},{9,1},{17,9},{25,17},{10,2},{18,10},{26,18},{... | collective-permute-start | bytes 331784 | tf_op jit(solution)/shard_map/ppermute | solution.py:629
  20.1 16.1 %collective-permute-start.6 = (f32[61,8,128]{2,1,0:T(8,128)S(1)}, f32[61,8,128]{2,1,0:T(8,128)S(1)}, u32[]{:S(2)}, u32[]{:S(2)}) collective-permute-start(f32[61,8,128]{2,1,0:T(8,128)S(1)} %get-tuple-element.27), channel_id=1, source_target_pairs={{0,32},{32,0},{1,33},{33,1},{2,34},{34,2},{3,35},{35,3},{4,36},{36... | collective-permute-start | bytes 749576 | tf_op jit(solution)/shard_map/ppermute | solution.py:681
  28.0 8.3 %collective-permute-start.4 = (f32[51,8,128]{2,1,0:T(8,128)S(1)}, f32[51,8,128]{2,1,0:T(8,128)S(1)}, u32[]{:S(2)}, u32[]{:S(2)}) collective-permute-start(f32[51,8,128]{2,1,0:T(8,128)S(1)} %shard_map.73), channel_id=1, source_target_pairs={{32,64},{96,128},{160,192},{224,256},{288,320},{352,384},{416,448}... | collective-permute-start | bytes 626696 | tf_op jit(solution)/shard_map/ppermute | solution.py:675
  29.9 6.3 %collective-permute-start.5 = (f32[10,8,128]{2,1,0:T(8,128)S(1)}, f32[10,8,128]{2,1,0:T(8,128)S(1)}, u32[]{:S(2)}, u32[]{:S(2)}) collective-permute-start(f32[10,8,128]{2,1,0:T(8,128)S(1)} %get-tuple-element.26), channel_id=1, source_target_pairs={{32,64},{96,128},{160,192},{224,256},{288,320},{352,384},{416,448}... | collective-permute-start | bytes 122888 | tf_op jit(solution)/shard_map/ppermute | solution.py:680
